TPU v7x, 256 devices: a whole 4x4x8 slice. The times are simulated.
256 devices in a mesh: facet: 64 (over z, x, core), stokes: 4 (over y).
Axes of the slice: x: 4, y: 4, z: 8, core: 2. Of those that a mesh axis runs over, the one named last changes fastest.
Arguments:
- strips: bfloat16 [4, 4096, 16384], P('stokes', 'facet'), may hold values from -6 to 6
- sub_u: int32 [128], replicated, may hold values from 0 to 4095
- counts: int32 [128], P('facet'), may hold values from 1 to 64, 4096 in all
- uvw: int32 [3, 128, 8192], P(None, 'facet'), may hold values from 0 to 255
- mueller: float32 [4, 4, 128, 64], P(None, None, 'facet'), may hold values from -3 to 3
- observed: float32 [4, 128, 2, 8192], P('stokes', 'facet'), may hold values from -6 to 6
Outputs:
- image_out: bfloat16 [4, 4096, 16384], P('stokes', 'facet')
- residual_vis: float32 [4, 128, 2, 8192], P('stokes', 'facet')
Inputs may be any that keep to these rules, and one draw needn't show every extreme that they name: Block counts of one subgrid are at most 64; some subgrid has exactly 64.
All inputs are finite; a program needn't handle non-finite values.
Results may differ from a plain program's by a relative error of at most 0.018.
Values may be sent and summed in bfloat16 or wider, within the bound.
No kernel may reach another device: no remote copies, remote signals or barrier semaphores. Data moves between devices by JAX's collectives and lax.ppermute only.
A program may use at most 128 MiB of HBM per device.

v0:
```python
import math

import jax
import jax.numpy as jnp
from jax import lax
from jax.sharding import PartitionSpec as P

K = 64
G = 256
MAXB = 64
BLOCK = 128
VISITS = 8192


full_turn = 2.0 * math.pi


def cut_along(array, dim, count):
    before, after = (array.shape[:dim], array.shape[dim + 1 :])
    return jnp.moveaxis(array.reshape(*before, count, -1, *after), dim, 0)


def sum_at_owner(array, axis, dim):
    count = lax.axis_size(axis)
    pieces = lax.all_to_all(cut_along(array, dim, count), axis, 0, 0, tiled=True)
    return jnp.sum(pieces.astype(jnp.float32), axis=0)


def turn(phase, period):
    angle = phase.astype(jnp.float32) * (full_turn / period)
    return (jnp.cos(angle), jnp.sin(angle))


def stack_right(real, imag):
    return jnp.concatenate([jnp.concatenate([real, imag], 1), jnp.concatenate([-imag, real], 1)], 0)


def column_table(length, samples):
    lpos = jnp.arange(length, dtype=jnp.int32)[:, None]
    cpos = jnp.arange(samples, dtype=jnp.int32)[None, :]
    cosine, sine = turn(4 * cpos * lpos % length, length)
    scale = 1.0 / math.sqrt(length)
    return stack_right(cosine * scale, -sine * scale).astype(jnp.bfloat16)


def interp_table(width, samples):
    upos = jnp.arange(width, dtype=jnp.int32)[:, None, None]
    kpos = jnp.arange(samples, dtype=jnp.int32)[None, :, None]
    mpos = jnp.arange(samples, dtype=jnp.int32)[None, None, :] - samples // 2
    cosine, sine = turn(jnp.remainder(mpos * (upos - 4 * kpos), width), width)
    return (jnp.sum(cosine, 2) / (2.0 * samples), jnp.sum(sine, 2) / (2.0 * samples))


def facet_table(real, imag, facets, rows, total):
    width, samples = real.shape
    centre = (facets * rows + rows // 2)[None, :, None]
    upos = jnp.arange(width, dtype=jnp.int32)[:, None, None]
    kpos = jnp.arange(samples, dtype=jnp.int32)[None, None, :]
    phase = 4 * kpos * centre % total - upos * centre % total
    cosine, sine = turn(phase, total)
    e_real = real[:, None, :] * cosine - imag[:, None, :] * sine
    e_imag = real[:, None, :] * sine + imag[:, None, :] * cosine
    return (e_real, e_imag)


def row_table(offsets, positions, total, samples):
    kpos = jnp.arange(samples, dtype=jnp.int32)
    freq = (offsets[:, None] + 4 * kpos[None, :]) % total
    phase = freq[:, :, None] * positions[None, None, :] % total
    cosine, sine = turn(phase, total)
    scale = 1.0 / math.sqrt(total)
    return ((cosine * scale).astype(jnp.bfloat16), (-sine * scale).astype(jnp.bfloat16))


def join(first, second, conj):
    half = first.shape[-1] // 2
    if conj:
        real = first[..., :half] + second[..., half:]
        imag = first[..., half:] - second[..., :half]
    else:
        real = first[..., :half] - second[..., half:]
        imag = first[..., half:] + second[..., :half]
    return jnp.concatenate([real, imag], -1)


def cein(form, left_re, left_im, packed, conj):
    first = jnp.einsum(form, left_re, packed, preferred_element_type=jnp.float32)
    second = jnp.einsum(form, left_im, packed, preferred_element_type=jnp.float32)
    return join(first, second, conj)


def select_table(cells, width):
    grid_pos = jnp.arange(width, dtype=jnp.int32)[None, :]
    return (cells[:, None] == grid_pos).astype(jnp.bfloat16)


def body(strips, sub_u, counts, uvw, mueller, observed):
    nfac = lax.axis_size("facet")
    here = lax.axis_index("facet")
    plane = lax.axis_index("stokes")
    rows = strips.shape[1]
    total = rows * nfac
    owned = counts.shape[0]
    nsub = sub_u.shape[0]
    column = column_table(strips.shape[2] // 2, K)
    coeffs = jnp.dot(strips[0], column, preferred_element_type=jnp.float32).astype(jnp.bfloat16)
    b_re, b_im = interp_table(G, K)
    e_re, e_im = facet_table(b_re, b_im, jnp.arange(nfac, dtype=jnp.int32), rows, total)
    e_re = e_re.astype(jnp.bfloat16)
    e_im = e_im.astype(jnp.bfloat16)
    interp_pack = jnp.concatenate([b_re, b_im], 1).astype(jnp.bfloat16)
    positions = here * rows + jnp.arange(rows, dtype=jnp.int32)
    r_re, r_im = row_table(sub_u, positions, total, K)
    outgoing = cein("jkr,rc->jkc", r_re, r_im, coeffs, False).astype(jnp.bfloat16)
    received = lax.all_to_all(outgoing, "facet", split_axis=0, concat_axis=0, tiled=True).reshape(
        nfac, owned, K, 2 * K
    )
    lifted = cein("ufk,fjkc->juc", e_re, e_im, received, False).astype(jnp.bfloat16)

    def pick_rows(items):
        lifted_one, u_cells, w_cells = items
        picked = jnp.dot(select_table(u_cells, G), lifted_one, preferred_element_type=jnp.float32)
        weights = jnp.dot(select_table(w_cells, G), interp_pack, preferred_element_type=jnp.float32)
        return (picked, weights)

    picked, weights = lax.map(pick_rows, (lifted, uvw[0], uvw[1]))
    y_re = picked[..., :K]
    y_im = picked[..., K:]
    w_re = weights[..., :K]
    w_im = weights[..., K:]
    m_re = jnp.sum(y_re * w_re - y_im * w_im, -1)
    m_im = jnp.sum(y_re * w_im + y_im * w_re, -1)
    cosine, sine = turn(uvw[2], G)
    mod_re = m_re * cosine + m_im * sine
    mod_im = m_im * cosine - m_re * sine
    model = jnp.stack([mod_re, mod_im], 1).reshape(owned, 2, MAXB, BLOCK)
    live = (jnp.arange(MAXB, dtype=jnp.int32)[None, :] < counts[:, None]).astype(jnp.float32)[
        :, None, :, None
    ]
    seen = observed[0].reshape(owned, 2, MAXB, BLOCK)
    row_mix = lax.dynamic_index_in_dim(mueller, plane, 0, keepdims=False)
    col_mix = lax.dynamic_index_in_dim(mueller, plane, 1, keepdims=False)
    corr = sum_at_owner(
        (col_mix[:, :, None, :, None] * model[None]).astype(jnp.bfloat16), "stokes", 0
    )[0]
    resid = (seen - corr) * live
    back = sum_at_owner(
        (row_mix[:, :, None, :, None] * resid[None]).astype(jnp.bfloat16), "stokes", 0
    )[0]
    back = back.reshape(owned, 2, VISITS)
    g_re = back[:, 0] * cosine - back[:, 1] * sine
    g_im = back[:, 1] * cosine + back[:, 0] * sine
    v_re = g_re[..., None] * w_re + g_im[..., None] * w_im
    v_im = g_im[..., None] * w_re - g_re[..., None] * w_im
    spread_vals = jnp.concatenate([v_re, v_im], -1).astype(jnp.bfloat16)

    def spread_rows(items):
        vals_one, u_cells = items
        return lax.dot_general(
            select_table(u_cells, G),
            vals_one,
            (((0,), (0,)), ((), ())),
            preferred_element_type=jnp.float32,
        )

    lifted_adj = lax.map(spread_rows, (spread_vals, uvw[0])).astype(jnp.bfloat16)
    patches_adj = cein("ufk,juc->fjkc", e_re, e_im, lifted_adj, True).astype(jnp.bfloat16)
    returned = lax.all_to_all(
        patches_adj, "facet", split_axis=0, concat_axis=0, tiled=True
    ).reshape(nsub, K, 2 * K)
    sums = cein("jkr,jkc->rc", r_re, r_im, returned, True)
    image = lax.dot_general(
        sums.astype(jnp.bfloat16),
        column,
        (((1,), (1,)), ((), ())),
        preferred_element_type=jnp.float32,
    )
    image_out = (8.0 * image).astype(jnp.bfloat16)[None]
    return (image_out, resid.reshape(owned, 2, VISITS)[None])


def solution(mesh):
    placed = (
        P("stokes", "facet", None),
        P(),
        P("facet"),
        P(None, "facet", None),
        P(None, None, "facet", None),
        P("stokes", "facet", None, None),
    )
    return jax.shard_map(
        body,
        mesh=mesh,
        in_specs=placed,
        out_specs=(P("stokes", "facet", None), P("stokes", "facet", None, None)),
        check_vma=False,
    )
```

profile of v0, /device:TPU:1, one launch (start us, length us, event | category | flops | bytes accessed | tf_op | source)
XLA Modules:
  0.0 359.6 jit_solution(14623068846076330779)
XLA Ops:
  0.7 10.0 %fusion.50 = (bf16[8192,64]{0,1:T(8,128)(2,1)S(1)}, bf16[8192,64]{0,1:T(8,128)(2,1)}, bf16[8192,64]{0,1:T(8,128)(2,1)}) fusion(s32[64]{0:T(128)S(1)} %iota_multiply_fusion), kind=kLoop, calls=%fused_computation.92 | loop fusion | flops 11010048 | bytes 3145984 | tf_op jit(solution)/shard_map/convert.17
  10.6 0.7 add_select_fusion.6
  11.4 6.5 %fusion.66 = bf16[128,64,1]{0,1,2:T(8,128)(2,1)S(1)} fusion(bf16[1,64,16384]{2,1,0:T(8,128)(2,1)S(1)} %copy-done, bf16[8192,64]{0,1:T(8,128)(2,1)} %get-tuple-element.154, bf16[8192,64]{0,1:T(8,128)(2,1)} %get-tuple-element.153, bf16[8192,64]{0,1:T(8,128)(2,1)S(1)} %get-tuple-element.152), kind=kOutput, calls=%fused_computation.98 | convolution fusion | flops 285220864 | bytes 5259264 | tf_op jit(solution)/shard_map/dot_general | solution.py:106
  17.9 7.9 %fusion.69 = f32[128,64,128]{0,2,1:T(8,128)S(1)} fusion(bf16[128,64,1]{0,1,2:T(8,128)(2,1)S(1)} %fusion.66, s32[64]{0:T(128)S(1)} %iota_add_fusion.1, s32[128,64]{0,1:T(8,128)S(1)} %add_select_fusion.6), kind=kOutput, calls=%fused_computation.99 | convolution fusion | flops 142606336 | bytes 4243712 | tf_op jit(solution)/shard_map/jkr,rc->jkc/dot_general | solution.py:87
  25.9 8.4 %fusion.70 = f32[128,64,128]{0,2,1:T(8,128)S(1)} fusion(bf16[128,64,1]{0,1,2:T(8,128)(2,1)S(1)} %fusion.66, s32[64]{0:T(128)S(1)} %iota_add_fusion.1, s32[128,64]{0,1:T(8,128)S(1)} %add_select_fusion.6), kind=kOutput, calls=%fused_computation.100 | convolution fusion | flops 143130624 | bytes 4243712 | tf_op jit(solution)/shard_map/jkr,rc->jkc/dot_general | solution.py:88
  34.3 1.0 fusion.34
  35.3 0.1 pad_maximum_fusion.1
  35.5 2.8 copy.41
  38.2 13.3 %all-to-all-start = ((bf16[128,64,128]{2,1,0:T(8,128)(2,1)}), bf16[128,64,128]{2,1,0:T(8,128)(2,1)}, u32[]{:S(2)}, u32[]{:S(2)}) async-start(bf16[128,64,128]{2,1,0:T(8,128)(2,1)} %copy.41), calls=%async_computation | async-start | bytes 4194304 | tf_op jit(solution)/shard_map/all_to_all | solution.py:115
  51.6 18.3 %cosine_reduce_fusion = (f32[256,64]{0,1:T(8,128)S(1)}, f32[256,64]{0,1:T(8,128)S(1)}) fusion(s32[256,64]{0,1:T(8,128)S(1)} %iota_subtract_fusion, s32[64]{0:T(128)S(1)} %iota_add_fusion), kind=kLoop, calls=%fused_computation.49 | loop fusion | flops 16744448 | bytes 196864 | tf_op jit(solution)/shard_map/reduce_sum | solution.py:51
  69.9 0.1 copy.43
  70.1 0.1 reshape_squeeze.6
  70.4 0.1 add_select_fusion.3
  70.5 1.2 fusion.122
  71.6 29.5 %all-to-all-done = bf16[128,64,128]{2,1,0:T(8,128)(2,1)} async-done(((bf16[128,64,128]{2,1,0:T(8,128)(2,1)}), bf16[128,64,128]{2,1,0:T(8,128)(2,1)}, u32[]{:S(2)}, u32[]{:S(2)}) %all-to-all-start) | async-done | bytes 2097184 | tf_op jit(solution)/shard_map/all_to_all | solution.py:115
  101.2 18.5 %fusion.51 = f32[2,256,128]{1,2,0:T(8,128)S(1)} fusion(bf16[64,2,64,128]{3,2,1,0:T(8,128)(2,1)} %bitcast.13, f32[256,64]{0,1:T(8,128)S(1)} %get-tuple-element.155, s32[256,64]{0,1:T(8,128)S(1)} %add_select_fusion.3, s32[64,64]{1,0:T(8,128)S(1)} %add_select_fusion.5, f32[256,64]{0,1:T(8,128)S(1)} %get-tuple-element.149), kind=kOutput, calls=%fused_computation.93 | convolution fusion | flops 544210944 | bytes 2572288 | tf_op jit(solution)/shard_map/ufk,fjkc->juc/dot_general | solution.py:87
  119.7 18.7 %fusion.54 = f32[2,256,128]{1,2,0:T(8,128)S(1)} fusion(bf16[64,2,64,128]{3,2,1,0:T(8,128)(2,1)} %bitcast.13, f32[256,64]{0,1:T(8,128)S(1)} %get-tuple-element.155, s32[256,64]{0,1:T(8,128)S(1)} %add_select_fusion.3, s32[64,64]{1,0:T(8,128)S(1)} %add_select_fusion.5, f32[256,64]{0,1:T(8,128)S(1)} %get-tuple-element.149), kind=kOutput, calls=%fused_computation.94 | convolution fusion | flops 544210944 | bytes 2572288 | tf_op jit(solution)/shard_map/ufk,fjkc->juc/dot_general | solution.py:88
  138.4 22.7 %while.22 = (s32[]{:T(128)}, f32[2,8192,128]{2,1,0:T(8,128)}, f32[2,8192,128]{2,1,0:T(8,128)}, s32[2,8192]{1,0:T(2,128)S(1)}, bf16[2,256,128]{1,2,0:T(8,128)(2,1...) while((s32[]{:T(128)}, f32[2,8192,128]{2,1,0:T(8,128)}, ...), condition=%wide.region_3.4_spmd, body=%wide.region_2.3_spmd.sunk | while | flops 1077936128 | bytes 8717913 | solution.py:126
  138.7 5.6 %fusion.139 = f32[2,8192,128]{2,1,0:T(8,128)} fusion(f32[2,8192,128]{2,1,0:T(8,128)} %get-tuple-element.238, s32[]{:T(128)} %get-tuple-element.237, s32[8192]{0:T(1024)S(1)} %bitcast.187, bf16[2,256,128]{1,2,0:T(8,128)(2,1)S(1)} %get-tuple-element.249), kind=kOutput, calls=%fused_computation.3.clone.1 | convolution fusion | flops 538968064 | bytes 4293632 | tf_op jit(solution)/shard_map/while/body/eval_jaxpr/dot_general | solution.py:122
  144.2 5.6 %fusion.140 = f32[2,8192,128]{2,1,0:T(8,128)} fusion(f32[2,8192,128]{2,1,0:T(8,128)} %get-tuple-element.239, s32[]{:T(128)} %get-tuple-element.237, bf16[256,128]{1,0:T(8,128)(2,1)S(1)} %get-tuple-element.251, s32[8192]{0:T(1024)S(1)} %bitcast.186), kind=kOutput, calls=%fused_computation.1.clone.1 | convolution fusion | flops 538968064 | bytes 4293120 | tf_op jit(solution)/shard_map/while/body/eval_jaxpr/dot_general | solution.py:123
  149.9 5.6 %fusion.139 = f32[2,8192,128]{2,1,0:T(8,128)} fusion(f32[2,8192,128]{2,1,0:T(8,128)} %get-tuple-element.238, s32[]{:T(128)} %get-tuple-element.237, s32[8192]{0:T(1024)S(1)} %bitcast.187, bf16[2,256,128]{1,2,0:T(8,128)(2,1)S(1)} %get-tuple-element.249), kind=kOutput, calls=%fused_computation.3.clone.1 | convolution fusion | flops 538968064 | bytes 4293632 | tf_op jit(solution)/shard_map/while/body/eval_jaxpr/dot_general | solution.py:122
  155.5 5.6 %fusion.140 = f32[2,8192,128]{2,1,0:T(8,128)} fusion(f32[2,8192,128]{2,1,0:T(8,128)} %get-tuple-element.239, s32[]{:T(128)} %get-tuple-element.237, bf16[256,128]{1,0:T(8,128)(2,1)S(1)} %get-tuple-element.251, s32[8192]{0:T(1024)S(1)} %bitcast.186), kind=kOutput, calls=%fused_computation.1.clone.1 | convolution fusion | flops 538968064 | bytes 4293120 | tf_op jit(solution)/shard_map/while/body/eval_jaxpr/dot_general | solution.py:123
  161.2 19.5 %subtract_reduce_fusion = (f32[2,8192]{1,0:T(2,128)S(1)}, f32[2,8192]{1,0:T(2,128)S(1)}) fusion(f32[2,8192,128]{2,1,0:T(8,128)} %get-tuple-element.62, f32[2,8192,128]{2,1,0:T(8,128)} %get-tuple-element.63), kind=kLoop, calls=%fused_computation.28 | loop fusion | flops 8355840 | bytes 16908288 | tf_op jit(solution)/shard_map/reduce_sum | solution.py:131
  180.7 0.8 multiply_convert_fusion.8
  181.5 4.2 %all-to-all-start.1 = ((bf16[4,1,2,2,64,128]{5,4,3,2,1,0:T(8,128)(2,1)}), bf16[4,1,2,2,64,128]{5,4,3,2,1,0:T(8,128)(2,1)S(1)}, u32[]{:S(2)}, u32[]{:S(2)}) async-start(bf16[4,1,2,2,64,128]{5,4,3,2,1,0:T(8,128)(2,1)} %multiply_convert_fusion.8), calls=%async_computation.1 | async-start | bytes 524288 | tf_op jit(solution)/shard_map/all_to_all | solution.py:25
  185.8 5.5 %all-to-all-done.1 = bf16[4,1,2,2,64,128]{5,4,3,2,1,0:T(8,128)(2,1)S(1)} async-done(((bf16[4,1,2,2,64,128]{5,4,3,2,1,0:T(8,128)(2,1)}), bf16[4,1,2,2,64,128]{5,4,3,2,1,0:T(8,128)(2,1)S(1)}, u32[]{:S(2)}, u32[]{:S(2)}) %all-to-all-start.1) | async-done | bytes 262176 | tf_op jit(solution)/shard_map/all_to_all | solution.py:25
  191.3 0.8 multiply_convert_fusion.7
  192.2 3.4 all-to-all-start.2
  195.6 5.5 %all-to-all-done.2 = bf16[4,1,2,2,64,128]{5,4,3,2,1,0:T(8,128)(2,1)S(1)} async-done(((bf16[4,1,2,2,64,128]{5,4,3,2,1,0:T(8,128)(2,1)}), bf16[4,1,2,2,64,128]{5,4,3,2,1,0:T(8,128)(2,1)S(1)}, u32[]{:S(2)}, u32[]{:S(2)}) %all-to-all-start.2) | async-done | bytes 262176 | tf_op jit(solution)/shard_map/all_to_all | solution.py:25
  201.2 0.1 fusion.124
  201.3 1.1 fusion.78
  202.4 10.7 %add_convert_fusion = (bf16[2,8192,64]{2,1,0:T(8,128)(2,1)S(1)}, bf16[2,8192,64]{2,1,0:T(8,128)(2,1)S(1)}) fusion(f32[2,8192,128]{2,1,0:T(8,128)} %get-tuple-element.63, f32[2,8192]{1,0:T(2,128)S(1)} %get-tuple-element.137, f32[2,8192]{1,0:T(2,128)S(1)} %get-tuple-element.136), kind=kLoop, calls=%fused_computation.26 | loop fusion | flops 8388608 | bytes 12713984 | tf_op jit(solution)/shard_map/convert.4
  213.1 3.7 %pad_maximum_fusion = bf16[2,8192,128]{2,1,0:T(8,128)(2,1)} fusion(bf16[2,8192,64]{2,1,0:T(8,128)(2,1)S(1)} %get-tuple-element.129, bf16[2,8192,64]{2,1,0:T(8,128)(2,1)S(1)} %get-tuple-element.128), kind=kLoop, calls=%fused_computation.42 | loop fusion | flops 8388608 | bytes 8388608 | tf_op jit(solution)/shard_map/concatenate | solution.py:155
  216.7 10.8 %while.23 = (s32[]{:T(128)}, bf16[2,256,128]{2,1,0:T(8,128)(2,1)S(1)}, s32[2,8192]{1,0:T(2,128)S(1)}, bf16[2,8192,128]{2,1,0:T(8,128)(2,1)}, s32[]{:T(128)}) while((s32[]{:T(128)}, bf16[2,256,128]{2,1,0:T(8,128)(2,1)S(1)}, s32[2,8192]{1,0:T(2,128)S(1)}, bf16[2,8192,128]{2,1,0:T(8,128)(2,1)}, s32[]{:T(128)}) %tuple.67), condition=%wide.region_9.10_spmd, body=%wide.region_8.9_spmd.sunk | while | flops 538968064 | bytes 2327617 | solution.py:166
  216.8 5.2 %fusion.142 = bf16[2,256,128]{2,1,0:T(8,128)(2,1)S(1)} fusion(bf16[2,256,128]{2,1,0:T(8,128)(2,1)S(1)} %get-tuple-element.259, s32[]{:T(128)} %get-tuple-element.258, bf16[2,8192,128]{2,1,0:T(8,128)(2,1)} %get-tuple-element.266, s32[8192]{0:T(1024)S(1)} %bitcast.190), kind=kOutput, calls=%fused_computation.19.clone.1 | convolution fusion | flops 538968064 | bytes 2262016 | tf_op jit(solution)/shard_map/while/body/eval_jaxpr/dot_general | solution.py:159
  222.0 5.2 %fusion.142 = bf16[2,256,128]{2,1,0:T(8,128)(2,1)S(1)} fusion(bf16[2,256,128]{2,1,0:T(8,128)(2,1)S(1)} %get-tuple-element.259, s32[]{:T(128)} %get-tuple-element.258, bf16[2,8192,128]{2,1,0:T(8,128)(2,1)} %get-tuple-element.266, s32[8192]{0:T(1024)S(1)} %bitcast.190), kind=kOutput, calls=%fused_computation.19.clone.1 | convolution fusion | flops 538968064 | bytes 2262016 | tf_op jit(solution)/shard_map/while/body/eval_jaxpr/dot_general | solution.py:159
  227.6 16.5 %convolution_bitcast_fusion.3 = f32[64,2,64,128]{3,2,0,1:T(8,128)S(1)} fusion(f32[256,64]{0,1:T(8,128)S(1)} %get-tuple-element.155, s32[256,64]{0,1:T(8,128)S(1)} %add_select_fusion.3, s32[64,64]{1,0:T(8,128)S(1)} %add_select_fusion.5, f32[256,64]{0,1:T(8,128)S(1)} %get-tuple-element.149, bf16[2,256,128]{2,1,0:T(8,128)(2,1)S(1)} %get-tuple-element.64), kind=kOutput, calls=%fused_computation.59 | convolution fusion | flops 544210944 | bytes 4538368 | tf_op jit(solution)/shard_map/ufk,juc->fjkc/dot_general | solution.py:87
  244.1 16.7 %convolution_bitcast_fusion.2 = f32[64,2,64,128]{3,2,0,1:T(8,128)S(1)} fusion(f32[256,64]{0,1:T(8,128)S(1)} %get-tuple-element.155, s32[256,64]{0,1:T(8,128)S(1)} %add_select_fusion.3, s32[64,64]{1,0:T(8,128)S(1)} %add_select_fusion.5, f32[256,64]{0,1:T(8,128)S(1)} %get-tuple-element.149, bf16[2,256,128]{2,1,0:T(8,128)(2,1)S(1)} %get-tuple-element.64), kind=kOutput, calls=%fused_computation.58 | convolution fusion | flops 544210944 | bytes 4538368 | tf_op jit(solution)/shard_map/ufk,juc->fjkc/dot_general | solution.py:88
  260.7 2.4 fusion.24
  263.1 1.2 pad_maximum_fusion.2
  264.3 1.6 copy.47
  265.9 9.7 %all-to-all-start.3 = ((bf16[64,2,64,128]{3,2,1,0:T(8,128)(2,1)}), bf16[64,2,64,128]{3,2,1,0:T(8,128)(2,1)S(1)}, u32[]{:S(2)}, u32[]{:S(2)}) async-start(bf16[64,2,64,128]{3,2,1,0:T(8,128)(2,1)} %copy.47), calls=%async_computation.3 | async-start | bytes 4194304 | tf_op jit(solution)/shard_map/all_to_all | solution.py:168
  275.6 0.7 copy.90
  276.4 1.6 subtract_multiply_fusion
  278.0 47.1 %all-to-all-done.3 = bf16[64,2,64,128]{3,2,1,0:T(8,128)(2,1)S(1)} async-done(((bf16[64,2,64,128]{3,2,1,0:T(8,128)(2,1)}), bf16[64,2,64,128]{3,2,1,0:T(8,128)(2,1)S(1)}, u32[]{:S(2)}, u32[]{:S(2)}) %all-to-all-start.3) | async-done | bytes 2097184 | tf_op jit(solution)/shard_map/all_to_all | solution.py:168
  325.1 9.3 %fusion.57 = f32[64,128]{1,0:T(8,128)S(1)} fusion(bf16[128,64,128]{2,1,0:T(8,128)(2,1)S(1)} %bitcast.188, s32[64]{0:T(128)S(1)} %iota_add_fusion.1, s32[128,64]{0,1:T(8,128)} %copy-done.6), kind=kOutput, calls=%fused_computation.95 | convolution fusion | flops 142606336 | bytes 2162944 | tf_op jit(solution)/shard_map/jkr,jkc->rc/dot_general | solution.py:87
  334.4 8.8 %fusion.60 = f32[64,128]{1,0:T(8,128)S(1)} fusion(bf16[128,64,128]{2,1,0:T(8,128)(2,1)S(1)} %bitcast.189, s32[64]{0:T(128)S(1)} %iota_add_fusion.1, s32[128,64]{0,1:T(8,128)S(1)} %copy-done.7), kind=kOutput, calls=%fused_computation.96 | convolution fusion | flops 143130624 | bytes 2162944 | tf_op jit(solution)/shard_map/jkr,jkc->rc/dot_general | solution.py:88
  343.3 16.0 %fusion.19 = bf16[1,64,16384]{2,1,0:T(8,128)(2,1)} fusion(bf16[8192,64]{0,1:T(8,128)(2,1)S(1)} %copy-done.3, bf16[8192,64]{0,1:T(8,128)(2,1)S(1)} %copy-done.2, bf16[8192,64]{0,1:T(8,128)(2,1)S(1)} %get-tuple-element.152, bf16[64,64]{1,0:T(8,128)(2,1)S(1)} %get-tuple-element.147, bf16[64,64]{1,0:T(8,128)(2,1)S(1)} %get-tuple-element.146), kind=kOutput, calls=%fused_computation.24 | convolution fusion | flops 287342592 | bytes 5259264 | tf_op jit(solution)/shard_map/dot_general | solution.py:172
  (49 shorter events, 1.1 us)
Async XLA Ops:
  0.6 10.8 %copy-start = (bf16[1,64,16384]{2,1,0:T(8,128)(2,1)S(1)}, bf16[1,64,16384]{2,1,0:T(8,128)(2,1)}, u32[]{:S(2)}) copy-start(bf16[1,64,16384]{2,1,0:T(8,128)(2,1)} %param.10) | copy-start | bytes 6291460
  11.4 14.5 %copy-start.6 = (s32[128,64]{0,1:T(8,128)}, s32[128,64]{0,1:T(8,128)S(1)}, u32[]{:S(2)}) copy-start(s32[128,64]{0,1:T(8,128)S(1)} %add_select_fusion.6) | copy-start | bytes 98308
  38.2 31.8 %copy-start.4 = (f32[1,2,2,8192]{3,2,1,0:T(2,128)S(1)}, f32[1,2,2,8192]{3,2,1,0:T(2,128)}, u32[]{:S(2)}) copy-start(f32[1,2,2,8192]{3,2,1,0:T(2,128)} %param.15) | copy-start | bytes 393220
  38.2 32.0 %copy-start.8 = (f32[4,4,2,64]{3,2,1,0:T(2,128)S(1)}, f32[4,4,2,64]{3,2,1,0:T(2,128)}, u32[]{:S(2)}) copy-start(f32[4,4,2,64]{3,2,1,0:T(2,128)} %param.14) | copy-start | bytes 24580
  38.2 32.2 %copy-start.5 = (s32[3,2,8192]{2,1,0:T(2,128)S(1)}, s32[3,2,8192]{2,1,0:T(2,128)}, u32[]{:S(2)}) copy-start(s32[3,2,8192]{2,1,0:T(2,128)} %param.13) | copy-start | bytes 589828
  38.2 62.9 %all-to-all-start = ((bf16[128,64,128]{2,1,0:T(8,128)(2,1)}), bf16[128,64,128]{2,1,0:T(8,128)(2,1)}, u32[]{:S(2)}, u32[]{:S(2)}) async-start(bf16[128,64,128]{2,1,0:T(8,128)(2,1)} %copy.41), calls=%async_computation | async-start | bytes 4194304 | tf_op jit(solution)/shard_map/all_to_all | solution.py:115
  161.2 24.5 %copy-start.9 = (s32[2]{0:T(128)S(1)}, s32[2]{0:T(128)}, u32[]{:S(2)}) copy-start(s32[2]{0:T(128)} %param.12) | copy-start | bytes 28
  181.5 9.7 %all-to-all-start.1 = ((bf16[4,1,2,2,64,128]{5,4,3,2,1,0:T(8,128)(2,1)}), bf16[4,1,2,2,64,128]{5,4,3,2,1,0:T(8,128)(2,1)S(1)}, u32[]{:S(2)}, u32[]{:S(2)}) async-start(bf16[4,1,2,2,64,128]{5,4,3,2,1,0:T(8,128)(2,1)} %multiply_convert_fusion.8), calls=%async_computation.1 | async-start | bytes 524288 | tf_op jit(solution)/shard_map/all_to_all | solution.py:25
  192.2 8.9 %all-to-all-start.2 = ((bf16[4,1,2,2,64,128]{5,4,3,2,1,0:T(8,128)(2,1)}), bf16[4,1,2,2,64,128]{5,4,3,2,1,0:T(8,128)(2,1)S(1)}, u32[]{:S(2)}, u32[]{:S(2)}) async-start(bf16[4,1,2,2,64,128]{5,4,3,2,1,0:T(8,128)(2,1)} %multiply_convert_fusion.7), calls=%async_computation.2 | async-start | bytes 524288 | tf_op jit(solution)/shard_map/all_to_all | solution.py:25
  265.9 59.2 %all-to-all-start.3 = ((bf16[64,2,64,128]{3,2,1,0:T(8,128)(2,1)}), bf16[64,2,64,128]{3,2,1,0:T(8,128)(2,1)S(1)}, u32[]{:S(2)}, u32[]{:S(2)}) async-start(bf16[64,2,64,128]{3,2,1,0:T(8,128)(2,1)} %copy.47), calls=%async_computation.3 | async-start | bytes 4194304 | tf_op jit(solution)/shard_map/all_to_all | solution.py:168
  325.1 9.3 %copy-start.7 = (s32[128,64]{0,1:T(8,128)S(1)}, s32[128,64]{0,1:T(8,128)}, u32[]{:S(2)}) copy-start(s32[128,64]{0,1:T(8,128)} %copy-done.6) | copy-start | bytes 98308
  334.4 8.9 %copy-start.2 = (bf16[8192,64]{0,1:T(8,128)(2,1)S(1)}, bf16[8192,64]{0,1:T(8,128)(2,1)}, u32[]{:S(2)}) copy-start(bf16[8192,64]{0,1:T(8,128)(2,1)} %get-tuple-element.153) | copy-start | bytes 3145732
  334.4 8.9 %copy-start.3 = (bf16[8192,64]{0,1:T(8,128)(2,1)S(1)}, bf16[8192,64]{0,1:T(8,128)(2,1)}, u32[]{:S(2)}) copy-start(bf16[8192,64]{0,1:T(8,128)(2,1)} %get-tuple-element.154) | copy-start | bytes 3145732
  343.3 16.1 %copy-start.1 = (bf16[1,64,16384]{2,1,0:T(8,128)(2,1)S(1)}, bf16[1,64,16384]{2,1,0:T(8,128)(2,1)}, u32[]{:S(2)}) copy-start(bf16[1,64,16384]{2,1,0:T(8,128)(2,1)} %param.10) | copy-start | bytes 6291460
where the time goes:
time: 364 us; the launch traced here: 360 us
  matrix products  160 us (44%)
  waiting for transfers between devices  87.6 us (24%)
  other arithmetic  73.6 us (20%)
  starting transfers between devices  30.6 us (8%)
  local copies, waits for them, and re-layouts  5.85 us (2%)
    dot_general x4, matrix products, cein(): jnp.einsum(form, left_im, packed, preferred_element_type=jnp.float32)  52.5 us
    dot_general x4, matrix products, cein(): jnp.einsum(form, left_re, packed, preferred_element_type=jnp.float32)  52.2 us
    all_to_all x1, waiting for transfers between devices, body(): lax.all_to_all(patches_adj, 'facet', split_axis=0, concat_axis=0, tiled=T...  47.1 us
    all_to_all x1, waiting for transfers between devices, body(): lax.all_to_all(outgoing, 'facet', split_axis=0, concat_axis=0, tiled=True)  29.5 us
    another operation x9, other arithmetic  24.2 us
    reduce_sum x1, other arithmetic, body(): m_re = jnp.sum(y_re * w_re - y_im * w_im, -1)  19.5 us
    reduce_sum x1, other arithmetic, interp_table(): jnp.sum(cosine, 2) / (2.0 * samples)  18.3 us
    dot_general x1, matrix products, body(): lax.dot_general(sums.astype(jnp.bfloat16), column, (((1,), (1,)), ((), ()...  16 us
  transfers between devices with their start and end apart: 4, of which 4 were waited for; matrix products, arithmetic and copies ran while one was open for 6% of the time, Pallas kernels for 0%

commit v1 on v0

v1 whole, which is shorter than its diff:
```python
import functools
import math

import jax
import jax.numpy as jnp
import numpy as np
from jax import lax
from jax.experimental import pallas as pl
from jax.experimental.pallas import tpu as pltpu
from jax.sharding import PartitionSpec as P

K = 64
G = 256
L = 8192
PERIOD = 2048
ROWS = 64
FACETS = 64
TOTAL = 4096
MAXB = 64
BLOCK = 128
VISITS = 8192
CHUNK = 512

f32 = jnp.float32
bf16 = jnp.bfloat16


@functools.cache
def tables():
    lpos = np.arange(PERIOD)[None, :]
    cpos = np.arange(K)[:, None]
    angle = 2.0 * np.pi * ((4 * cpos * lpos) % L) / L
    column = np.concatenate([np.cos(angle), -np.sin(angle)], 0) / math.sqrt(L)
    upos = np.arange(G)[:, None]
    kpos = np.arange(K)[None, :]
    mpos = np.arange(K) - K // 2
    phase = (mpos[None, None, :] * (upos - 4 * kpos)[:, :, None]) % G
    interp = np.exp(2j * np.pi * phase / G).sum(2) / (2.0 * K)
    interp_t = np.concatenate([interp.real.T, interp.imag.T], 0)
    dpos = np.arange(ROWS) - ROWS // 2
    lift = interp @ np.exp(-2j * np.pi * np.arange(K)[:, None] * dpos[None, :] / 1024)
    lift = lift * np.exp(-2j * np.pi * upos / 128) / math.sqrt(TOTAL)
    lift_t = np.concatenate([lift.real.T, lift.imag.T], 0)
    lift_s = np.concatenate([-lift.imag.T, lift.real.T], 0)
    return (
        column.astype(np.float32),
        interp_t.astype(np.float32),
        lift_t.astype(np.float32),
        lift_s.astype(np.float32),
    )


def half_sign():
    lane = lax.broadcasted_iota(jnp.int32, (1, 2 * K), 1)
    return jnp.where(lane < K, 1.0, -1.0).astype(f32)


def swap(x):
    return pltpu.roll(x, K, 1)


def one_hot(cells):
    grid_pos = lax.broadcasted_iota(jnp.int32, (G, cells.shape[1]), 0)
    return jnp.where(grid_pos == cells, 1.0, 0.0).astype(bf16)


def nt_dot(a, b):
    return lax.dot_general(a, b, (((1,), (1,)), ((), ())), preferred_element_type=f32)


def column_kernel(strips_ref, column_ref, out_ref):
    parts = []
    for base in (0, L):
        folded = strips_ref[:, base : base + PERIOD].astype(f32)
        for turn in range(1, 4):
            start = base + turn * PERIOD
            folded = folded + strips_ref[:, start : start + PERIOD].astype(f32)
        parts.append(folded.astype(bf16))
    product = nt_dot(column_ref[...], jnp.concatenate(parts, 0))
    out_ref[...] = (product[:K] - half_sign() * swap(product[K:])).astype(bf16)


def weights_kernel(cells_ref, interp_ref, out_ref):
    for sub in range(2):

        def chunk(n, carry):
            at = pl.ds(pl.multiple_of(n * CHUNK, CHUNK), CHUNK)
            picked = jnp.dot(
                interp_ref[...], one_hot(cells_ref[1, sub : sub + 1, at]), preferred_element_type=f32
            )
            out_ref[sub, :, at] = picked.astype(bf16)
            return carry

        lax.fori_loop(0, VISITS // CHUNK, chunk, 0, unroll=2)


def facet_lift(cos_row, sin_row, lift_ref, lift_s_ref):
    return (cos_row * lift_ref[...] + sin_row * lift_s_ref[...]).astype(bf16)


def model_kernel(
    mine_ref, other_ref, cos_ref, sin_ref, fcos_ref, fsin_ref, lift_ref, lift_s_ref, cells_ref,
    weights_ref, seen_ref, out_ref, rows_ref, lifted_ref, samples_ref,
):
    sign = half_sign()
    rows_ref[...] = jnp.zeros_like(rows_ref)
    for side, source in enumerate((mine_ref, other_ref)):

        def pair(i, carry):
            lefts, rights = [], []
            for e in range(2):
                q = 2 * i + e
                p = side * 32 + q
                first = source[q].astype(f32)
                second = swap(first)
                rights.append(
                    facet_lift(fcos_ref[pl.ds(p, 1), :], fsin_ref[pl.ds(p, 1), :], lift_ref, lift_s_ref)
                )
                blocks = []
                for sub in range(2):
                    pr = cos_ref[pl.ds(sub * FACETS + p, 1), :]
                    pi = sin_ref[pl.ds(sub * FACETS + p, 1), :]
                    blocks.append((first * (pr * sign) - second * pi).astype(bf16))
                    blocks.append((second * pr + first * (pi * sign)).astype(bf16))
                lefts.append(jnp.concatenate(blocks, 0))
            left = jnp.concatenate(lefts, 1)
            right = jnp.concatenate(rights, 0)
            rows_ref[...] += jnp.dot(left, right, preferred_element_type=f32)
            return carry

        lax.fori_loop(0, 16, pair, 0, unroll=2)
    lifted_ref[...] = rows_ref[...].astype(bf16)
    per = CHUNK // BLOCK
    for sub in range(2):

        def chunk(n, carry):
            at = pl.ds(pl.multiple_of(n * CHUNK, CHUNK), CHUNK)
            picked = jnp.dot(
                lifted_ref[sub * 2 * K : (sub + 1) * 2 * K, :],
                one_hot(cells_ref[0, sub : sub + 1, at]),
                preferred_element_type=f32,
            )
            w_re = weights_ref[sub, :K, at].astype(f32)
            w_im = weights_ref[sub, K:, at].astype(f32)
            y_re, y_im = picked[:K], picked[K:]
            m_re = jnp.sum(y_re * w_re - y_im * w_im, 0, keepdims=True)
            m_im = jnp.sum(y_re * w_im + y_im * w_re, 0, keepdims=True)
            for b in range(per):
                lanes = slice(b * BLOCK, (b + 1) * BLOCK)
                samples_ref[pl.ds(2 * sub * MAXB + n * per + b, 1), :] = m_re[:, lanes]
                samples_ref[pl.ds((2 * sub + 1) * MAXB + n * per + b, 1), :] = m_im[:, lanes]
            return carry

        lax.fori_loop(0, VISITS // CHUNK, chunk, 0, unroll=2)
    out_ref[: 4 * MAXB, :] = samples_ref[...].astype(bf16)
    out_ref[4 * MAXB :, :] = seen_ref[...].astype(bf16)


def residual_kernel(
    counts_ref, a_ref, b_ref, c_ref, d_ref, seen_ref, mix_ref, cos_ref, sin_ref, cells_ref, weights_ref,
    resid_ref, out_ref, back_ref,
):
    planes = (a_ref, b_ref, c_ref, d_ref)
    block = lax.broadcasted_iota(jnp.int32, (MAXB, BLOCK), 0)
    for sub in range(2):
        live = block < counts_ref[sub]
        here = slice(sub * MAXB, (sub + 1) * MAXB)
        re = slice(2 * sub * MAXB, (2 * sub + 1) * MAXB)
        im = slice((2 * sub + 1) * MAXB, (2 * sub + 2) * MAXB)
        seen_re = slice(4 * MAXB + re.start, 4 * MAXB + re.stop)
        seen_im = slice(4 * MAXB + im.start, 4 * MAXB + im.stop)
        cosine, sine = cos_ref[here, :], sin_ref[here, :]
        s_re = [p[re, :].astype(f32) for p in planes]
        s_im = [p[im, :].astype(f32) for p in planes]
        back_re = jnp.zeros((MAXB, BLOCK), f32)
        back_im = jnp.zeros((MAXB, BLOCK), f32)
        for corr in range(4):
            mix = [mix_ref[here, 4 * corr + t : 4 * corr + t + 1] for t in range(4)]
            m_re = sum(m * s for m, s in zip(mix, s_re))
            m_im = sum(m * s for m, s in zip(mix, s_im))
            o_re = seen_ref[re, :] if corr == 0 else planes[corr][seen_re, :].astype(f32)
            o_im = seen_ref[im, :] if corr == 0 else planes[corr][seen_im, :].astype(f32)
            r_re = jnp.where(live, o_re - (m_re * cosine + m_im * sine), 0.0)
            r_im = jnp.where(live, o_im - (m_im * cosine - m_re * sine), 0.0)
            if corr == 0:
                resid_ref[re, :] = r_re
                resid_ref[im, :] = r_im
            back_re = back_re + mix[0] * r_re
            back_im = back_im + mix[0] * r_im
        back_ref[re, :] = back_re * cosine - back_im * sine
        back_ref[im, :] = back_im * cosine + back_re * sine
    per = CHUNK // BLOCK
    for sub in range(2):

        def chunk(n, total):
            at = pl.ds(pl.multiple_of(n * CHUNK, CHUNK), CHUNK)

            def row(part):
                base = (2 * sub + part) * MAXB + n * per
                return jnp.concatenate([back_ref[pl.ds(base + b, 1), :] for b in range(per)], 1)

            g_re, g_im = row(0), row(1)
            w_re = weights_ref[sub, :K, at].astype(f32)
            w_im = weights_ref[sub, K:, at].astype(f32)
            v_re = (g_re * w_re + g_im * w_im).astype(bf16)
            v_im = (g_im * w_re - g_re * w_im).astype(bf16)
            return total + nt_dot(one_hot(cells_ref[0, sub : sub + 1, at]), jnp.concatenate([v_re, v_im], 0))

        total = lax.fori_loop(0, VISITS // CHUNK, chunk, jnp.zeros((G, 2 * K), f32), unroll=2)
        out_ref[sub * 2 * K : (sub + 1) * 2 * K, :] = jnp.transpose(total).astype(bf16)


def share_kernel(
    mine_ref, other_ref, cos_ref, sin_ref, fcos_ref, fsin_ref, lift_ref, lift_s_ref, out_ref
):
    sign = half_sign()
    left = jnp.concatenate([mine_ref[...], other_ref[...]], 0)

    def pair(i, carry):
        rights = []
        for e in range(2):
            q = 2 * i + e
            rights.append(
                facet_lift(fcos_ref[pl.ds(q, 1), :], fsin_ref[pl.ds(q, 1), :], lift_ref, lift_s_ref)
            )
        product = nt_dot(left, jnp.concatenate(rights, 0))
        for e in range(2):
            q = 2 * i + e
            total = jnp.zeros((K, 2 * ROWS), f32)
            for sub in range(4):
                g_re = product[sub * 2 * K : sub * 2 * K + K, e * 128 : (e + 1) * 128]
                g_im = product[sub * 2 * K + K : (sub + 1) * 2 * K, e * 128 : (e + 1) * 128]
                g_re = g_re * sign
                pr = cos_ref[pl.ds(sub * 32 + q, 1), :]
                pi = sin_ref[pl.ds(sub * 32 + q, 1), :]
                total = total + (g_re + swap(g_im)) * pr + (swap(g_re) + g_im) * (pi * sign)
            out_ref[q] = total.astype(bf16)
        return carry

    lax.fori_loop(0, 16, pair, 0, unroll=2)


def image_kernel(shares_ref, column_ref, out_ref):
    total = shares_ref[0].astype(f32)
    for q in range(1, 32):
        total = total + shares_ref[q].astype(f32)
    total = total.astype(bf16).astype(f32)
    both = jnp.concatenate([total, half_sign() * swap(total)], 0)
    left = jnp.transpose(both).astype(bf16)
    image = (8.0 * jnp.dot(left, column_ref[...], preferred_element_type=f32)).astype(bf16)
    for turn in range(4):
        out_ref[:, turn * PERIOD : (turn + 1) * PERIOD] = image[:ROWS]
        out_ref[:, L + turn * PERIOD : L + (turn + 1) * PERIOD] = image[ROWS:]


def call(kernel, out_shape, scratch=(), smem=0, count=1):
    vmem = pl.BlockSpec(memory_space=pltpu.VMEM)

    def run(*args):
        specs = [pl.BlockSpec(memory_space=pltpu.SMEM)] * smem + [vmem] * (len(args) - smem)
        return pl.pallas_call(
            kernel,
            out_shape=out_shape,
            in_specs=specs,
            out_specs=jax.tree.map(lambda _: vmem, out_shape),
            scratch_shapes=list(scratch),
        )(*args)

    return run


def shape(dims, dtype):
    return jax.ShapeDtypeStruct(dims, dtype)


def turn(phase, period):
    angle = phase.astype(f32) * (2.0 * math.pi / period)
    return (jnp.cos(angle), -jnp.sin(angle))


def row_phases(offsets, facets):
    rows = facets[:, None] * ROWS + jnp.tile(jnp.arange(ROWS, dtype=jnp.int32), 2)[None, :]
    phase = (offsets[:, None, None] * rows[None]) % TOTAL
    cosine, sine = turn(phase.reshape(-1, 2 * ROWS), TOTAL)
    return (cosine, sine)


def facet_phases(facets):
    phase = (facets[:, None] * jnp.arange(G, dtype=jnp.int32)[None, :]) % FACETS
    return turn(phase, FACETS)


def body(strips, sub_u, counts, uvw, mueller, observed):
    column, interp_t, lift_t, lift_s = tables()
    column = jnp.asarray(column, bf16)
    interp_t = jnp.asarray(interp_t, bf16)
    lift_t = jnp.asarray(lift_t)
    lift_s = jnp.asarray(lift_s)
    here = lax.axis_index("facet")
    plane = lax.axis_index("stokes")
    core = here % 2
    groups = [[2 * q + side for q in range(32)] for side in range(2)]
    partner = [(i, i ^ 1) for i in range(FACETS)]
    step = jnp.arange(32, dtype=jnp.int32)

    coeffs = call(column_kernel, shape((K, 2 * ROWS), bf16))(strips[0], column)
    spread = jnp.broadcast_to(coeffs[None], (32, K, 2 * ROWS))
    mine = lax.all_to_all(spread, "facet", 0, 0, axis_index_groups=groups, tiled=True)
    other = lax.ppermute(mine, "facet", partner)

    weights = call(weights_kernel, shape((2, 2 * K, VISITS), bf16))(uvw, interp_t)
    own_facets = 2 * step + core
    other_facets = 2 * step + 1 - core
    offsets = lax.dynamic_slice_in_dim(sub_u, 2 * here, 2)
    other_offsets = lax.dynamic_slice_in_dim(sub_u, 2 * (here + 1 - 2 * core), 2)
    all_facets = jnp.concatenate([own_facets, other_facets])
    cos_f, sin_f = row_phases(offsets, all_facets)
    cos_a, sin_a = row_phases(jnp.concatenate([offsets, other_offsets]), own_facets)
    fcos, fsin = facet_phases(all_facets)
    seen = observed.reshape(4 * MAXB, BLOCK)
    vcos, vsin = turn(uvw[2].reshape(2 * MAXB, BLOCK), G)
    vsin = -vsin
    mix = jnp.concatenate([mueller, mueller], 0)
    mix = jnp.concatenate([mix, mix], 1)
    mix = lax.dynamic_slice(mix, (plane, plane, 0, 0), (4, 4, 2, MAXB))
    mix = jnp.transpose(mix.reshape(16, 2 * MAXB))

    sent = call(
        model_kernel,
        shape((8 * MAXB, BLOCK), bf16),
        (
            pltpu.VMEM((4 * K, G), f32),
            pltpu.VMEM((4 * K, G), bf16),
            pltpu.VMEM((4 * MAXB, BLOCK), f32),
        ),
    )(mine, other, cos_f, sin_f, fcos, fsin, lift_t, lift_s, uvw, weights, seen)
    planes = [sent] + [
        lax.ppermute(sent, "stokes", [(i, (i - k) % 4) for i in range(4)]) for k in (1, 2, 3)
    ]
    resid, adj = call(
        residual_kernel,
        (shape((4 * MAXB, BLOCK), f32), shape((4 * K, G), bf16)),
        (pltpu.VMEM((4 * MAXB, BLOCK), f32),),
        smem=1,
    )(counts, *planes, seen, mix, vcos, vsin, uvw, weights)
    other_adj = lax.ppermute(adj, "facet", partner)
    shares = call(share_kernel, shape((32, K, 2 * ROWS), bf16))(
        adj, other_adj, cos_a, sin_a, fcos[:32], fsin[:32], lift_t, lift_s
    )
    shares = lax.all_to_all(shares, "facet", 0, 0, axis_index_groups=groups, tiled=True)
    image = call(image_kernel, shape((ROWS, 2 * L), bf16))(shares, column)
    return (image[None], resid.reshape(1, 2, 2, VISITS))


def solution(mesh):
    placed = (
        P("stokes", "facet", None),
        P(),
        P("facet"),
        P(None, "facet", None),
        P(None, None, "facet", None),
        P("stokes", "facet", None, None),
    )
    return jax.shard_map(
        body,
        mesh=mesh,
        in_specs=placed,
        out_specs=(P("stokes", "facet", None), P("stokes", "facet", None, None)),
        check_vma=False,
    )
```

time: 364 us -> 108 us (0.30); the launches traced: 360 us -> 108 us
  matrix products: 160 us -> 0 us
  other arithmetic: 73.6 us -> 5.06 us
  waiting for transfers between devices: 87.6 us -> 27.9 us
  Pallas kernels: 0 us -> 41.2 us
  starting transfers between devices: 30.6 us -> 22.9 us
  local copies, waits for them, and re-layouts: 5.85 us -> 9.92 us
    dot_general x16 -> x0, matrix products: 160 us -> none  [the longest x4 52.5 us: cein(): jnp.einsum(form, left_im, packed, preferred_element_type=jnp.float32)]
    all_to_all x4 -> x2, waiting for transfers between devices: 87.6 us -> 22.4 us  [the longest x1 15.9 us: body(): lax.all_to_all(shares, 'facet', 0, 0, axis_index_groups=groups, tiled=True)]
    pallas_call x0 -> x6, Pallas kernels: none -> 41.2 us  [run(): pl.pallas_call(kernel, out_shape=out_shape, in_specs=specs, out_specs=jax...]
    reduce_sum x4 -> x0, other arithmetic: 37.8 us -> none  [the longest x1 19.5 us: body(): m_re = jnp.sum(y_re * w_re - y_im * w_im, -1)]
    another operation x9 -> x0, other arithmetic: 24.2 us -> none
    all_to_all x4 -> x2, starting transfers between devices: 30.6 us -> 16.2 us  [the longest x1 11.9 us: body(): lax.all_to_all(spread, 'facet', 0, 0, axis_index_groups=groups, tiled=True)]
    ppermute x0 -> x5, starting transfers between devices: none -> 6.69 us  [the longest x3 3.78 us: body(): lax.ppermute(sent, 'stokes', [(i, (i - k) % 4) for i in range(4)])]
    ppermute x0 -> x5, waiting for transfers between devices: none -> 5.41 us  [the longest x3 5.28 us: body(): lax.ppermute(sent, 'stokes', [(i, (i - k) % 4) for i in range(4)])]
  transfers between devices with their start and end apart: 4 -> 7, of which waited for: 4 -> 6; matrix products, arithmetic and copies ran while one was open for 6% -> 10% of each run, Pallas kernels for 0% -> 6%
where the time goes in v1:
time: 108 us
  Pallas kernels  41.2 us (38%)
  waiting for transfers between devices  27.9 us (26%)
  starting transfers between devices  22.9 us (21%)
  local copies, waits for them, and re-layouts  9.92 us (9%)
  other arithmetic  5.06 us (5%)
    pallas_call x6, Pallas kernels, run(): pl.pallas_call(kernel, out_shape=out_shape, in_specs=specs, out_specs=jax...  41.2 us
    all_to_all x1, waiting for transfers between devices, body(): lax.all_to_all(shares, 'facet', 0, 0, axis_index_groups=groups, tiled=True)  15.9 us
    all_to_all x1, starting transfers between devices, body(): lax.all_to_all(spread, 'facet', 0, 0, axis_index_groups=groups, tiled=True)  11.9 us
    all_to_all x1, waiting for transfers between devices, body(): lax.all_to_all(spread, 'facet', 0, 0, axis_index_groups=groups, tiled=True)  6.58 us
    ppermute x3, waiting for transfers between devices, body(): lax.ppermute(sent, 'stokes', [(i, (i - k) % 4) for i in range(4)])  5.28 us
    all_to_all x1, starting transfers between devices, body(): lax.all_to_all(shares, 'facet', 0, 0, axis_index_groups=groups, tiled=True)  4.37 us
    ppermute x3, starting transfers between devices, body(): lax.ppermute(sent, 'stokes', [(i, (i - k) % 4) for i in range(4)])  3.78 us
    neg x3, other arithmetic, turn(): return (jnp.cos(angle), -jnp.sin(angle))  2.97 us
  transfers between devices with their start and end apart: 7, of which 6 were waited for; matrix products, arithmetic and copies ran while one was open for 10% of the time, Pallas kernels for 6%

profile of v1, /device:TPU:1, one launch (start us, length us, event | category | flops | bytes accessed | tf_op | source)
XLA Modules:
  0.0 107.7 jit_solution(6272577401488170705)
XLA Ops:
  0.6 2.8 %shard_map.113 = bf16[64,128]{1,0:T(8,128)(2,1)} custom-call(bf16[64,16384]{1,0:T(8,128)(2,1)} %bitcast.43, bf16[128,2048]{1,0:T(8,128)(2,1)} %constant.82.clone.column_ref), custom_call_target="tpu_custom_call" | custom-call | tf_op jit(solution)/shard_map/pallas_call | solution.py:261
  3.5 1.6 %broadcast_in_dim.4 = bf16[32,64,128]{2,1,0:T(8,128)(2,1)} broadcast(bf16[64,128]{1,0:T(8,128)(2,1)} %shard_map.113), dimensions={1,2} | broadcast | bytes 540672 | tf_op jit(solution)/shard_map/broadcast_in_dim | solution.py:307
  5.1 11.9 %all-to-all-start = ((bf16[32,64,128]{2,1,0:T(8,128)(2,1)}), bf16[32,64,128]{2,1,0:T(8,128)(2,1)S(1)}, u32[]{:S(2)}, u32[]{:S(2)}) async-start(bf16[32,64,128]{2,1,0:T(8,128)(2,1)} %broadcast_in_dim.4), calls=%async_computation | async-start | bytes 1048576 | tf_op jit(solution)/shard_map/all_to_all | solution.py:308
  17.0 0.1 fusion.27
  17.1 0.1 mul.118
  17.2 0.1 mul.119
  17.3 0.1 add.102
  17.3 0.8 reshape.110.seen_ref
  18.1 0.1 broadcast_multiply_fusion.1
  18.2 6.7 %shard_map.114.weights_ref = bf16[2,128,8192]{2,1,0:T(8,128)(2,1)} custom-call(s32[3,2,8192]{2,1,0:T(2,128)} %cells_ref.5, bf16[128,256]{1,0:T(8,128)(2,1)} %constant.83.clone.interp_ref), custom_call_target="tpu_custom_call" | custom-call | tf_op jit(solution)/shard_map/pallas_call | solution.py:261
  24.9 1.7 %fusion.18 = (f32[1,2,8192]{2,1,0:T(2,128)S(1)}, f32[1,2,8192]{2,1,0:T(2,128)S(1)}) fusion(s32[3,2,8192]{2,1,0:T(2,128)} %cells_ref.5), kind=kLoop, calls=%fused_computation.37 | loop fusion | flops 32768 | bytes 196608 | tf_op jit(solution)/shard_map/sin | solution.py:278
  26.7 6.6 %all-to-all-done.mine_ref = bf16[32,64,128]{2,1,0:T(8,128)(2,1)S(1)} async-done(((bf16[32,64,128]{2,1,0:T(8,128)(2,1)}), bf16[32,64,128]{2,1,0:T(8,128)(2,1)S(1)}, u32[]{:S(2)}, u32[]{:S(2)}) %all-to-all-start) | async-done | bytes 524320 | tf_op jit(solution)/shard_map/all_to_all | solution.py:308
  33.3 2.4 %collective-permute-start = (bf16[32,64,128]{2,1,0:T(8,128)(2,1)S(1)}, bf16[32,64,128]{2,1,0:T(8,128)(2,1)S(1)}, u32[]{:S(2)}, u32[]{:S(2)}) collective-permute-start(bf16[32,64,128]{2,1,0:T(8,128)(2,1)S(1)} %all-to-all-done.mine_ref), channel_id=1, source_target_pairs={{0,4},{4,0},{8,12},{12,8},{16,20},{20,16},{24,28},{28,24},{32,36},... | collective-permute-start | bytes 1572872 | tf_op jit(solution)/shard_map/ppermute | solution.py:309
  35.7 0.1 broadcast_add_fusion
  35.8 1.0 sine_negate_fusion.2
  36.7 0.1 fusion.23
  36.8 1.0 sine_negate_fusion.1
  37.8 0.0 collective-permute-done.other_ref
  37.8 0.8 copy-done.2
  38.6 12.7 %shard_map.115.a_ref = bf16[512,128]{1,0:T(8,128)(2,1)} custom-call(bf16[32,64,128]{2,1,0:T(8,128)(2,1)} %copy-done, bf16[32,64,128]{2,1,0:T(8,128)(2,1)} %copy-done.2, f32[128,128]{1,0:T(8,128)} %get-tuple-element.11.cos_ref, f32[128,128]{1,0:T(8,128)} %get-tuple-element.10.sin_ref, f32[64,256]{1,0:T(8,128)} %get-tuple-element.17.fcos_ref, ...), custom_call_target="tpu_custom_call" | custom-call | tf_op jit(solution)/shard_map/pallas_call | solution.py:261
  51.3 2.7 %collective-permute-start.1 = (bf16[512,128]{1,0:T(8,128)(2,1)}, bf16[512,128]{1,0:T(8,128)(2,1)S(1)}, u32[]{:S(2)}, u32[]{:S(2)}) collective-permute-start(bf16[512,128]{1,0:T(8,128)(2,1)} %shard_map.115.a_ref), channel_id=1, source_target_pairs={{0,3},{1,0},{2,1},{3,2},{4,7},{5,4},{6,5},{7,6},{8,11},{9,8},{10,9... | collective-permute-start | bytes 393224 | tf_op jit(solution)/shard_map/ppermute | solution.py:338
  54.0 0.3 collective-permute-start.2
  54.4 0.7 collective-permute-start.3
  55.1 0.1 pad_add_fusion.1
  55.1 0.6 slice.12.fcos_ref
  55.8 0.6 slice.13.fsin_ref
  56.4 0.1 reshape.111
  56.4 0.7 copy.13
  57.2 0.7 cos.17.cos_ref
  57.8 0.7 sin.18.sin_ref
  58.5 0.1 mul.137
  58.6 0.1 mul.138
  58.7 1.2 %collective-permute-done.1.b_ref = bf16[512,128]{1,0:T(8,128)(2,1)S(1)} collective-permute-done((bf16[512,128]{1,0:T(8,128)(2,1)}, bf16[512,128]{1,0:T(8,128)(2,1)S(1)}, u32[]{:S(2)}, u32[]{:S(2)}) %collective-permute-start.1) | collective-permute-done | bytes 131104 | tf_op jit(solution)/shard_map/ppermute | solution.py:338
  59.8 0.7 collective-permute-done.2.c_ref
  60.5 3.4 %collective-permute-done.3.d_ref = bf16[512,128]{1,0:T(8,128)(2,1)S(1)} collective-permute-done((bf16[512,128]{1,0:T(8,128)(2,1)}, bf16[512,128]{1,0:T(8,128)(2,1)S(1)}, u32[]{:S(2)}, u32[]{:S(2)}) %collective-permute-start.3) | collective-permute-done | bytes 131104 | tf_op jit(solution)/shard_map/ppermute | solution.py:338
  64.0 0.6 copy-done.7
  64.6 9.5 %shard_map.116 = (f32[256,128]{1,0:T(8,128)}, bf16[256,256]{1,0:T(8,128)(2,1)}) custom-call(s32[2]{0:T(128)} %counts_ref.1, bf16[512,128]{1,0:T(8,128)(2,1)} %shard_map.115.a_ref, bf16[512,128]{1,0:T(8,128)(2,1)} %copy-done.5, bf16[512,128]{1,0:T(8,128)(2,1)} %copy-done.6, bf16[512,128]{1,0:T(8,128)(2,1)} %copy-done.7, f32[256,128]{1,0:T(8,128)} %reshape.110.seen_ref, ...), custom_call_target="tpu_custom_call" | custom-call | tf_op jit(solution)/shard_map/pallas_call | solution.py:261
  74.1 0.5 collective-permute-start.4
  74.6 0.1 broadcast_add_fusion.1
  74.7 1.0 sine_negate_fusion
  75.7 0.1 collective-permute-done.4.other_ref
  75.8 0.7 copy-done.8
  76.5 6.4 %shard_map.117 = bf16[32,64,128]{2,1,0:T(8,128)(2,1)} custom-call(bf16[256,256]{1,0:T(8,128)(2,1)} %get-tuple-element.4.mine_ref, bf16[256,256]{1,0:T(8,128)(2,1)} %copy-done.8, f32[128,128]{1,0:T(8,128)} %get-tuple-element.13.cos_ref, f32[128,128]{1,0:T(8,128)} %get-tuple-element.12.sin_ref, f32[32,256]{1,0:T(8,128)} %slice.12.fcos_ref, ...), custom_call_target="tpu_custom_call" | custom-call | tf_op jit(solution)/shard_map/pallas_call | solution.py:261
  82.9 4.4 %all-to-all-start.1 = ((bf16[32,64,128]{2,1,0:T(8,128)(2,1)}), bf16[32,64,128]{2,1,0:T(8,128)(2,1)S(1)}, u32[]{:S(2)}, u32[]{:S(2)}) async-start(bf16[32,64,128]{2,1,0:T(8,128)(2,1)} %shard_map.117), calls=%async_computation.1 | async-start | bytes 1048576 | tf_op jit(solution)/shard_map/all_to_all | solution.py:350
  87.3 0.7 reshape.112
  88.0 15.9 %all-to-all-done.1.shares_ref = bf16[32,64,128]{2,1,0:T(8,128)(2,1)S(1)} async-done(((bf16[32,64,128]{2,1,0:T(8,128)(2,1)}), bf16[32,64,128]{2,1,0:T(8,128)(2,1)S(1)}, u32[]{:S(2)}, u32[]{:S(2)}) %all-to-all-start.1) | async-done | bytes 524320 | tf_op jit(solution)/shard_map/all_to_all | solution.py:350
  103.9 0.8 copy-done.1
  104.7 3.0 %shard_map.118 = bf16[64,16384]{1,0:T(8,128)(2,1)} custom-call(bf16[32,64,128]{2,1,0:T(8,128)(2,1)} %copy-done.1, bf16[128,2048]{1,0:T(8,128)(2,1)} %constant.82.clone.column_ref), custom_call_target="tpu_custom_call" | custom-call | tf_op jit(solution)/shard_map/pallas_call | solution.py:261
  (25 shorter events, 0.1 us)
Async XLA Ops:
  0.6 16.4 %copy-start.12 = (s32[128]{0:T(128)S(1)}, s32[128]{0:T(128)}, u32[]{:S(2)}) copy-start(s32[128]{0:T(128)} %param.11) | copy-start | bytes 1540
  0.6 16.7 %copy-start.9 = (f32[1,2,2,8192]{3,2,1,0:T(2,128)S(1)}, f32[1,2,2,8192]{3,2,1,0:T(2,128)}, u32[]{:S(2)}) copy-start(f32[1,2,2,8192]{3,2,1,0:T(2,128)} %param.15) | copy-start | bytes 393220
  5.1 28.1 %all-to-all-start = ((bf16[32,64,128]{2,1,0:T(8,128)(2,1)}), bf16[32,64,128]{2,1,0:T(8,128)(2,1)S(1)}, u32[]{:S(2)}, u32[]{:S(2)}) async-start(bf16[32,64,128]{2,1,0:T(8,128)(2,1)} %broadcast_in_dim.4), calls=%async_computation | async-start | bytes 1048576 | tf_op jit(solution)/shard_map/all_to_all | solution.py:308
  18.2 18.6 %copy-start.11 = (f32[4,4,2,64]{3,2,1,0:T(2,128)S(1)}, f32[4,4,2,64]{3,2,1,0:T(2,128)}, u32[]{:S(2)}) copy-start(f32[4,4,2,64]{3,2,1,0:T(2,128)} %param.14) | copy-start | bytes 24580
  33.3 4.6 %copy-start = (bf16[32,64,128]{2,1,0:T(8,128)(2,1)}, bf16[32,64,128]{2,1,0:T(8,128)(2,1)S(1)}, u32[]{:S(2)}) copy-start(bf16[32,64,128]{2,1,0:T(8,128)(2,1)S(1)} %all-to-all-done.mine_ref) | copy-start | bytes 1572868
  33.3 4.5 %collective-permute-start = (bf16[32,64,128]{2,1,0:T(8,128)(2,1)S(1)}, bf16[32,64,128]{2,1,0:T(8,128)(2,1)S(1)}, u32[]{:S(2)}, u32[]{:S(2)}) collective-permute-start(bf16[32,64,128]{2,1,0:T(8,128)(2,1)S(1)} %all-to-all-done.mine_ref), channel_id=1, source_target_pairs={{0,4},{4,0},{8,12},{12,8},{16,20},{20,16},{24,28},{28,24},{32,36},... | collective-permute-start | bytes 1572872 | tf_op jit(solution)/shard_map/ppermute | solution.py:309
  37.8 0.8 copy-start.2
  38.6 16.5 %copy-start.4 = (f32[64,256]{1,0:T(8,128)S(1)}, f32[64,256]{1,0:T(8,128)}, u32[]{:S(2)}) copy-start(f32[64,256]{1,0:T(8,128)} %get-tuple-element.17.fcos_ref) | copy-start | bytes 196612
  38.6 17.1 %copy-start.3 = (f32[64,256]{1,0:T(8,128)S(1)}, f32[64,256]{1,0:T(8,128)}, u32[]{:S(2)}) copy-start(f32[64,256]{1,0:T(8,128)} %get-tuple-element.16.fsin_ref) | copy-start | bytes 196612
  51.3 8.6 %collective-permute-start.1 = (bf16[512,128]{1,0:T(8,128)(2,1)}, bf16[512,128]{1,0:T(8,128)(2,1)S(1)}, u32[]{:S(2)}, u32[]{:S(2)}) collective-permute-start(bf16[512,128]{1,0:T(8,128)(2,1)} %shard_map.115.a_ref), channel_id=1, source_target_pairs={{0,3},{1,0},{2,1},{3,2},{4,7},{5,4},{6,5},{7,6},{8,11},{9,8},{10,9... | collective-permute-start | bytes 393224 | tf_op jit(solution)/shard_map/ppermute | solution.py:338
  54.0 6.5 %collective-permute-start.2 = (bf16[512,128]{1,0:T(8,128)(2,1)}, bf16[512,128]{1,0:T(8,128)(2,1)S(1)}, u32[]{:S(2)}, u32[]{:S(2)}) collective-permute-start(bf16[512,128]{1,0:T(8,128)(2,1)} %shard_map.115.a_ref), channel_id=1, source_target_pairs={{0,2},{1,3},{2,0},{3,1},{4,6},{5,7},{6,4},{7,5},{8,10},{9,11},{10,... | collective-permute-start | bytes 393224 | tf_op jit(solution)/shard_map/ppermute | solution.py:338
  54.4 9.6 %collective-permute-start.3 = (bf16[512,128]{1,0:T(8,128)(2,1)}, bf16[512,128]{1,0:T(8,128)(2,1)S(1)}, u32[]{:S(2)}, u32[]{:S(2)}) collective-permute-start(bf16[512,128]{1,0:T(8,128)(2,1)} %shard_map.115.a_ref), channel_id=1, source_target_pairs={{0,1},{1,2},{2,3},{3,0},{4,5},{5,6},{6,7},{7,4},{8,9},{9,10},{10,1... | collective-permute-start | bytes 393224 | tf_op jit(solution)/shard_map/ppermute | solution.py:338
  59.8 4.1 %copy-start.5 = (bf16[512,128]{1,0:T(8,128)(2,1)}, bf16[512,128]{1,0:T(8,128)(2,1)S(1)}, u32[]{:S(2)}) copy-start(bf16[512,128]{1,0:T(8,128)(2,1)S(1)} %collective-permute-done.1.b_ref) | copy-start | bytes 393220
  60.5 3.4 %copy-start.6 = (bf16[512,128]{1,0:T(8,128)(2,1)}, bf16[512,128]{1,0:T(8,128)(2,1)S(1)}, u32[]{:S(2)}) copy-start(bf16[512,128]{1,0:T(8,128)(2,1)S(1)} %collective-permute-done.2.c_ref) | copy-start | bytes 393220
  64.0 0.6 copy-start.7
  74.1 13.1 %copy-start.10 = (f32[256,128]{1,0:T(8,128)S(1)}, f32[256,128]{1,0:T(8,128)}, u32[]{:S(2)}) copy-start(f32[256,128]{1,0:T(8,128)} %get-tuple-element.5) | copy-start | bytes 393220
  74.1 1.7 %collective-permute-start.4 = (bf16[256,256]{1,0:T(8,128)(2,1)}, bf16[256,256]{1,0:T(8,128)(2,1)S(1)}, u32[]{:S(2)}, u32[]{:S(2)}) collective-permute-start(bf16[256,256]{1,0:T(8,128)(2,1)} %get-tuple-element.4.mine_ref), channel_id=1, source_target_pairs={{0,4},{4,0},{8,12},{12,8},{16,20},{20,16},{24,28},{28,24},{32,36},... | collective-permute-start | bytes 393224 | tf_op jit(solution)/shard_map/ppermute | solution.py:346
  75.8 0.7 copy-start.8
  82.9 21.0 %all-to-all-start.1 = ((bf16[32,64,128]{2,1,0:T(8,128)(2,1)}), bf16[32,64,128]{2,1,0:T(8,128)(2,1)S(1)}, u32[]{:S(2)}, u32[]{:S(2)}) async-start(bf16[32,64,128]{2,1,0:T(8,128)(2,1)} %shard_map.117), calls=%async_computation.1 | async-start | bytes 1048576 | tf_op jit(solution)/shard_map/all_to_all | solution.py:350
  103.9 0.8 copy-start.1

commit v2 on v1

--- a/solution.py
+++ b/solution.py
@@ -29,14 +29,14 @@
 def tables():
     lpos = np.arange(PERIOD)[None, :]
     cpos = np.arange(K)[:, None]
-    angle = 2.0 * np.pi * ((4 * cpos * lpos) % L) / L
+    angle = 2.0 * np.pi * ((4 * cpos * (lpos - 16)) % L) / L
     column = np.concatenate([np.cos(angle), -np.sin(angle)], 0) / math.sqrt(L)
     upos = np.arange(G)[:, None]
     kpos = np.arange(K)[None, :]
     mpos = np.arange(K) - K // 2
     phase = (mpos[None, None, :] * (upos - 4 * kpos)[:, :, None]) % G
     interp = np.exp(2j * np.pi * phase / G).sum(2) / (2.0 * K)
-    interp_t = np.concatenate([interp.real.T, interp.imag.T], 0)
+    kernel_t = (interp * np.exp(2j * np.pi * (upos - 4 * kpos) / 512)).real.T
     dpos = np.arange(ROWS) - ROWS // 2
     lift = interp @ np.exp(-2j * np.pi * np.arange(K)[:, None] * dpos[None, :] / 1024)
     lift = lift * np.exp(-2j * np.pi * upos / 128) / math.sqrt(TOTAL)
@@ -44,7 +44,7 @@
     lift_s = np.concatenate([-lift.imag.T, lift.real.T], 0)
     return (
         column.astype(np.float32),
-        interp_t.astype(np.float32),
+        kernel_t.astype(np.float32),
         lift_t.astype(np.float32),
         lift_s.astype(np.float32),
     )
@@ -77,18 +77,86 @@
             folded = folded + strips_ref[:, start : start + PERIOD].astype(f32)
         parts.append(folded.astype(bf16))
     product = nt_dot(column_ref[...], jnp.concatenate(parts, 0))
-    out_ref[...] = (product[:K] - half_sign() * swap(product[K:])).astype(bf16)
-
-
-def weights_kernel(cells_ref, interp_ref, out_ref):
+    coeffs = (product[:K] - half_sign() * swap(product[K:])).astype(bf16)
+    for q in range(32):
+        out_ref[q] = coeffs
+
+
+def turn(n, period):
+    t = n.astype(f32) * (4.0 / period)
+    q = jnp.floor(t + 0.5)
+    x = (t - q) * (math.pi / 2)
+    quarter = q.astype(jnp.int32) & 3
+    y = x * x
+    s = x * (1.0 + y * (-1.0 / 6 + y * (1.0 / 120 + y * (-1.0 / 5040 + y * (1.0 / 362880)))))
+    c = 1.0 + y * (-0.5 + y * (1.0 / 24 + y * (-1.0 / 720 + y * (1.0 / 40320))))
+    odd = (quarter & 1) == 1
+    cosine = jnp.where(odd, s, c)
+    sine = jnp.where(odd, c, s)
+    cosine = jnp.where((quarter == 1) | (quarter == 2), -cosine, cosine)
+    sine = jnp.where(quarter >= 2, sine, -sine)
+    return cosine, sine
+
+
+def prepare_kernel(
+    here_ref, sub_ref, cells_ref, kernel_ref, mueller_ref, observed_ref,
+    cos_ref, sin_ref, acos_ref, asin_ref, fcos_ref, fsin_ref, vcos_ref, vsin_ref, mix_ref,
+    seen_ref, sent_ref, weights_ref, steps_ref, rows_ref,
+):
+    here, plane = here_ref[0], here_ref[1]
+    core = here & 1
+    step = lax.broadcasted_iota(jnp.int32, (32, 2 * ROWS), 0)
+    lane = lax.broadcasted_iota(jnp.int32, (32, 2 * ROWS), 1) & (ROWS - 1)
+    mine = (2 * step + core) * ROWS + lane
+    other = (2 * step + 1 - core) * ROWS + lane
+    for sub in range(2):
+        offset = sub_ref[2 * here + sub]
+        cosine, sine = turn((mine * offset) & (TOTAL - 1), TOTAL)
+        cos_ref[sub * FACETS : sub * FACETS + 32, :] = cosine
+        sin_ref[sub * FACETS : sub * FACETS + 32, :] = sine
+        acos_ref[sub * 32 : sub * 32 + 32, :] = cosine
+        asin_ref[sub * 32 : sub * 32 + 32, :] = sine
+        cosine, sine = turn((other * offset) & (TOTAL - 1), TOTAL)
+        cos_ref[sub * FACETS + 32 : (sub + 1) * FACETS, :] = cosine
+        sin_ref[sub * FACETS + 32 : (sub + 1) * FACETS, :] = sine
+        offset = sub_ref[2 * (here + 1 - 2 * core) + sub]
+        cosine, sine = turn((mine * offset) & (TOTAL - 1), TOTAL)
+        acos_ref[64 + sub * 32 : 96 + sub * 32, :] = cosine
+        asin_ref[64 + sub * 32 : 96 + sub * 32, :] = sine
+    step = lax.broadcasted_iota(jnp.int32, (32, G), 0)
+    lane = lax.broadcasted_iota(jnp.int32, (32, G), 1)
+    for side, facet in enumerate((2 * step + core, 2 * step + 1 - core)):
+        cosine, sine = turn((facet * lane) & (FACETS - 1), FACETS)
+        fcos_ref[side * 32 : side * 32 + 32, :] = cosine
+        fsin_ref[side * 32 : side * 32 + 32, :] = sine
+    for sub in range(2):
+        for b in range(MAXB):
+            lanes = slice(b * BLOCK, (b + 1) * BLOCK)
+            steps_ref[sub * MAXB + b : sub * MAXB + b + 1, :] = (
+                2 * cells_ref[2, sub : sub + 1, lanes] + cells_ref[1, sub : sub + 1, lanes]
+            )
+            for part in range(2):
+                at = (2 * sub + part) * MAXB + b
+                seen_ref[at : at + 1, :] = observed_ref[sub, part : part + 1, lanes]
+    sent_ref[...] = seen_ref[...].astype(bf16)
+    cosine, sine = turn(steps_ref[...] & (2 * G - 1), 2 * G)
+    vcos_ref[...] = cosine
+    vsin_ref[...] = -sine
+    rows_ref[...] = jnp.zeros_like(rows_ref)
+    for corr in range(4):
+        for t in range(4):
+            entry = mueller_ref[(plane + corr) & 3, (plane + t) & 3]
+            at = 4 * corr + t
+            rows_ref[at : at + 1, :] = jnp.concatenate([entry[0:1, :], entry[1:2, :]], 1)
+    mix_ref[...] = jnp.transpose(rows_ref[...])
     for sub in range(2):
 
         def chunk(n, carry):
             at = pl.ds(pl.multiple_of(n * CHUNK, CHUNK), CHUNK)
             picked = jnp.dot(
-                interp_ref[...], one_hot(cells_ref[1, sub : sub + 1, at]), preferred_element_type=f32
+                kernel_ref[...], one_hot(cells_ref[1, sub : sub + 1, at]), preferred_element_type=f32
             )
-            out_ref[sub, :, at] = picked.astype(bf16)
+            weights_ref[sub, :, at] = picked.astype(bf16)
             return carry
 
         lax.fori_loop(0, VISITS // CHUNK, chunk, 0, unroll=2)
@@ -100,7 +168,7 @@
 
 def model_kernel(
     mine_ref, other_ref, cos_ref, sin_ref, fcos_ref, fsin_ref, lift_ref, lift_s_ref, cells_ref,
-    weights_ref, seen_ref, out_ref, rows_ref, lifted_ref, samples_ref,
+    weights_ref, out_ref, rows_ref, lifted_ref, samples_ref,
 ):
     sign = half_sign()
     rows_ref[...] = jnp.zeros_like(rows_ref)
@@ -140,11 +208,9 @@
                 one_hot(cells_ref[0, sub : sub + 1, at]),
                 preferred_element_type=f32,
             )
-            w_re = weights_ref[sub, :K, at].astype(f32)
-            w_im = weights_ref[sub, K:, at].astype(f32)
-            y_re, y_im = picked[:K], picked[K:]
-            m_re = jnp.sum(y_re * w_re - y_im * w_im, 0, keepdims=True)
-            m_im = jnp.sum(y_re * w_im + y_im * w_re, 0, keepdims=True)
+            weight = weights_ref[sub, :, at].astype(f32)
+            m_re = jnp.sum(picked[:K] * weight, 0, keepdims=True)
+            m_im = jnp.sum(picked[K:] * weight, 0, keepdims=True)
             for b in range(per):
                 lanes = slice(b * BLOCK, (b + 1) * BLOCK)
                 samples_ref[pl.ds(2 * sub * MAXB + n * per + b, 1), :] = m_re[:, lanes]
@@ -152,23 +218,21 @@
             return carry
 
         lax.fori_loop(0, VISITS // CHUNK, chunk, 0, unroll=2)
-    out_ref[: 4 * MAXB, :] = samples_ref[...].astype(bf16)
-    out_ref[4 * MAXB :, :] = seen_ref[...].astype(bf16)
+    out_ref[...] = samples_ref[...].astype(bf16)
 
 
 def residual_kernel(
-    counts_ref, a_ref, b_ref, c_ref, d_ref, seen_ref, mix_ref, cos_ref, sin_ref, cells_ref, weights_ref,
+    counts_ref, a_ref, b_ref, c_ref, d_ref, oa_ref, ob_ref, oc_ref, od_ref, mix_ref, cos_ref, sin_ref, cells_ref, weights_ref,
     resid_ref, out_ref, back_ref,
 ):
     planes = (a_ref, b_ref, c_ref, d_ref)
+    seen = (oa_ref, ob_ref, oc_ref, od_ref)
     block = lax.broadcasted_iota(jnp.int32, (MAXB, BLOCK), 0)
     for sub in range(2):
         live = block < counts_ref[sub]
         here = slice(sub * MAXB, (sub + 1) * MAXB)
         re = slice(2 * sub * MAXB, (2 * sub + 1) * MAXB)
         im = slice((2 * sub + 1) * MAXB, (2 * sub + 2) * MAXB)
-        seen_re = slice(4 * MAXB + re.start, 4 * MAXB + re.stop)
-        seen_im = slice(4 * MAXB + im.start, 4 * MAXB + im.stop)
         cosine, sine = cos_ref[here, :], sin_ref[here, :]
         s_re = [p[re, :].astype(f32) for p in planes]
         s_im = [p[im, :].astype(f32) for p in planes]
@@ -178,8 +242,8 @@
             mix = [mix_ref[here, 4 * corr + t : 4 * corr + t + 1] for t in range(4)]
             m_re = sum(m * s for m, s in zip(mix, s_re))
             m_im = sum(m * s for m, s in zip(mix, s_im))
-            o_re = seen_ref[re, :] if corr == 0 else planes[corr][seen_re, :].astype(f32)
-            o_im = seen_ref[im, :] if corr == 0 else planes[corr][seen_im, :].astype(f32)
+            o_re = seen[corr][re, :].astype(f32)
+            o_im = seen[corr][im, :].astype(f32)
             r_re = jnp.where(live, o_re - (m_re * cosine + m_im * sine), 0.0)
             r_im = jnp.where(live, o_im - (m_im * cosine - m_re * sine), 0.0)
             if corr == 0:
@@ -200,10 +264,9 @@
                 return jnp.concatenate([back_ref[pl.ds(base + b, 1), :] for b in range(per)], 1)
 
             g_re, g_im = row(0), row(1)
-            w_re = weights_ref[sub, :K, at].astype(f32)
-            w_im = weights_ref[sub, K:, at].astype(f32)
-            v_re = (g_re * w_re + g_im * w_im).astype(bf16)
-            v_im = (g_im * w_re - g_re * w_im).astype(bf16)
+            weight = weights_ref[sub, :, at].astype(f32)
+            v_re = (g_re * weight).astype(bf16)
+            v_im = (g_im * weight).astype(bf16)
             return total + nt_dot(one_hot(cells_ref[0, sub : sub + 1, at]), jnp.concatenate([v_re, v_im], 0))
 
         total = lax.fori_loop(0, VISITS // CHUNK, chunk, jnp.zeros((G, 2 * K), f32), unroll=2)
@@ -253,7 +316,7 @@
         out_ref[:, L + turn * PERIOD : L + (turn + 1) * PERIOD] = image[ROWS:]
 
 
-def call(kernel, out_shape, scratch=(), smem=0, count=1):
+def call(kernel, out_shape, scratch=(), smem=0, limit=16, flops=10**9):
     vmem = pl.BlockSpec(memory_space=pltpu.VMEM)
 
     def run(*args):
@@ -264,6 +327,8 @@
             in_specs=specs,
             out_specs=jax.tree.map(lambda _: vmem, out_shape),
             scratch_shapes=list(scratch),
+            cost_estimate=pl.CostEstimate(flops=flops, bytes_accessed=2**20, transcendentals=0),
+            compiler_params=pltpu.CompilerParams(vmem_limit_bytes=limit * 2**20),
         )(*args)
 
     return run
@@ -273,79 +338,59 @@
     return jax.ShapeDtypeStruct(dims, dtype)
 
 
-def turn(phase, period):
-    angle = phase.astype(f32) * (2.0 * math.pi / period)
-    return (jnp.cos(angle), -jnp.sin(angle))
-
-
-def row_phases(offsets, facets):
-    rows = facets[:, None] * ROWS + jnp.tile(jnp.arange(ROWS, dtype=jnp.int32), 2)[None, :]
-    phase = (offsets[:, None, None] * rows[None]) % TOTAL
-    cosine, sine = turn(phase.reshape(-1, 2 * ROWS), TOTAL)
-    return (cosine, sine)
-
-
-def facet_phases(facets):
-    phase = (facets[:, None] * jnp.arange(G, dtype=jnp.int32)[None, :]) % FACETS
-    return turn(phase, FACETS)
-
-
 def body(strips, sub_u, counts, uvw, mueller, observed):
-    column, interp_t, lift_t, lift_s = tables()
+    column, kernel_t, lift_t, lift_s = tables()
     column = jnp.asarray(column, bf16)
-    interp_t = jnp.asarray(interp_t, bf16)
+    kernel_t = jnp.asarray(kernel_t, bf16)
     lift_t = jnp.asarray(lift_t)
     lift_s = jnp.asarray(lift_s)
     here = lax.axis_index("facet")
     plane = lax.axis_index("stokes")
-    core = here % 2
     groups = [[2 * q + side for q in range(32)] for side in range(2)]
     partner = [(i, i ^ 1) for i in range(FACETS)]
-    step = jnp.arange(32, dtype=jnp.int32)
-
-    coeffs = call(column_kernel, shape((K, 2 * ROWS), bf16))(strips[0], column)
-    spread = jnp.broadcast_to(coeffs[None], (32, K, 2 * ROWS))
+
+    def to_stokes(array):
+        return [array] + [
+            lax.ppermute(array, "stokes", [(i, (i - k) % 4) for i in range(4)]) for k in (1, 2, 3)
+        ]
+
+    spread = call(column_kernel, shape((32, K, 2 * ROWS), bf16))(strips[0], column)
     mine = lax.all_to_all(spread, "facet", 0, 0, axis_index_groups=groups, tiled=True)
+    square = shape((128, 128), f32)
+    half = shape((FACETS, G), f32)
+    cos_f, sin_f, cos_a, sin_a, fcos, fsin, vcos, vsin, mix, seen, sent, weights = call(
+        prepare_kernel,
+        (square, square, square, square, half, half, square, square, square)
+        + (
+            shape((4 * MAXB, BLOCK), f32),
+            shape((4 * MAXB, BLOCK), bf16),
+            shape((2, K, VISITS), bf16),
+        ),
+        (pltpu.VMEM((128, 128), jnp.int32), pltpu.VMEM((128, 128), f32)),
+        smem=2,
+        flops=10**10,
+    )(jnp.stack([here, plane]), sub_u, uvw, kernel_t, mueller, observed[0])
+    seen = [seen] + to_stokes(sent)[1:]
+    mine, weights = lax.optimization_barrier((mine, weights))
     other = lax.ppermute(mine, "facet", partner)
-
-    weights = call(weights_kernel, shape((2, 2 * K, VISITS), bf16))(uvw, interp_t)
-    own_facets = 2 * step + core
-    other_facets = 2 * step + 1 - core
-    offsets = lax.dynamic_slice_in_dim(sub_u, 2 * here, 2)
-    other_offsets = lax.dynamic_slice_in_dim(sub_u, 2 * (here + 1 - 2 * core), 2)
-    all_facets = jnp.concatenate([own_facets, other_facets])
-    cos_f, sin_f = row_phases(offsets, all_facets)
-    cos_a, sin_a = row_phases(jnp.concatenate([offsets, other_offsets]), own_facets)
-    fcos, fsin = facet_phases(all_facets)
-    seen = observed.reshape(4 * MAXB, BLOCK)
-    vcos, vsin = turn(uvw[2].reshape(2 * MAXB, BLOCK), G)
-    vsin = -vsin
-    mix = jnp.concatenate([mueller, mueller], 0)
-    mix = jnp.concatenate([mix, mix], 1)
-    mix = lax.dynamic_slice(mix, (plane, plane, 0, 0), (4, 4, 2, MAXB))
-    mix = jnp.transpose(mix.reshape(16, 2 * MAXB))
-
-    sent = call(
+    samples = call(
         model_kernel,
-        shape((8 * MAXB, BLOCK), bf16),
+        shape((4 * MAXB, BLOCK), bf16),
         (
             pltpu.VMEM((4 * K, G), f32),
             pltpu.VMEM((4 * K, G), bf16),
             pltpu.VMEM((4 * MAXB, BLOCK), f32),
         ),
-    )(mine, other, cos_f, sin_f, fcos, fsin, lift_t, lift_s, uvw, weights, seen)
-    planes = [sent] + [
-        lax.ppermute(sent, "stokes", [(i, (i - k) % 4) for i in range(4)]) for k in (1, 2, 3)
-    ]
+    )(mine, other, cos_f, sin_f, fcos, fsin, lift_t, lift_s, uvw, weights)
     resid, adj = call(
         residual_kernel,
         (shape((4 * MAXB, BLOCK), f32), shape((4 * K, G), bf16)),
         (pltpu.VMEM((4 * MAXB, BLOCK), f32),),
         smem=1,
-    )(counts, *planes, seen, mix, vcos, vsin, uvw, weights)
+    )(counts, *to_stokes(samples), *seen, mix, vcos, vsin, uvw, weights)
     other_adj = lax.ppermute(adj, "facet", partner)
     shares = call(share_kernel, shape((32, K, 2 * ROWS), bf16))(
-        adj, other_adj, cos_a, sin_a, fcos[:32], fsin[:32], lift_t, lift_s
+        adj, other_adj, cos_a, sin_a, fcos, fsin, lift_t, lift_s
     )
     shares = lax.all_to_all(shares, "facet", 0, 0, axis_index_groups=groups, tiled=True)
     image = call(image_kernel, shape((ROWS, 2 * L), bf16))(shares, column)

time: 108 us -> 94.3 us (0.87)
  Pallas kernels: 41.2 us -> 28.1 us
  starting transfers between devices: 22.9 us -> 27.9 us
  other arithmetic: 5.06 us -> 0.08 us
  local copies, waits for them, and re-layouts: 9.92 us -> 8.59 us
    pallas_call x6, Pallas kernels: 41.2 us -> 28.1 us  [run(): pl.pallas_call(kernel, out_shape=out_shape, in_specs=specs, out_specs=jax...]
    unnamed x26 -> x46, local copies, waits for them, and re-layouts: 2.94 us -> 7.86 us
    ppermute x3 -> x6, starting transfers between devices: 3.78 us -> 7.25 us  [to_stokes(): lax.ppermute(array, 'stokes', [(i, (i - k) % 4) for i in range(4)])]
    neg x3 -> x0, other arithmetic: 2.97 us -> none  [turn(): return (jnp.cos(angle), -jnp.sin(angle))]
    sin x1 -> x0, other arithmetic: 1.72 us -> none  [turn(): return (jnp.cos(angle), -jnp.sin(angle))]
    broadcast_in_dim x1 -> x0, local copies, waits for them, and re-layouts: 1.63 us -> none  [body(): spread = jnp.broadcast_to(coeffs[None], (32, K, 2 * ROWS))]
    reshape x3 -> x0, local copies, waits for them, and re-layouts: 1.57 us -> none  [the longest x2 0.8 us: body(): mix = jnp.transpose(mix.reshape(16, 2 * MAXB))]
    ppermute x1, starting transfers between devices: 0.49 us -> 1.89 us  [body(): other_adj = lax.ppermute(adj, 'facet', partner)]
  transfers between devices with their start and end apart: 7 -> 10, of which waited for: 6 -> 5; matrix products, arithmetic and copies ran while one was open for 10% -> 1% of each run, Pallas kernels for 6% -> 14%
where the time goes in v2:
time: 94.3 us; the launch traced here: 93.9 us
  waiting for transfers between devices  28.5 us (30%)
  Pallas kernels  28.1 us (30%)
  starting transfers between devices  27.9 us (30%)
  local copies, waits for them, and re-layouts  8.59 us (9%)
    pallas_call x6, Pallas kernels, run(): pl.pallas_call(kernel, out_shape=out_shape, in_specs=specs, out_specs=jax...  28.1 us
    all_to_all x1, waiting for transfers between devices, body(): lax.all_to_all(shares, 'facet', 0, 0, axis_index_groups=groups, tiled=True)  15.9 us
    all_to_all x1, starting transfers between devices, body(): lax.all_to_all(spread, 'facet', 0, 0, axis_index_groups=groups, tiled=True)  11.9 us
    unnamed x46, local copies, waits for them, and re-layouts  7.86 us
    ppermute x6, starting transfers between devices, to_stokes(): lax.ppermute(array, 'stokes', [(i, (i - k) % 4) for i in range(4)])  7.25 us
    all_to_all x1, waiting for transfers between devices, body(): lax.all_to_all(spread, 'facet', 0, 0, axis_index_groups=groups, tiled=True)  6.45 us
    ppermute x6, waiting for transfers between devices, to_stokes(): lax.ppermute(array, 'stokes', [(i, (i - k) % 4) for i in range(4)])  5.15 us
    all_to_all x1, starting transfers between devices, body(): lax.all_to_all(shares, 'facet', 0, 0, axis_index_groups=groups, tiled=True)  4.36 us
  transfers between devices with their start and end apart: 10, of which 5 were waited for; matrix products, arithmetic and copies ran while one was open for 1% of the time, Pallas kernels for 14%

profile of v2, /device:TPU:1, one launch (start us, length us, event | category | flops | bytes accessed | tf_op | source)
XLA Modules:
  0.0 93.9 jit_solution(16546925771832866817)
XLA Ops:
  0.6 0.0 copy-start.3
  0.6 1.6 %copy-done.3 = bf16[1,64,16384]{2,1,0:T(8,128)(2,1)S(1)} copy-done((bf16[1,64,16384]{2,1,0:T(8,128)(2,1)S(1)}, bf16[1,64,16384]{2,1,0:T(8,128)(2,1)}, u32[]{:S(2)}) %copy-start.3) | copy-done | bytes 2097176
  2.2 1.0 %copy-done.8 = bf16[128,2048]{1,0:T(8,128)(2,1)S(1)} copy-done((bf16[128,2048]{1,0:T(8,128)(2,1)S(1)}, bf16[128,2048]{1,0:T(8,128)(2,1)}, u32[]{:S(2)}) %copy-start.8) | copy-done | bytes 524312
  3.3 1.4 %shard_map.113 = bf16[32,64,128]{2,1,0:T(8,128)(2,1)} custom-call(bf16[64,16384]{1,0:T(8,128)(2,1)S(1)} %bitcast.5, bf16[128,2048]{1,0:T(8,128)(2,1)S(1)} %copy-done.8), custom_call_target="tpu_custom_call" | custom-call | flops 1000000000 | bytes 1048576 | tf_op jit(solution)/shard_map/pallas_call | solution.py:324
  4.6 11.9 %all-to-all-start = ((bf16[32,64,128]{2,1,0:T(8,128)(2,1)}), bf16[32,64,128]{2,1,0:T(8,128)(2,1)S(1)}, u32[]{:S(2)}, u32[]{:S(2)}) async-start(bf16[32,64,128]{2,1,0:T(8,128)(2,1)} %shard_map.113), calls=%async_computation | async-start | bytes 1048576 | tf_op jit(solution)/shard_map/all_to_all | solution.py:358
  16.5 0.1 pad_add_fusion.here_ref
  16.6 0.0 copy-done
  16.6 0.0 copy-done.4
  16.6 0.0 copy-done.5
  16.6 0.7 copy-done.6
  17.2 0.8 copy-done.10
  18.0 4.5 %shard_map.114 = (f32[128,128]{1,0:T(8,128)S(1)}, f32[128,128]{1,0:T(8,128)S(1)}, f32[128,128]{1,0:T(8,128)S(1)}, f32[128,128]{1,0:T(8,128)S(1)}, f32[64,256]{1,...) custom-call(s32[2]{0:T(128)S(1)} %pad_add_fusion.here_ref, ...), custom_call_target="tpu_custom_call" | custom-call | flops 10000000000 | bytes 1048576 | tf_op jit(solution)/shard_map/pallas_call | solution.py:324
  22.5 0.0 copy-start.11
  22.6 0.6 copy-done.11
  23.2 0.6 copy-done.13
  23.8 0.6 copy-done.15
  24.4 0.6 copy-done.17
  25.1 0.6 copy-done.19
  25.7 0.6 copy-done.21
  26.3 6.4 %all-to-all-done.mine_ref = bf16[32,64,128]{2,1,0:T(8,128)(2,1)S(1)} async-done(((bf16[32,64,128]{2,1,0:T(8,128)(2,1)}), bf16[32,64,128]{2,1,0:T(8,128)(2,1)S(1)}, u32[]{:S(2)}, u32[]{:S(2)}) %all-to-all-start) | async-done | bytes 524320 | tf_op jit(solution)/shard_map/all_to_all | solution.py:358
  32.8 2.5 %collective-permute-start = (bf16[32,64,128]{2,1,0:T(8,128)(2,1)S(1)}, bf16[32,64,128]{2,1,0:T(8,128)(2,1)S(1)}, u32[]{:S(2)}, u32[]{:S(2)}) collective-permute-start(bf16[32,64,128]{2,1,0:T(8,128)(2,1)S(1)} %all-to-all-done.mine_ref), channel_id=1, source_target_pairs={{0,4},{4,0},{8,12},{12,8},{16,20},{20,16},{24,28},{28,24},{32,36},... | collective-permute-start | bytes 1572872 | tf_op jit(solution)/shard_map/ppermute | solution.py:375
  35.3 2.7 %collective-permute-start.4 = (bf16[256,128]{1,0:T(8,128)(2,1)S(1)}, bf16[256,128]{1,0:T(8,128)(2,1)S(1)}, u32[]{:S(2)}, u32[]{:S(2)}) collective-permute-start(bf16[256,128]{1,0:T(8,128)(2,1)S(1)} %get-tuple-element.26), channel_id=1, source_target_pairs={{0,3},{1,0},{2,1},{3,2},{4,7},{5,4},{6,5},{7,6},{8,11},{9,8},{10,9... | collective-permute-start | bytes 196616 | tf_op jit(solution)/shard_map/ppermute | solution.py:354
  38.0 0.3 collective-permute-start.5
  38.4 0.7 collective-permute-start.6
  39.1 0.0 collective-permute-done.other_ref
  39.1 0.0 copy-done.1
  39.1 0.0 copy-done.2
  39.1 8.8 %shard_map.115.a_ref = bf16[256,128]{1,0:T(8,128)(2,1)S(1)} custom-call(bf16[32,64,128]{2,1,0:T(8,128)(2,1)S(1)} %all-to-all-done.mine_ref, bf16[32,64,128]{2,1,0:T(8,128)(2,1)S(1)} %collective-permute-done.other_ref, f32[128,128]{1,0:T(8,128)S(1)} %get-tuple-element.20.cos_ref, f32[128,128]{1,0:T(8,128)S(1)} %get-tuple-element.21.sin_ref, ...), custom_call_target="tpu_custom_call" | custom-call | flops 1000000000 | bytes 1048576 | tf_op jit(solution)/shard_map/pallas_call | solution.py:324
  47.9 2.1 %collective-permute-start.1 = (bf16[256,128]{1,0:T(8,128)(2,1)S(1)}, bf16[256,128]{1,0:T(8,128)(2,1)S(1)}, u32[]{:S(2)}, u32[]{:S(2)}) collective-permute-start(bf16[256,128]{1,0:T(8,128)(2,1)S(1)} %shard_map.115.a_ref), channel_id=1, source_target_pairs={{0,3},{1,0},{2,1},{3,2},{4,7},{5,4},{6,5},{7,6},{8,11},{9,8},{10,9... | collective-permute-start | bytes 196616 | tf_op jit(solution)/shard_map/ppermute | solution.py:354
  50.0 1.4 %collective-permute-start.2 = (bf16[256,128]{1,0:T(8,128)(2,1)S(1)}, bf16[256,128]{1,0:T(8,128)(2,1)S(1)}, u32[]{:S(2)}, u32[]{:S(2)}) collective-permute-start(bf16[256,128]{1,0:T(8,128)(2,1)S(1)} %shard_map.115.a_ref), channel_id=1, source_target_pairs={{0,2},{1,3},{2,0},{3,1},{4,6},{5,7},{6,4},{7,5},{8,10},{9,11},{10,... | collective-permute-start | bytes 196616 | tf_op jit(solution)/shard_map/ppermute | solution.py:354
  51.4 0.0 collective-permute-done.4.ob_ref
  51.4 0.0 collective-permute-start.3
  51.4 0.0 collective-permute-done.5.oc_ref
  51.4 0.0 collective-permute-done.6.od_ref
  51.4 0.0 collective-permute-done.1.b_ref
  51.4 3.2 %collective-permute-done.2.c_ref = bf16[256,128]{1,0:T(8,128)(2,1)S(1)} collective-permute-done((bf16[256,128]{1,0:T(8,128)(2,1)S(1)}, bf16[256,128]{1,0:T(8,128)(2,1)S(1)}, u32[]{:S(2)}, u32[]{:S(2)}) %collective-permute-start.2) | collective-permute-done | bytes 65568 | tf_op jit(solution)/shard_map/ppermute | solution.py:354
  54.6 2.0 %collective-permute-done.3.d_ref = bf16[256,128]{1,0:T(8,128)(2,1)S(1)} collective-permute-done((bf16[256,128]{1,0:T(8,128)(2,1)S(1)}, bf16[256,128]{1,0:T(8,128)(2,1)S(1)}, u32[]{:S(2)}, u32[]{:S(2)}) %collective-permute-start.3) | collective-permute-done | bytes 65568 | tf_op jit(solution)/shard_map/ppermute | solution.py:354
  56.6 0.0 copy-done.7
  56.6 0.0 copy-done.14
  56.6 6.4 %shard_map.116 = (f32[256,128]{1,0:T(8,128)S(1)}, bf16[256,256]{1,0:T(8,128)(2,1)S(1)}) custom-call(s32[2]{0:T(128)S(1)} %copy-done.7, bf16[256,128]{1,0:T(8,128)(2,1)S(1)} %shard_map.115.a_ref, bf16[256,128]{1,0:T(8,128)(2,1)S(1)} %collective-permute-done.1.b_ref, bf16[256,128]{1,0:T(8,128)(2,1)S(1)} %collective-permute-done.2.c_ref, ...), custom_call_target="tpu_custom_call" | custom-call | flops 1000000000 | bytes 1048576 | tf_op jit(solution)/shard_map/pallas_call | solution.py:324
  63.0 1.9 %collective-permute-start.7 = (bf16[256,256]{1,0:T(8,128)(2,1)S(1)}, bf16[256,256]{1,0:T(8,128)(2,1)S(1)}, u32[]{:S(2)}, u32[]{:S(2)}) collective-permute-start(bf16[256,256]{1,0:T(8,128)(2,1)S(1)} %get-tuple-element.30.mine_ref), channel_id=1, source_target_pairs={{0,4},{4,0},{8,12},{12,8},{16,20},{20,16},{24,28},{28,24},{32,36},... | collective-permute-start | bytes 393224 | tf_op jit(solution)/shard_map/ppermute | solution.py:391
  64.9 1.0 %collective-permute-done.7.other_ref = bf16[256,256]{1,0:T(8,128)(2,1)S(1)} collective-permute-done((bf16[256,256]{1,0:T(8,128)(2,1)S(1)}, bf16[256,256]{1,0:T(8,128)(2,1)S(1)}, u32[]{:S(2)}, u32[]{:S(2)}) %collective-permute-start.7) | collective-permute-done | bytes 131104 | tf_op jit(solution)/shard_map/ppermute | solution.py:391
  65.9 5.2 %shard_map.117 = bf16[32,64,128]{2,1,0:T(8,128)(2,1)} custom-call(bf16[256,256]{1,0:T(8,128)(2,1)S(1)} %get-tuple-element.30.mine_ref, bf16[256,256]{1,0:T(8,128)(2,1)S(1)} %collective-permute-done.7.other_ref, f32[128,128]{1,0:T(8,128)S(1)} %copy-done.20, f32[128,128]{1,0:T(8,128)S(1)} %copy-done.22, f32[64,256]{1,0:T(8,128)S(1)} %get-tuple-element.22.fcos_ref, ...), custom_call_target="tpu_custom_call" | custom-call | flops 1000000000 | bytes 1048576 | tf_op jit(solution)/shard_map/pallas_call | solution.py:324
  71.1 4.4 %all-to-all-start.1 = ((bf16[32,64,128]{2,1,0:T(8,128)(2,1)}), bf16[32,64,128]{2,1,0:T(8,128)(2,1)S(1)}, u32[]{:S(2)}, u32[]{:S(2)}) async-start(bf16[32,64,128]{2,1,0:T(8,128)(2,1)} %shard_map.117), calls=%async_computation.1 | async-start | bytes 1048576 | tf_op jit(solution)/shard_map/all_to_all | solution.py:395
  75.5 0.7 reshape.7
  76.2 15.9 %all-to-all-done.1.shares_ref = bf16[32,64,128]{2,1,0:T(8,128)(2,1)S(1)} async-done(((bf16[32,64,128]{2,1,0:T(8,128)(2,1)}), bf16[32,64,128]{2,1,0:T(8,128)(2,1)S(1)}, u32[]{:S(2)}, u32[]{:S(2)}) %all-to-all-start.1) | async-done | bytes 524320 | tf_op jit(solution)/shard_map/all_to_all | solution.py:395
  92.1 0.0 copy-done.9
  92.1 1.8 %shard_map.118 = bf16[64,16384]{1,0:T(8,128)(2,1)} custom-call(bf16[32,64,128]{2,1,0:T(8,128)(2,1)S(1)} %all-to-all-done.1.shares_ref, bf16[128,2048]{1,0:T(8,128)(2,1)S(1)} %copy-done.9), custom_call_target="tpu_custom_call" | custom-call | flops 1000000000 | bytes 1048576 | tf_op jit(solution)/shard_map/pallas_call | solution.py:324
  (26 shorter events, 0.0 us)
Async XLA Ops:
  0.6 1.6 %copy-start.3 = (bf16[1,64,16384]{2,1,0:T(8,128)(2,1)S(1)}, bf16[1,64,16384]{2,1,0:T(8,128)(2,1)}, u32[]{:S(2)}) copy-start(bf16[1,64,16384]{2,1,0:T(8,128)(2,1)} %param.10) | copy-start | bytes 6291460
  2.2 1.0 %copy-start.8 = (bf16[128,2048]{1,0:T(8,128)(2,1)S(1)}, bf16[128,2048]{1,0:T(8,128)(2,1)}, u32[]{:S(2)}) copy-start(bf16[128,2048]{1,0:T(8,128)(2,1)} %constant.17.clone.column_ref) | copy-start | bytes 1572868
  3.3 13.3 %copy-start = (s32[3,2,8192]{2,1,0:T(2,128)S(1)}, s32[3,2,8192]{2,1,0:T(2,128)}, u32[]{:S(2)}) copy-start(s32[3,2,8192]{2,1,0:T(2,128)} %cells_ref.5) | copy-start | bytes 589828
  3.3 13.3 %copy-start.4 = (f32[1,2,2,8192]{3,2,1,0:T(2,128)S(1)}, f32[1,2,2,8192]{3,2,1,0:T(2,128)}, u32[]{:S(2)}) copy-start(f32[1,2,2,8192]{3,2,1,0:T(2,128)} %param.15) | copy-start | bytes 393220
  3.3 13.3 %copy-start.5 = (f32[4,4,2,64]{3,2,1,0:T(2,128)S(1)}, f32[4,4,2,64]{3,2,1,0:T(2,128)}, u32[]{:S(2)}) copy-start(f32[4,4,2,64]{3,2,1,0:T(2,128)} %mueller_ref.1) | copy-start | bytes 24580
  4.6 28.1 %all-to-all-start = ((bf16[32,64,128]{2,1,0:T(8,128)(2,1)}), bf16[32,64,128]{2,1,0:T(8,128)(2,1)S(1)}, u32[]{:S(2)}, u32[]{:S(2)}) async-start(bf16[32,64,128]{2,1,0:T(8,128)(2,1)} %shard_map.113), calls=%async_computation | async-start | bytes 1048576 | tf_op jit(solution)/shard_map/all_to_all | solution.py:358
  16.6 0.7 copy-start.6
  17.2 0.8 copy-start.10
  18.0 21.1 %copy-start.1 = (f32[128,256]{1,0:T(8,128)S(1)}, f32[128,256]{1,0:T(8,128)}, u32[]{:S(2)}) copy-start(f32[128,256]{1,0:T(8,128)} %constant.19.clone.lift_ref) | copy-start | bytes 393220
  18.0 21.1 %copy-start.2 = (f32[128,256]{1,0:T(8,128)S(1)}, f32[128,256]{1,0:T(8,128)}, u32[]{:S(2)}) copy-start(f32[128,256]{1,0:T(8,128)} %constant.20.clone.lift_s_ref) | copy-start | bytes 393220
  22.5 0.7 copy-start.11
  23.2 0.6 copy-start.13
  23.8 0.6 copy-start.15
  24.4 0.6 copy-start.17
  25.1 0.6 copy-start.19
  25.7 0.6 copy-start.21
  26.3 30.2 %copy-start.7 = (s32[2]{0:T(128)S(1)}, s32[2]{0:T(128)}, u32[]{:S(2)}) copy-start(s32[2]{0:T(128)} %counts_ref.1) | copy-start | bytes 28
  32.8 23.8 %copy-start.12 = (f32[256,128]{1,0:T(8,128)S(1)}, f32[256,128]{1,0:T(8,128)}, u32[]{:S(2)}) copy-start(f32[256,128]{1,0:T(8,128)} %copy-done.11) | copy-start | bytes 393220
  32.8 23.8 %copy-start.14 = (f32[128,128]{1,0:T(8,128)S(1)}, f32[128,128]{1,0:T(8,128)}, u32[]{:S(2)}) copy-start(f32[128,128]{1,0:T(8,128)} %copy-done.13) | copy-start | bytes 196612
  32.8 23.8 %copy-start.16 = (f32[128,128]{1,0:T(8,128)S(1)}, f32[128,128]{1,0:T(8,128)}, u32[]{:S(2)}) copy-start(f32[128,128]{1,0:T(8,128)} %copy-done.15) | copy-start | bytes 196612
  32.8 23.8 %copy-start.18 = (f32[128,128]{1,0:T(8,128)S(1)}, f32[128,128]{1,0:T(8,128)}, u32[]{:S(2)}) copy-start(f32[128,128]{1,0:T(8,128)} %copy-done.17) | copy-start | bytes 196612
  32.8 6.3 %collective-permute-start = (bf16[32,64,128]{2,1,0:T(8,128)(2,1)S(1)}, bf16[32,64,128]{2,1,0:T(8,128)(2,1)S(1)}, u32[]{:S(2)}, u32[]{:S(2)}) collective-permute-start(bf16[32,64,128]{2,1,0:T(8,128)(2,1)S(1)} %all-to-all-done.mine_ref), channel_id=1, source_target_pairs={{0,4},{4,0},{8,12},{12,8},{16,20},{20,16},{24,28},{28,24},{32,36},... | collective-permute-start | bytes 1572872 | tf_op jit(solution)/shard_map/ppermute | solution.py:375
  35.3 16.1 %collective-permute-start.4 = (bf16[256,128]{1,0:T(8,128)(2,1)S(1)}, bf16[256,128]{1,0:T(8,128)(2,1)S(1)}, u32[]{:S(2)}, u32[]{:S(2)}) collective-permute-start(bf16[256,128]{1,0:T(8,128)(2,1)S(1)} %get-tuple-element.26), channel_id=1, source_target_pairs={{0,3},{1,0},{2,1},{3,2},{4,7},{5,4},{6,5},{7,6},{8,11},{9,8},{10,9... | collective-permute-start | bytes 196616 | tf_op jit(solution)/shard_map/ppermute | solution.py:354
  38.0 13.4 %collective-permute-start.5 = (bf16[256,128]{1,0:T(8,128)(2,1)S(1)}, bf16[256,128]{1,0:T(8,128)(2,1)S(1)}, u32[]{:S(2)}, u32[]{:S(2)}) collective-permute-start(bf16[256,128]{1,0:T(8,128)(2,1)S(1)} %get-tuple-element.26), channel_id=1, source_target_pairs={{0,2},{1,3},{2,0},{3,1},{4,6},{5,7},{6,4},{7,5},{8,10},{9,11},{10,... | collective-permute-start | bytes 196616 | tf_op jit(solution)/shard_map/ppermute | solution.py:354
  38.4 13.0 %collective-permute-start.6 = (bf16[256,128]{1,0:T(8,128)(2,1)S(1)}, bf16[256,128]{1,0:T(8,128)(2,1)S(1)}, u32[]{:S(2)}, u32[]{:S(2)}) collective-permute-start(bf16[256,128]{1,0:T(8,128)(2,1)S(1)} %get-tuple-element.26), channel_id=1, source_target_pairs={{0,1},{1,2},{2,3},{3,0},{4,5},{5,6},{6,7},{7,4},{8,9},{9,10},{10,1... | collective-permute-start | bytes 196616 | tf_op jit(solution)/shard_map/ppermute | solution.py:354
  47.9 18.0 %copy-start.20 = (f32[128,128]{1,0:T(8,128)S(1)}, f32[128,128]{1,0:T(8,128)}, u32[]{:S(2)}) copy-start(f32[128,128]{1,0:T(8,128)} %copy-done.19) | copy-start | bytes 196612
  47.9 18.0 %copy-start.22 = (f32[128,128]{1,0:T(8,128)S(1)}, f32[128,128]{1,0:T(8,128)}, u32[]{:S(2)}) copy-start(f32[128,128]{1,0:T(8,128)} %copy-done.21) | copy-start | bytes 196612
  47.9 3.5 %collective-permute-start.1 = (bf16[256,128]{1,0:T(8,128)(2,1)S(1)}, bf16[256,128]{1,0:T(8,128)(2,1)S(1)}, u32[]{:S(2)}, u32[]{:S(2)}) collective-permute-start(bf16[256,128]{1,0:T(8,128)(2,1)S(1)} %shard_map.115.a_ref), channel_id=1, source_target_pairs={{0,3},{1,0},{2,1},{3,2},{4,7},{5,4},{6,5},{7,6},{8,11},{9,8},{10,9... | collective-permute-start | bytes 196616 | tf_op jit(solution)/shard_map/ppermute | solution.py:354
  50.0 4.6 %collective-permute-start.2 = (bf16[256,128]{1,0:T(8,128)(2,1)S(1)}, bf16[256,128]{1,0:T(8,128)(2,1)S(1)}, u32[]{:S(2)}, u32[]{:S(2)}) collective-permute-start(bf16[256,128]{1,0:T(8,128)(2,1)S(1)} %shard_map.115.a_ref), channel_id=1, source_target_pairs={{0,2},{1,3},{2,0},{3,1},{4,6},{5,7},{6,4},{7,5},{8,10},{9,11},{10,... | collective-permute-start | bytes 196616 | tf_op jit(solution)/shard_map/ppermute | solution.py:354
  51.4 5.2 %collective-permute-start.3 = (bf16[256,128]{1,0:T(8,128)(2,1)S(1)}, bf16[256,128]{1,0:T(8,128)(2,1)S(1)}, u32[]{:S(2)}, u32[]{:S(2)}) collective-permute-start(bf16[256,128]{1,0:T(8,128)(2,1)S(1)} %shard_map.115.a_ref), channel_id=1, source_target_pairs={{0,1},{1,2},{2,3},{3,0},{4,5},{5,6},{6,7},{7,4},{8,9},{9,10},{10,1... | collective-permute-start | bytes 196616 | tf_op jit(solution)/shard_map/ppermute | solution.py:354
  63.0 2.9 %collective-permute-start.7 = (bf16[256,256]{1,0:T(8,128)(2,1)S(1)}, bf16[256,256]{1,0:T(8,128)(2,1)S(1)}, u32[]{:S(2)}, u32[]{:S(2)}) collective-permute-start(bf16[256,256]{1,0:T(8,128)(2,1)S(1)} %get-tuple-element.30.mine_ref), channel_id=1, source_target_pairs={{0,4},{4,0},{8,12},{12,8},{16,20},{20,16},{24,28},{28,24},{32,36},... | collective-permute-start | bytes 393224 | tf_op jit(solution)/shard_map/ppermute | solution.py:391
  65.9 26.2 %copy-start.9 = (bf16[128,2048]{1,0:T(8,128)(2,1)S(1)}, bf16[128,2048]{1,0:T(8,128)(2,1)}, u32[]{:S(2)}) copy-start(bf16[128,2048]{1,0:T(8,128)(2,1)} %constant.17.clone.column_ref) | copy-start | bytes 1572868
  71.1 21.0 %all-to-all-start.1 = ((bf16[32,64,128]{2,1,0:T(8,128)(2,1)}), bf16[32,64,128]{2,1,0:T(8,128)(2,1)S(1)}, u32[]{:S(2)}, u32[]{:S(2)}) async-start(bf16[32,64,128]{2,1,0:T(8,128)(2,1)} %shard_map.117), calls=%async_computation.1 | async-start | bytes 1048576 | tf_op jit(solution)/shard_map/all_to_all | solution.py:395

commit v3 on v2

v3 whole, which is shorter than its diff:
```python
import functools
import math

import jax
import jax.numpy as jnp
import numpy as np
from jax import lax
from jax.experimental import pallas as pl
from jax.experimental.pallas import tpu as pltpu
from jax.sharding import PartitionSpec as P


K = 64
G = 256
L = 8192
PERIOD = 2048
ROWS = 64
FACETS = 64
TOTAL = 4096
MAXB = 64
BLOCK = 128
VISITS = 8192
CHUNK = 512
GROUP = 4

f32 = jnp.float32
bf16 = jnp.bfloat16


@functools.cache
def tables():
    lpos = np.arange(PERIOD)[None, :]
    cpos = np.arange(K)[:, None]
    angle = 2.0 * np.pi * ((4 * cpos * (lpos - 16)) % L) / L
    column = np.concatenate([np.cos(angle), -np.sin(angle)], 0) / math.sqrt(L)
    upos = np.arange(G)[:, None]
    kpos = np.arange(K)[None, :]
    mpos = np.arange(K) - K // 2
    phase = (mpos[None, None, :] * (upos - 4 * kpos)[:, :, None]) % G
    interp = np.exp(2j * np.pi * phase / G).sum(2) / (2.0 * K)
    kernel_t = (interp * np.exp(2j * np.pi * (upos - 4 * kpos) / 512)).real.T
    dpos = np.arange(ROWS) - ROWS // 2
    lift = interp @ np.exp(-2j * np.pi * np.arange(K)[:, None] * dpos[None, :] / 1024)
    lift = lift * np.exp(-2j * np.pi * upos / 128) / math.sqrt(TOTAL)
    lift_t = np.concatenate([lift.real.T, lift.imag.T], 0)
    lift_s = np.concatenate([-lift.imag.T, lift.real.T], 0)
    return (
        column.astype(np.float32),
        kernel_t.astype(np.float32),
        lift_t.astype(np.float32),
        lift_s.astype(np.float32),
    )


def half_sign():
    lane = lax.broadcasted_iota(jnp.int32, (1, 2 * K), 1)
    return jnp.where(lane < K, 1.0, -1.0).astype(f32)


def swap(x):
    return pltpu.roll(x, K, 1)


def one_hot(cells):
    grid_pos = lax.broadcasted_iota(jnp.int32, (G, cells.shape[1]), 0)
    return jnp.where(grid_pos == cells, 1.0, 0.0).astype(bf16)


def nt_dot(a, b):
    return lax.dot_general(a, b, (((1,), (1,)), ((), ())), preferred_element_type=f32)


def column_kernel(strips_ref, column_ref, out_ref, strips_buf, column_buf, sems):
    copies = [
        pltpu.make_async_copy(
            strips_ref.at[:, pl.ds(i * PERIOD, PERIOD)], strips_buf.at[i], sems.at[i]
        )
        for i in range(8)
    ]
    table = pltpu.make_async_copy(column_ref, column_buf, sems.at[8])
    for copy in copies:
        copy.start()
    table.start()
    parts = []
    for part in range(2):
        copies[4 * part].wait()
        copies[4 * part + 1].wait()
        folded = strips_buf[4 * part].astype(f32) + strips_buf[4 * part + 1].astype(f32)
        copies[4 * part + 2].wait()
        copies[4 * part + 3].wait()
        folded = folded + strips_buf[4 * part + 2].astype(f32) + strips_buf[4 * part + 3].astype(f32)
        parts.append(folded.astype(bf16))
    table.wait()
    product = nt_dot(column_buf[...], jnp.concatenate(parts, 0))
    coeffs = (product[:K] - half_sign() * swap(product[K:])).astype(bf16)
    for q in range(32):
        out_ref[q] = coeffs


def turn(n, period):
    t = n.astype(f32) * (4.0 / period)
    q = jnp.floor(t + 0.5)
    x = (t - q) * (math.pi / 2)
    quarter = q.astype(jnp.int32) & 3
    y = x * x
    s = x * (1.0 + y * (-1.0 / 6 + y * (1.0 / 120 + y * (-1.0 / 5040 + y * (1.0 / 362880)))))
    c = 1.0 + y * (-0.5 + y * (1.0 / 24 + y * (-1.0 / 720 + y * (1.0 / 40320))))
    odd = (quarter & 1) == 1
    cosine = jnp.where(odd, s, c)
    sine = jnp.where(odd, c, s)
    cosine = jnp.where((quarter == 1) | (quarter == 2), -cosine, cosine)
    sine = jnp.where(quarter >= 2, sine, -sine)
    return cosine, sine


def prepare_kernel(
    here_ref, cells_ref, kernel_ref, mueller_ref, observed_ref, vcos_ref, vsin_ref, mix_ref, seen_ref,
    sent_ref, weights_ref, steps_ref, rows_ref,
):
    plane = here_ref[1]
    for sub in range(2):
        for b in range(MAXB):
            lanes = slice(b * BLOCK, (b + 1) * BLOCK)
            steps_ref[sub * MAXB + b : sub * MAXB + b + 1, :] = (
                2 * cells_ref[2, sub : sub + 1, lanes] + cells_ref[1, sub : sub + 1, lanes]
            )
            for part in range(2):
                at = (2 * sub + part) * MAXB + b
                seen_ref[at : at + 1, :] = observed_ref[sub, part : part + 1, lanes]
    sent_ref[...] = seen_ref[...].astype(bf16)
    cosine, sine = turn(steps_ref[...] & (2 * G - 1), 2 * G)
    vcos_ref[...] = cosine
    vsin_ref[...] = -sine
    rows_ref[...] = jnp.zeros_like(rows_ref)
    for corr in range(4):
        for t in range(4):
            entry = mueller_ref[(plane + corr) & 3, (plane + t) & 3]
            at = 4 * corr + t
            rows_ref[at : at + 1, :] = jnp.concatenate([entry[0:1, :], entry[1:2, :]], 1)
    for t in range(4):
        rows_ref[16 + t : 17 + t, :] = sum(
            rows_ref[4 * corr : 4 * corr + 1, :] * rows_ref[4 * corr + t : 4 * corr + t + 1, :]
            for corr in range(4)
        )
    mix_ref[...] = jnp.transpose(rows_ref[...])
    for sub in range(2):

        def chunk(n, carry):
            at = pl.ds(pl.multiple_of(n * CHUNK, CHUNK), CHUNK)
            picked = jnp.dot(
                kernel_ref[...], one_hot(cells_ref[1, sub : sub + 1, at]), preferred_element_type=f32
            )
            weights_ref[sub, :, at] = picked.astype(bf16)
            return carry

        lax.fori_loop(0, VISITS // CHUNK, chunk, 0, unroll=2)


def phases(offsets, parity, cos_ref, sin_ref, fcos_ref, fsin_ref):
    step = lax.broadcasted_iota(jnp.int32, (32, 2 * ROWS), 0)
    lane = lax.broadcasted_iota(jnp.int32, (32, 2 * ROWS), 1) & (ROWS - 1)
    rows = (2 * step + parity) * ROWS + lane
    for i, offset in enumerate(offsets):
        cosine, sine = turn((rows * offset) & (TOTAL - 1), TOTAL)
        cos_ref[32 * i : 32 * i + 32, :] = cosine
        sin_ref[32 * i : 32 * i + 32, :] = sine
    step = lax.broadcasted_iota(jnp.int32, (32, G), 0)
    lane = lax.broadcasted_iota(jnp.int32, (32, G), 1)
    cosine, sine = turn(((2 * step + parity) * lane) & (FACETS - 1), FACETS)
    fcos_ref[...] = cosine
    fsin_ref[...] = sine


def facet_lift(cos_row, sin_row, lift_ref, lift_s_ref):
    return (cos_row * lift_ref[...] + sin_row * lift_s_ref[...]).astype(bf16)


def lift(here_ref, sub_ref, side, source, lift_ref, lift_s_ref, total_ref, tables):
    cos_ref, sin_ref, fcos_ref, fsin_ref = tables
    here = here_ref[0]
    core = here & 1
    offsets = [sub_ref[2 * here + sub] for sub in range(2)]
    phases(offsets, core if side == 0 else 1 - core, *tables)
    sign = half_sign()

    def group(i, carry):
        lefts, rights = [], []
        for e in range(GROUP):
            q = GROUP * i + e
            first = source[q].astype(f32)
            second = swap(first)
            rights.append(
                facet_lift(fcos_ref[pl.ds(q, 1), :], fsin_ref[pl.ds(q, 1), :], lift_ref, lift_s_ref)
            )
            blocks = []
            for sub in range(2):
                pr = cos_ref[pl.ds(sub * 32 + q, 1), :]
                pi = sin_ref[pl.ds(sub * 32 + q, 1), :]
                blocks.append((first * (pr * sign) - second * pi).astype(bf16))
                blocks.append((second * pr + first * (pi * sign)).astype(bf16))
            lefts.append(jnp.concatenate(blocks, 0))
        left = jnp.concatenate(lefts, 1)
        right = jnp.concatenate(rights, 0)
        total_ref[...] += jnp.dot(left, right, preferred_element_type=f32)
        return carry

    lax.fori_loop(0, 32 // GROUP, group, 0)


def lift_kernel(here_ref, sub_ref, mine_ref, lift_ref, lift_s_ref, rows_ref, *tables):
    rows_ref[...] = jnp.zeros_like(rows_ref)
    lift(here_ref, sub_ref, 0, mine_ref, lift_ref, lift_s_ref, rows_ref, tables)


def model_kernel(
    here_ref, sub_ref, start_ref, other_ref, lift_ref, lift_s_ref, cells_ref, weights_ref,
    out_ref, rows_ref, lifted_ref, samples_ref, *tables
):
    rows_ref[...] = start_ref[...]
    lift(here_ref, sub_ref, 1, other_ref, lift_ref, lift_s_ref, rows_ref, tables)
    lifted_ref[...] = rows_ref[...].astype(bf16)
    per = CHUNK // BLOCK
    for sub in range(2):

        def chunk(n, carry):
            at = pl.ds(pl.multiple_of(n * CHUNK, CHUNK), CHUNK)
            picked = jnp.dot(
                lifted_ref[sub * 2 * K : (sub + 1) * 2 * K, :],
                one_hot(cells_ref[0, sub : sub + 1, at]),
                preferred_element_type=f32,
            )
            weight = weights_ref[sub, :, at].astype(f32)
            m_re = jnp.sum(picked[:K] * weight, 0, keepdims=True)
            m_im = jnp.sum(picked[K:] * weight, 0, keepdims=True)
            for b in range(per):
                lanes = slice(b * BLOCK, (b + 1) * BLOCK)
                samples_ref[pl.ds(2 * sub * MAXB + n * per + b, 1), :] = m_re[:, lanes]
                samples_ref[pl.ds((2 * sub + 1) * MAXB + n * per + b, 1), :] = m_im[:, lanes]
            return carry

        lax.fori_loop(0, VISITS // CHUNK, chunk, 0, unroll=2)
    out_ref[...] = samples_ref[...].astype(bf16)


def parts_of(sub):
    return (
        slice(sub * MAXB, (sub + 1) * MAXB),
        slice(2 * sub * MAXB, (2 * sub + 1) * MAXB),
        slice((2 * sub + 1) * MAXB, (2 * sub + 2) * MAXB),
    )


def observed_kernel(a_ref, b_ref, c_ref, d_ref, mix_ref, cos_ref, sin_ref, out_ref):
    for sub in range(2):
        here, re, im = parts_of(sub)
        cosine, sine = cos_ref[here, :], sin_ref[here, :]
        back_re = jnp.zeros((MAXB, BLOCK), f32)
        back_im = jnp.zeros((MAXB, BLOCK), f32)
        for corr, seen in enumerate((a_ref, b_ref, c_ref, d_ref)):
            mix = mix_ref[here, 4 * corr : 4 * corr + 1]
            back_re = back_re + mix * seen[re, :].astype(f32)
            back_im = back_im + mix * seen[im, :].astype(f32)
        out_ref[re, :] = back_re * cosine - back_im * sine
        out_ref[im, :] = back_im * cosine + back_re * sine


def residual_kernel(
    counts_ref, a_ref, b_ref, c_ref, d_ref, seen_ref, turned_ref, mix_ref, cos_ref, sin_ref, cells_ref,
    weights_ref, resid_ref, out_ref, back_ref,
):
    planes = (a_ref, b_ref, c_ref, d_ref)
    block = lax.broadcasted_iota(jnp.int32, (MAXB, BLOCK), 0)
    for sub in range(2):
        live = block < counts_ref[sub]
        here, re, im = parts_of(sub)
        cosine, sine = cos_ref[here, :], sin_ref[here, :]
        s_re = [p[re, :].astype(f32) for p in planes]
        s_im = [p[im, :].astype(f32) for p in planes]

        def mixed(first, samples):
            return sum(mix_ref[here, first + t : first + t + 1] * s for t, s in enumerate(samples))

        m_re, m_im = mixed(0, s_re), mixed(0, s_im)
        resid_ref[re, :] = jnp.where(live, seen_ref[re, :] - (m_re * cosine + m_im * sine), 0.0)
        resid_ref[im, :] = jnp.where(live, seen_ref[im, :] - (m_im * cosine - m_re * sine), 0.0)
        back_ref[re, :] = jnp.where(live, turned_ref[re, :] - mixed(16, s_re), 0.0)
        back_ref[im, :] = jnp.where(live, turned_ref[im, :] - mixed(16, s_im), 0.0)
    per = CHUNK // BLOCK
    for sub in range(2):

        def chunk(n, total):
            at = pl.ds(pl.multiple_of(n * CHUNK, CHUNK), CHUNK)

            def row(part):
                base = (2 * sub + part) * MAXB + n * per
                return jnp.concatenate([back_ref[pl.ds(base + b, 1), :] for b in range(per)], 1)

            g_re, g_im = row(0), row(1)
            weight = weights_ref[sub, :, at].astype(f32)
            v_re = (g_re * weight).astype(bf16)
            v_im = (g_im * weight).astype(bf16)
            return total + nt_dot(one_hot(cells_ref[0, sub : sub + 1, at]), jnp.concatenate([v_re, v_im], 0))

        total = lax.fori_loop(0, VISITS // CHUNK, chunk, jnp.zeros((G, 2 * K), f32), unroll=2)
        out_ref[sub * 2 * K : (sub + 1) * 2 * K, :] = jnp.transpose(total).astype(bf16)


def share_kernel(
    here_ref, sub_ref, mine_ref, other_ref, lift_ref, lift_s_ref, out_ref, *tables
):
    cos_ref, sin_ref, fcos_ref, fsin_ref = tables
    sign = half_sign()
    here = here_ref[0]
    core = here & 1
    firsts = (2 * here, 2 * (here + 1 - 2 * core))
    phases([sub_ref[first + sub] for first in firsts for sub in range(2)], core, *tables)
    left = jnp.concatenate([mine_ref[...], other_ref[...]], 0)

    def pair(i, carry):
        rights = []
        for e in range(2):
            q = 2 * i + e
            rights.append(
                facet_lift(fcos_ref[pl.ds(q, 1), :], fsin_ref[pl.ds(q, 1), :], lift_ref, lift_s_ref)
            )
        product = nt_dot(left, jnp.concatenate(rights, 0))
        for e in range(2):
            q = 2 * i + e
            total = jnp.zeros((K, 2 * ROWS), f32)
            swapped = jnp.zeros((K, 2 * ROWS), f32)
            for sub in range(4):
                g_re = product[sub * 2 * K : sub * 2 * K + K, e * 128 : (e + 1) * 128]
                g_im = product[sub * 2 * K + K : (sub + 1) * 2 * K, e * 128 : (e + 1) * 128]
                pr = cos_ref[pl.ds(sub * 32 + q, 1), :]
                pi = sin_ref[pl.ds(sub * 32 + q, 1), :]
                total = total + (g_re * pr + g_im * pi)
                swapped = swapped + (g_im * pr - g_re * pi)
            out_ref[q] = (total * sign + swap(swapped)).astype(bf16)
        return carry

    lax.fori_loop(0, 16, pair, 0, unroll=2)


def image_kernel(shares_ref, column_ref, out_ref):
    total = shares_ref[0].astype(f32)
    for q in range(1, 32):
        total = total + shares_ref[q].astype(f32)
    total = total.astype(bf16).astype(f32)
    both = jnp.concatenate([total, half_sign() * swap(total)], 0)
    left = jnp.transpose(both).astype(bf16)
    image = (8.0 * jnp.dot(left, column_ref[...], preferred_element_type=f32)).astype(bf16)
    for turn in range(4):
        out_ref[:, turn * PERIOD : (turn + 1) * PERIOD] = image[:ROWS]
        out_ref[:, L + turn * PERIOD : L + (turn + 1) * PERIOD] = image[ROWS:]


def call(kernel, out_shape, scratch=(), smem=0, limit=16, flops=10**9, hbm=False):
    vmem = pl.BlockSpec(memory_space=pltpu.VMEM)

    def run(*args):
        place = pl.BlockSpec(memory_space=pltpu.HBM) if hbm else vmem
        specs = [pl.BlockSpec(memory_space=pltpu.SMEM)] * smem + [place] * (len(args) - smem)
        return pl.pallas_call(
            kernel,
            out_shape=out_shape,
            in_specs=specs,
            out_specs=jax.tree.map(lambda _: vmem, out_shape),
            scratch_shapes=list(scratch),
            cost_estimate=pl.CostEstimate(flops=flops, bytes_accessed=2**20, transcendentals=0),
            compiler_params=pltpu.CompilerParams(vmem_limit_bytes=limit * 2**20),
        )(*args)

    return run


def shape(dims, dtype):
    return jax.ShapeDtypeStruct(dims, dtype)


def column_of_subgrids(strips, sub_u, counts, uvw, mueller, observed):
    column, kernel_t, lift_t, lift_s = tables()
    column = jnp.asarray(column, bf16)
    kernel_t = jnp.asarray(kernel_t, bf16)
    lift_t = jnp.asarray(lift_t)
    lift_s = jnp.asarray(lift_s)
    here = lax.axis_index("facet")
    plane = lax.axis_index("stokes")
    groups = [[2 * q + side for q in range(32)] for side in range(2)]
    partner = [(i, i ^ 1) for i in range(FACETS)]

    def to_stokes(array):
        out = [array]
        for k in (1, 2, 3):
            out.append(lax.ppermute(array, "stokes", [(i, (i - k) % 4) for i in range(4)]))
        return out

    spread = call(
        column_kernel,
        shape((32, K, 2 * ROWS), bf16),
        (
            pltpu.VMEM((8, ROWS, PERIOD), bf16),
            pltpu.VMEM((2 * K, PERIOD), bf16),
            pltpu.SemaphoreType.DMA((9,)),
        ),
        limit=60,
        hbm=True,
    )(strips[0], column)
    mine = lax.all_to_all(spread, "facet", 0, 0, axis_index_groups=groups, tiled=True)
    square = shape((128, 128), f32)
    position = jnp.stack([here, plane])
    vcos, vsin, mix, seen, sent, weights = call(
        prepare_kernel,
        (
            square,
            square,
            square,
            shape((4 * MAXB, BLOCK), f32),
            shape((4 * MAXB, BLOCK), bf16),
            shape((2, K, VISITS), bf16),
        ),
        (pltpu.VMEM((128, 128), jnp.int32), pltpu.VMEM((128, 128), f32)),
        smem=1,
        flops=10**10,
    )(position, uvw, kernel_t, mueller, observed[0])
    turned = call(observed_kernel, shape((4 * MAXB, BLOCK), f32))(
        seen, *to_stokes(sent)[1:], mix, vcos, vsin
    )
    other = lax.ppermute(mine, "facet", partner)

    def scratch(offsets):
        return tuple(
            pltpu.VMEM(dims, f32) for dims in ((32 * offsets, 128), (32 * offsets, 128), (32, G), (32, G))
        )

    rows = call(lift_kernel, shape((4 * K, G), f32), scratch(2), smem=2)(
        position, sub_u, mine, lift_t, lift_s
    )
    samples = call(
        model_kernel,
        shape((4 * MAXB, BLOCK), bf16),
        (
            pltpu.VMEM((4 * K, G), f32),
            pltpu.VMEM((4 * K, G), bf16),
            pltpu.VMEM((4 * MAXB, BLOCK), f32),
        )
        + scratch(2),
        smem=2,
    )(position, sub_u, rows, other, lift_t, lift_s, uvw, weights)
    resid, adj = call(
        residual_kernel,
        (shape((4 * MAXB, BLOCK), f32), shape((4 * K, G), bf16)),
        (pltpu.VMEM((4 * MAXB, BLOCK), f32),),
        smem=1,
    )(counts, *to_stokes(samples), seen, turned, mix, vcos, vsin, uvw, weights)
    other_adj = lax.ppermute(adj, "facet", partner)
    shares = call(share_kernel, shape((32, K, 2 * ROWS), bf16), scratch(4), smem=2)(
        position, sub_u, adj, other_adj, lift_t, lift_s
    )
    shares = lax.all_to_all(shares, "facet", 0, 0, axis_index_groups=groups, tiled=True)
    image = call(image_kernel, shape((ROWS, 2 * L), bf16))(shares, column)
    return (image[None], resid.reshape(1, 2, 2, VISITS))


def solution(mesh):
    placed = (
        P("stokes", "facet", None),
        P(),
        P("facet"),
        P(None, "facet", None),
        P(None, None, "facet", None),
        P("stokes", "facet", None, None),
    )
    return jax.shard_map(
        column_of_subgrids,
        mesh=mesh,
        in_specs=placed,
        out_specs=(P("stokes", "facet", None), P("stokes", "facet", None, None)),
        check_vma=False,
    )
```

time: 94.3 us -> 97.8 us (1.037)
  local copies, waits for them, and re-layouts: 8.59 us -> 0.78 us
  waiting for transfers between devices: 28.5 us -> 35.9 us
  Pallas kernels: 28.1 us -> 30.7 us
    all_to_all x2, waiting for transfers between devices: 22.3 us -> 32.1 us  [the longest x1 16.2 us: column_of_subgrids(): lax.all_to_all(spread, 'facet', 0, 0, axis_index_groups=groups, tiled=True)]
    unnamed x46 -> x18, local copies, waits for them, and re-layouts: 7.86 us -> 0.05 us
    pallas_call x6 -> x8, Pallas kernels: 28.1 us -> 30.7 us  [run(): pl.pallas_call(kernel, out_shape=out_shape, in_specs=specs, out_specs=jax...]
    ppermute x6, waiting for transfers between devices: 5.15 us -> 2.84 us  [to_stokes(): lax.ppermute(array, 'stokes', [(i, (i - k) % 4) for i in range(4)])]
  transfers between devices with their start and end apart: 10 -> 10, of which waited for: 5 -> 6; matrix products, arithmetic and copies ran while one was open for 1% -> 1% of each run, Pallas kernels for 14% -> 15%
where the time goes in v3:
time: 97.8 us; the launch traced here: 97 us
  waiting for transfers between devices  35.9 us (37%)
  Pallas kernels  30.7 us (31%)
  starting transfers between devices  28.8 us (29%)
    pallas_call x8, Pallas kernels, run(): pl.pallas_call(kernel, out_shape=out_shape, in_specs=specs, out_specs=jax...  30.7 us
    all_to_all x1, waiting for transfers between devices, column_of_subgrids(): lax.all_to_all(spread, 'facet', 0, 0, axis_index_groups=groups, tiled=True)  16.2 us
    all_to_all x1, waiting for transfers between devices, column_of_subgrids(): lax.all_to_all(shares, 'facet', 0, 0, axis_index_groups=groups, tiled=True)  15.9 us
    all_to_all x1, starting transfers between devices, column_of_subgrids(): lax.all_to_all(spread, 'facet', 0, 0, axis_index_groups=groups, tiled=True)  11.9 us
    ppermute x6, starting transfers between devices, to_stokes(): lax.ppermute(array, 'stokes', [(i, (i - k) % 4) for i in range(4)])  8.04 us
    all_to_all x1, starting transfers between devices, column_of_subgrids(): lax.all_to_all(shares, 'facet', 0, 0, axis_index_groups=groups, tiled=True)  4.37 us
    ppermute x6, waiting for transfers between devices, to_stokes(): lax.ppermute(array, 'stokes', [(i, (i - k) % 4) for i in range(4)])  2.84 us
    ppermute x1, starting transfers between devices, column_of_subgrids(): other = lax.ppermute(mine, 'facet', partner)  2.41 us
  transfers between devices with their start and end apart: 10, of which 6 were waited for; matrix products, arithmetic and copies ran while one was open for 1% of the time, Pallas kernels for 15%

profile of v3, /device:TPU:1, one launch (start us, length us, event | category | flops | bytes accessed | tf_op | source)
XLA Modules:
  0.0 97.0 jit_solution(14287546835172356054)
XLA Ops:
  0.6 0.0 copy-start
  0.6 0.0 copy-start.1
  0.7 0.0 copy-start.2
  0.7 0.0 copy-start.8
  0.7 3.0 %shard_map.113 = bf16[32,64,128]{2,1,0:T(8,128)(2,1)} custom-call(bf16[64,16384]{1,0:T(8,128)(2,1)} %bitcast.6, bf16[128,2048]{1,0:T(8,128)(2,1)} %constant.17.clone.column_ref), custom_call_target="tpu_custom_call" | custom-call | flops 1000000000 | bytes 1048576 | tf_op jit(solution)/shard_map/pallas_call | solution.py:363
  3.7 11.9 %all-to-all-start = ((bf16[32,64,128]{2,1,0:T(8,128)(2,1)}), bf16[32,64,128]{2,1,0:T(8,128)(2,1)S(1)}, u32[]{:S(2)}, u32[]{:S(2)}) async-start(bf16[32,64,128]{2,1,0:T(8,128)(2,1)} %shard_map.113), calls=%async_computation | async-start | bytes 1048576 | tf_op jit(solution)/shard_map/all_to_all | solution.py:408
  15.6 0.1 pad_add_fusion.here_ref
  15.7 16.2 %all-to-all-done.mine_ref = bf16[32,64,128]{2,1,0:T(8,128)(2,1)S(1)} async-done(((bf16[32,64,128]{2,1,0:T(8,128)(2,1)}), bf16[32,64,128]{2,1,0:T(8,128)(2,1)S(1)}, u32[]{:S(2)}, u32[]{:S(2)}) %all-to-all-start) | async-done | bytes 524320 | tf_op jit(solution)/shard_map/all_to_all | solution.py:408
  31.9 2.4 %collective-permute-start = (bf16[32,64,128]{2,1,0:T(8,128)(2,1)S(1)}, bf16[32,64,128]{2,1,0:T(8,128)(2,1)S(1)}, u32[]{:S(2)}, u32[]{:S(2)}) collective-permute-start(bf16[32,64,128]{2,1,0:T(8,128)(2,1)S(1)} %all-to-all-done.mine_ref), channel_id=1, source_target_pairs={{0,4},{4,0},{8,12},{12,8},{16,20},{20,16},{24,28},{28,24},{32,36},... | collective-permute-start | bytes 1572872 | tf_op jit(solution)/shard_map/ppermute | solution.py:428
  34.3 0.0 copy-done
  34.3 0.0 copy-done.1
  34.3 0.0 copy-done.2
  34.3 0.0 copy-done.8
  34.3 0.0 copy-start.4
  34.3 0.0 copy-start.6
  34.3 0.0 copy-start.7
  34.3 4.4 %shard_map.115 = (f32[128,128]{1,0:T(8,128)S(1)}, f32[128,128]{1,0:T(8,128)S(1)}, f32[128,128]{1,0:T(8,128)S(1)}, f32[256,128]{1,0:T(8,128)S(1)}, bf16[256,128]{...) custom-call(s32[2]{0:T(128)S(1)} %pad_add_fusion.here_ref, s32[3,2,8192]{2,1,0:T(2,128)S(1)} %copy-done, ...), custom_call_target="tpu_custom_call" | custom-call | flops 10000000000 | bytes 1048576 | tf_op jit(solution)/shard_map/pallas_call | solution.py:363
  38.8 1.4 %collective-permute-start.6 = (bf16[256,128]{1,0:T(8,128)(2,1)S(1)}, bf16[256,128]{1,0:T(8,128)(2,1)S(1)}, u32[]{:S(2)}, u32[]{:S(2)}) collective-permute-start(bf16[256,128]{1,0:T(8,128)(2,1)S(1)} %get-tuple-element.12), channel_id=1, source_target_pairs={{0,1},{1,2},{2,3},{3,0},{4,5},{5,6},{6,7},{7,4},{8,9},{9,10},{10,1... | collective-permute-start | bytes 196616 | tf_op jit(solution)/shard_map/ppermute | solution.py:394
  40.1 2.6 %collective-permute-start.5 = (bf16[256,128]{1,0:T(8,128)(2,1)S(1)}, bf16[256,128]{1,0:T(8,128)(2,1)S(1)}, u32[]{:S(2)}, u32[]{:S(2)}) collective-permute-start(bf16[256,128]{1,0:T(8,128)(2,1)S(1)} %get-tuple-element.12), channel_id=1, source_target_pairs={{0,2},{1,3},{2,0},{3,1},{4,6},{5,7},{6,4},{7,5},{8,10},{9,11},{10,... | collective-permute-start | bytes 196616 | tf_op jit(solution)/shard_map/ppermute | solution.py:394
  42.8 1.1 %collective-permute-start.4 = (bf16[256,128]{1,0:T(8,128)(2,1)S(1)}, bf16[256,128]{1,0:T(8,128)(2,1)S(1)}, u32[]{:S(2)}, u32[]{:S(2)}) collective-permute-start(bf16[256,128]{1,0:T(8,128)(2,1)S(1)} %get-tuple-element.12), channel_id=1, source_target_pairs={{0,3},{1,0},{2,1},{3,2},{4,7},{5,4},{6,5},{7,6},{8,11},{9,8},{10,9... | collective-permute-start | bytes 196616 | tf_op jit(solution)/shard_map/ppermute | solution.py:394
  43.8 0.0 copy-done.4
  43.8 0.0 copy-done.6
  43.8 0.0 copy-done.7
  43.8 3.0 %shard_map.114.start_ref = f32[256,256]{1,0:T(8,128)S(1)} custom-call(s32[2]{0:T(128)S(1)} %pad_add_fusion.here_ref, s32[128]{0:T(128)S(1)} %copy-done.4, bf16[32,64,128]{2,1,0:T(8,128)(2,1)S(1)} %all-to-all-done.mine_ref, f32[128,256]{1,0:T(8,128)S(1)} %copy-done.7, f32[128,256]{1,0:T(8,128)S(1)} %copy-done.6), custom_call_target="tpu_custom_call" | custom-call | flops 1000000000 | bytes 1048576 | tf_op jit(solution)/shard_map/pallas_call | solution.py:363
  46.8 0.0 collective-permute-done.other_ref
  46.8 6.9 %shard_map.116.a_ref = bf16[256,128]{1,0:T(8,128)(2,1)S(1)} custom-call(s32[2]{0:T(128)S(1)} %pad_add_fusion.here_ref, s32[128]{0:T(128)S(1)} %copy-done.4, f32[256,256]{1,0:T(8,128)S(1)} %shard_map.114.start_ref, bf16[32,64,128]{2,1,0:T(8,128)(2,1)S(1)} %collective-permute-done.other_ref, f32[128,256]{1,0:T(8,128)S(1)} %copy-done.7, ...), custom_call_target="tpu_custom_call" | custom-call | flops 1000000000 | bytes 1048576 | tf_op jit(solution)/shard_map/pallas_call | solution.py:363
  53.8 0.0 copy-start.3
  53.8 0.5 collective-permute-start.3
  54.3 0.8 collective-permute-start.2
  55.1 0.0 collective-permute-done.6.d_ref
  55.1 1.7 %collective-permute-start.1 = (bf16[256,128]{1,0:T(8,128)(2,1)S(1)}, bf16[256,128]{1,0:T(8,128)(2,1)S(1)}, u32[]{:S(2)}, u32[]{:S(2)}) collective-permute-start(bf16[256,128]{1,0:T(8,128)(2,1)S(1)} %shard_map.116.a_ref), channel_id=1, source_target_pairs={{0,3},{1,0},{2,1},{3,2},{4,7},{5,4},{6,5},{7,6},{8,11},{9,8},{10,9... | collective-permute-start | bytes 196616 | tf_op jit(solution)/shard_map/ppermute | solution.py:394
  56.8 0.0 collective-permute-done.5.c_ref
  56.8 0.0 collective-permute-done.4.b_ref
  56.8 0.2 shard_map.117.turned_ref
  56.9 1.3 %collective-permute-done.3.d_ref = bf16[256,128]{1,0:T(8,128)(2,1)S(1)} collective-permute-done((bf16[256,128]{1,0:T(8,128)(2,1)S(1)}, bf16[256,128]{1,0:T(8,128)(2,1)S(1)}, u32[]{:S(2)}, u32[]{:S(2)}) %collective-permute-start.3) | collective-permute-done | bytes 65568 | tf_op jit(solution)/shard_map/ppermute | solution.py:394
  58.2 0.7 collective-permute-done.2.c_ref
  58.9 0.9 collective-permute-done.1.b_ref
  59.8 0.0 copy-done.3
  59.8 6.3 %shard_map.118 = (f32[256,128]{1,0:T(8,128)S(1)}, bf16[256,256]{1,0:T(8,128)(2,1)S(1)}) custom-call(s32[2]{0:T(128)S(1)} %copy-done.3, bf16[256,128]{1,0:T(8,128)(2,1)S(1)} %shard_map.116.a_ref, bf16[256,128]{1,0:T(8,128)(2,1)S(1)} %collective-permute-done.1.b_ref, bf16[256,128]{1,0:T(8,128)(2,1)S(1)} %collective-permute-done.2.c_ref, ...), custom_call_target="tpu_custom_call" | custom-call | flops 1000000000 | bytes 1048576 | tf_op jit(solution)/shard_map/pallas_call | solution.py:363
  66.0 0.0 copy-start.5
  66.1 2.1 %collective-permute-start.7 = (bf16[256,256]{1,0:T(8,128)(2,1)S(1)}, bf16[256,256]{1,0:T(8,128)(2,1)S(1)}, u32[]{:S(2)}, u32[]{:S(2)}) collective-permute-start(bf16[256,256]{1,0:T(8,128)(2,1)S(1)} %get-tuple-element.16.mine_ref), channel_id=1, source_target_pairs={{0,4},{4,0},{8,12},{12,8},{16,20},{20,16},{24,28},{28,24},{32,36},... | collective-permute-start | bytes 393224 | tf_op jit(solution)/shard_map/ppermute | solution.py:455
  68.1 1.0 %collective-permute-done.7.other_ref = bf16[256,256]{1,0:T(8,128)(2,1)S(1)} collective-permute-done((bf16[256,256]{1,0:T(8,128)(2,1)S(1)}, bf16[256,256]{1,0:T(8,128)(2,1)S(1)}, u32[]{:S(2)}, u32[]{:S(2)}) %collective-permute-start.7) | collective-permute-done | bytes 131104 | tf_op jit(solution)/shard_map/ppermute | solution.py:455
  69.1 5.1 %shard_map.119 = bf16[32,64,128]{2,1,0:T(8,128)(2,1)} custom-call(s32[2]{0:T(128)S(1)} %pad_add_fusion.here_ref, s32[128]{0:T(128)S(1)} %copy-done.4, bf16[256,256]{1,0:T(8,128)(2,1)S(1)} %get-tuple-element.16.mine_ref, bf16[256,256]{1,0:T(8,128)(2,1)S(1)} %collective-permute-done.7.other_ref, f32[128,256]{1,0:T(8,128)S(1)} %copy-done.7, ...), custom_call_target="tpu_custom_call" | custom-call | flops 1000000000 | bytes 1048576 | tf_op jit(solution)/shard_map/pallas_call | solution.py:363
  74.2 4.4 %all-to-all-start.1 = ((bf16[32,64,128]{2,1,0:T(8,128)(2,1)}), bf16[32,64,128]{2,1,0:T(8,128)(2,1)S(1)}, u32[]{:S(2)}, u32[]{:S(2)}) async-start(bf16[32,64,128]{2,1,0:T(8,128)(2,1)} %shard_map.119), calls=%async_computation.1 | async-start | bytes 1048576 | tf_op jit(solution)/shard_map/all_to_all | solution.py:459
  78.6 0.7 reshape.7
  79.3 15.9 %all-to-all-done.1.shares_ref = bf16[32,64,128]{2,1,0:T(8,128)(2,1)S(1)} async-done(((bf16[32,64,128]{2,1,0:T(8,128)(2,1)}), bf16[32,64,128]{2,1,0:T(8,128)(2,1)S(1)}, u32[]{:S(2)}, u32[]{:S(2)}) %all-to-all-start.1) | async-done | bytes 524320 | tf_op jit(solution)/shard_map/all_to_all | solution.py:459
  95.2 0.0 copy-done.5
  95.2 1.8 %shard_map.120 = bf16[64,16384]{1,0:T(8,128)(2,1)} custom-call(bf16[32,64,128]{2,1,0:T(8,128)(2,1)S(1)} %all-to-all-done.1.shares_ref, bf16[128,2048]{1,0:T(8,128)(2,1)S(1)} %copy-done.5), custom_call_target="tpu_custom_call" | custom-call | flops 1000000000 | bytes 1048576 | tf_op jit(solution)/shard_map/pallas_call | solution.py:363
Async XLA Ops:
  0.6 33.7 %copy-start = (s32[3,2,8192]{2,1,0:T(2,128)S(1)}, s32[3,2,8192]{2,1,0:T(2,128)}, u32[]{:S(2)}) copy-start(s32[3,2,8192]{2,1,0:T(2,128)} %cells_ref.5) | copy-start | bytes 589828
  0.6 33.7 %copy-start.1 = (f32[1,2,2,8192]{3,2,1,0:T(2,128)S(1)}, f32[1,2,2,8192]{3,2,1,0:T(2,128)}, u32[]{:S(2)}) copy-start(f32[1,2,2,8192]{3,2,1,0:T(2,128)} %param.15) | copy-start | bytes 393220
  0.7 33.6 %copy-start.2 = (f32[4,4,2,64]{3,2,1,0:T(2,128)S(1)}, f32[4,4,2,64]{3,2,1,0:T(2,128)}, u32[]{:S(2)}) copy-start(f32[4,4,2,64]{3,2,1,0:T(2,128)} %mueller_ref.1) | copy-start | bytes 24580
  0.7 33.6 %copy-start.8 = (bf16[64,256]{1,0:T(8,128)(2,1)S(1)}, bf16[64,256]{1,0:T(8,128)(2,1)}, u32[]{:S(2)}) copy-start(bf16[64,256]{1,0:T(8,128)(2,1)} %constant.18.clone.kernel_ref) | copy-start | bytes 98308
  3.7 28.2 %all-to-all-start = ((bf16[32,64,128]{2,1,0:T(8,128)(2,1)}), bf16[32,64,128]{2,1,0:T(8,128)(2,1)S(1)}, u32[]{:S(2)}, u32[]{:S(2)}) async-start(bf16[32,64,128]{2,1,0:T(8,128)(2,1)} %shard_map.113), calls=%async_computation | async-start | bytes 1048576 | tf_op jit(solution)/shard_map/all_to_all | solution.py:408
  31.9 15.0 %collective-permute-start = (bf16[32,64,128]{2,1,0:T(8,128)(2,1)S(1)}, bf16[32,64,128]{2,1,0:T(8,128)(2,1)S(1)}, u32[]{:S(2)}, u32[]{:S(2)}) collective-permute-start(bf16[32,64,128]{2,1,0:T(8,128)(2,1)S(1)} %all-to-all-done.mine_ref), channel_id=1, source_target_pairs={{0,4},{4,0},{8,12},{12,8},{16,20},{20,16},{24,28},{28,24},{32,36},... | collective-permute-start | bytes 1572872 | tf_op jit(solution)/shard_map/ppermute | solution.py:428
  34.3 9.5 %copy-start.4 = (s32[128]{0:T(128)S(1)}, s32[128]{0:T(128)}, u32[]{:S(2)}) copy-start(s32[128]{0:T(128)} %sub_ref.5) | copy-start | bytes 1540
  34.3 9.5 %copy-start.6 = (f32[128,256]{1,0:T(8,128)S(1)}, f32[128,256]{1,0:T(8,128)}, u32[]{:S(2)}) copy-start(f32[128,256]{1,0:T(8,128)} %constant.20.clone.lift_s_ref) | copy-start | bytes 393220
  34.3 9.5 %copy-start.7 = (f32[128,256]{1,0:T(8,128)S(1)}, f32[128,256]{1,0:T(8,128)}, u32[]{:S(2)}) copy-start(f32[128,256]{1,0:T(8,128)} %constant.19.clone.lift_ref) | copy-start | bytes 393220
  38.8 16.3 %collective-permute-start.6 = (bf16[256,128]{1,0:T(8,128)(2,1)S(1)}, bf16[256,128]{1,0:T(8,128)(2,1)S(1)}, u32[]{:S(2)}, u32[]{:S(2)}) collective-permute-start(bf16[256,128]{1,0:T(8,128)(2,1)S(1)} %get-tuple-element.12), channel_id=1, source_target_pairs={{0,1},{1,2},{2,3},{3,0},{4,5},{5,6},{6,7},{7,4},{8,9},{9,10},{10,1... | collective-permute-start | bytes 196616 | tf_op jit(solution)/shard_map/ppermute | solution.py:394
  40.1 16.6 %collective-permute-start.5 = (bf16[256,128]{1,0:T(8,128)(2,1)S(1)}, bf16[256,128]{1,0:T(8,128)(2,1)S(1)}, u32[]{:S(2)}, u32[]{:S(2)}) collective-permute-start(bf16[256,128]{1,0:T(8,128)(2,1)S(1)} %get-tuple-element.12), channel_id=1, source_target_pairs={{0,2},{1,3},{2,0},{3,1},{4,6},{5,7},{6,4},{7,5},{8,10},{9,11},{10,... | collective-permute-start | bytes 196616 | tf_op jit(solution)/shard_map/ppermute | solution.py:394
  42.8 14.0 %collective-permute-start.4 = (bf16[256,128]{1,0:T(8,128)(2,1)S(1)}, bf16[256,128]{1,0:T(8,128)(2,1)S(1)}, u32[]{:S(2)}, u32[]{:S(2)}) collective-permute-start(bf16[256,128]{1,0:T(8,128)(2,1)S(1)} %get-tuple-element.12), channel_id=1, source_target_pairs={{0,3},{1,0},{2,1},{3,2},{4,7},{5,4},{6,5},{7,6},{8,11},{9,8},{10,9... | collective-permute-start | bytes 196616 | tf_op jit(solution)/shard_map/ppermute | solution.py:394
  53.8 6.0 %copy-start.3 = (s32[2]{0:T(128)S(1)}, s32[2]{0:T(128)}, u32[]{:S(2)}) copy-start(s32[2]{0:T(128)} %counts_ref.1) | copy-start | bytes 28
  53.8 4.4 %collective-permute-start.3 = (bf16[256,128]{1,0:T(8,128)(2,1)S(1)}, bf16[256,128]{1,0:T(8,128)(2,1)S(1)}, u32[]{:S(2)}, u32[]{:S(2)}) collective-permute-start(bf16[256,128]{1,0:T(8,128)(2,1)S(1)} %shard_map.116.a_ref), channel_id=1, source_target_pairs={{0,1},{1,2},{2,3},{3,0},{4,5},{5,6},{6,7},{7,4},{8,9},{9,10},{10,1... | collective-permute-start | bytes 196616 | tf_op jit(solution)/shard_map/ppermute | solution.py:394
  54.3 4.6 %collective-permute-start.2 = (bf16[256,128]{1,0:T(8,128)(2,1)S(1)}, bf16[256,128]{1,0:T(8,128)(2,1)S(1)}, u32[]{:S(2)}, u32[]{:S(2)}) collective-permute-start(bf16[256,128]{1,0:T(8,128)(2,1)S(1)} %shard_map.116.a_ref), channel_id=1, source_target_pairs={{0,2},{1,3},{2,0},{3,1},{4,6},{5,7},{6,4},{7,5},{8,10},{9,11},{10,... | collective-permute-start | bytes 196616 | tf_op jit(solution)/shard_map/ppermute | solution.py:394
  55.1 4.7 %collective-permute-start.1 = (bf16[256,128]{1,0:T(8,128)(2,1)S(1)}, bf16[256,128]{1,0:T(8,128)(2,1)S(1)}, u32[]{:S(2)}, u32[]{:S(2)}) collective-permute-start(bf16[256,128]{1,0:T(8,128)(2,1)S(1)} %shard_map.116.a_ref), channel_id=1, source_target_pairs={{0,3},{1,0},{2,1},{3,2},{4,7},{5,4},{6,5},{7,6},{8,11},{9,8},{10,9... | collective-permute-start | bytes 196616 | tf_op jit(solution)/shard_map/ppermute | solution.py:394
  66.0 29.2 %copy-start.5 = (bf16[128,2048]{1,0:T(8,128)(2,1)S(1)}, bf16[128,2048]{1,0:T(8,128)(2,1)}, u32[]{:S(2)}) copy-start(bf16[128,2048]{1,0:T(8,128)(2,1)} %constant.17.clone.column_ref) | copy-start | bytes 1572868
  66.1 3.1 %collective-permute-start.7 = (bf16[256,256]{1,0:T(8,128)(2,1)S(1)}, bf16[256,256]{1,0:T(8,128)(2,1)S(1)}, u32[]{:S(2)}, u32[]{:S(2)}) collective-permute-start(bf16[256,256]{1,0:T(8,128)(2,1)S(1)} %get-tuple-element.16.mine_ref), channel_id=1, source_target_pairs={{0,4},{4,0},{8,12},{12,8},{16,20},{20,16},{24,28},{28,24},{32,36},... | collective-permute-start | bytes 393224 | tf_op jit(solution)/shard_map/ppermute | solution.py:455
  74.2 21.0 %all-to-all-start.1 = ((bf16[32,64,128]{2,1,0:T(8,128)(2,1)}), bf16[32,64,128]{2,1,0:T(8,128)(2,1)S(1)}, u32[]{:S(2)}, u32[]{:S(2)}) async-start(bf16[32,64,128]{2,1,0:T(8,128)(2,1)} %shard_map.119), calls=%async_computation.1 | async-start | bytes 1048576 | tf_op jit(solution)/shard_map/all_to_all | solution.py:459

commit v4 on v3

--- a/solution.py
+++ b/solution.py
@@ -20,8 +20,8 @@
 MAXB = 64
 BLOCK = 128
 VISITS = 8192
-CHUNK = 512
-GROUP = 4
+CHUNK = 4096
+GROUP = 16
 
 f32 = jnp.float32
 bf16 = jnp.bfloat16
@@ -338,7 +338,7 @@
             out_ref[q] = (total * sign + swap(swapped)).astype(bf16)
         return carry
 
-    lax.fori_loop(0, 16, pair, 0, unroll=2)
+    lax.fori_loop(0, 16, pair, 0, unroll=4)
 
 
 def image_kernel(shares_ref, column_ref, out_ref):

time: 97.8 us -> 88.1 us (0.901)
  Pallas kernels: 30.7 us -> 21 us
    pallas_call x8, Pallas kernels: 30.7 us -> 21 us  [run(): pl.pallas_call(kernel, out_shape=out_shape, in_specs=specs, out_specs=jax...]
  transfers between devices with their start and end apart: 10 -> 10, of which waited for: 6 -> 6; matrix products, arithmetic and copies ran while one was open for 1% -> 1% of each run, Pallas kernels for 15% -> 10%
where the time goes in v4:
time: 88.1 us; the launch traced here: 87.4 us
  waiting for transfers between devices  35.9 us (41%)
  starting transfers between devices  28.8 us (33%)
  Pallas kernels  21 us (24%)
    pallas_call x8, Pallas kernels, run(): pl.pallas_call(kernel, out_shape=out_shape, in_specs=specs, out_specs=jax...  21 us
    all_to_all x1, waiting for transfers between devices, column_of_subgrids(): lax.all_to_all(spread, 'facet', 0, 0, axis_index_groups=groups, tiled=True)  16.2 us
    all_to_all x1, waiting for transfers between devices, column_of_subgrids(): lax.all_to_all(shares, 'facet', 0, 0, axis_index_groups=groups, tiled=True)  15.9 us
    all_to_all x1, starting transfers between devices, column_of_subgrids(): lax.all_to_all(spread, 'facet', 0, 0, axis_index_groups=groups, tiled=True)  11.9 us
    ppermute x6, starting transfers between devices, to_stokes(): lax.ppermute(array, 'stokes', [(i, (i - k) % 4) for i in range(4)])  8.01 us
    all_to_all x1, starting transfers between devices, column_of_subgrids(): lax.all_to_all(shares, 'facet', 0, 0, axis_index_groups=groups, tiled=True)  4.39 us
    ppermute x6, waiting for transfers between devices, to_stokes(): lax.ppermute(array, 'stokes', [(i, (i - k) % 4) for i in range(4)])  2.84 us
    ppermute x1, starting transfers between devices, column_of_subgrids(): other = lax.ppermute(mine, 'facet', partner)  2.43 us
  transfers between devices with their start and end apart: 10, of which 6 were waited for; matrix products, arithmetic and copies ran while one was open for 1% of the time, Pallas kernels for 10%

profile of v4, /device:TPU:1, one launch (start us, length us, event | category | flops | bytes accessed | tf_op | source)
XLA Modules:
  0.0 87.4 jit_solution(14296294859416674816)
XLA Ops:
  0.6 0.0 copy-start
  0.6 0.0 copy-start.1
  0.7 0.0 copy-start.2
  0.7 0.0 copy-start.8
  0.7 3.0 %shard_map.113 = bf16[32,64,128]{2,1,0:T(8,128)(2,1)} custom-call(bf16[64,16384]{1,0:T(8,128)(2,1)} %bitcast.6, bf16[128,2048]{1,0:T(8,128)(2,1)} %constant.17.clone.column_ref), custom_call_target="tpu_custom_call" | custom-call | flops 1000000000 | bytes 1048576 | tf_op jit(solution)/shard_map/pallas_call | solution.py:363
  3.7 11.9 %all-to-all-start = ((bf16[32,64,128]{2,1,0:T(8,128)(2,1)}), bf16[32,64,128]{2,1,0:T(8,128)(2,1)S(1)}, u32[]{:S(2)}, u32[]{:S(2)}) async-start(bf16[32,64,128]{2,1,0:T(8,128)(2,1)} %shard_map.113), calls=%async_computation | async-start | bytes 1048576 | tf_op jit(solution)/shard_map/all_to_all | solution.py:408
  15.6 0.1 pad_add_fusion.here_ref
  15.7 16.2 %all-to-all-done.mine_ref = bf16[32,64,128]{2,1,0:T(8,128)(2,1)S(1)} async-done(((bf16[32,64,128]{2,1,0:T(8,128)(2,1)}), bf16[32,64,128]{2,1,0:T(8,128)(2,1)S(1)}, u32[]{:S(2)}, u32[]{:S(2)}) %all-to-all-start) | async-done | bytes 524320 | tf_op jit(solution)/shard_map/all_to_all | solution.py:408
  31.9 2.4 %collective-permute-start = (bf16[32,64,128]{2,1,0:T(8,128)(2,1)S(1)}, bf16[32,64,128]{2,1,0:T(8,128)(2,1)S(1)}, u32[]{:S(2)}, u32[]{:S(2)}) collective-permute-start(bf16[32,64,128]{2,1,0:T(8,128)(2,1)S(1)} %all-to-all-done.mine_ref), channel_id=1, source_target_pairs={{0,4},{4,0},{8,12},{12,8},{16,20},{20,16},{24,28},{28,24},{32,36},... | collective-permute-start | bytes 1572872 | tf_op jit(solution)/shard_map/ppermute | solution.py:428
  34.3 0.0 copy-done
  34.3 0.0 copy-done.1
  34.3 0.0 copy-done.2
  34.3 0.0 copy-done.8
  34.3 0.0 copy-start.4
  34.3 0.0 copy-start.6
  34.3 0.0 copy-start.7
  34.4 2.4 %shard_map.115 = (f32[128,128]{1,0:T(8,128)S(1)}, f32[128,128]{1,0:T(8,128)S(1)}, f32[128,128]{1,0:T(8,128)S(1)}, f32[256,128]{1,0:T(8,128)S(1)}, bf16[256,128]{...) custom-call(s32[2]{0:T(128)S(1)} %pad_add_fusion.here_ref, s32[3,2,8192]{2,1,0:T(2,128)S(1)} %copy-done, ...), custom_call_target="tpu_custom_call" | custom-call | flops 10000000000 | bytes 1048576 | tf_op jit(solution)/shard_map/pallas_call | solution.py:363
  36.8 1.4 %collective-permute-start.6 = (bf16[256,128]{1,0:T(8,128)(2,1)S(1)}, bf16[256,128]{1,0:T(8,128)(2,1)S(1)}, u32[]{:S(2)}, u32[]{:S(2)}) collective-permute-start(bf16[256,128]{1,0:T(8,128)(2,1)S(1)} %get-tuple-element.12), channel_id=1, source_target_pairs={{0,1},{1,2},{2,3},{3,0},{4,5},{5,6},{6,7},{7,4},{8,9},{9,10},{10,1... | collective-permute-start | bytes 196616 | tf_op jit(solution)/shard_map/ppermute | solution.py:394
  38.1 2.6 %collective-permute-start.5 = (bf16[256,128]{1,0:T(8,128)(2,1)S(1)}, bf16[256,128]{1,0:T(8,128)(2,1)S(1)}, u32[]{:S(2)}, u32[]{:S(2)}) collective-permute-start(bf16[256,128]{1,0:T(8,128)(2,1)S(1)} %get-tuple-element.12), channel_id=1, source_target_pairs={{0,2},{1,3},{2,0},{3,1},{4,6},{5,7},{6,4},{7,5},{8,10},{9,11},{10,... | collective-permute-start | bytes 196616 | tf_op jit(solution)/shard_map/ppermute | solution.py:394
  40.7 1.1 %collective-permute-start.4 = (bf16[256,128]{1,0:T(8,128)(2,1)S(1)}, bf16[256,128]{1,0:T(8,128)(2,1)S(1)}, u32[]{:S(2)}, u32[]{:S(2)}) collective-permute-start(bf16[256,128]{1,0:T(8,128)(2,1)S(1)} %get-tuple-element.12), channel_id=1, source_target_pairs={{0,3},{1,0},{2,1},{3,2},{4,7},{5,4},{6,5},{7,6},{8,11},{9,8},{10,9... | collective-permute-start | bytes 196616 | tf_op jit(solution)/shard_map/ppermute | solution.py:394
  41.8 0.0 copy-done.4
  41.8 0.0 copy-done.6
  41.8 0.0 copy-done.7
  41.8 2.0 %shard_map.114.start_ref = f32[256,256]{1,0:T(8,128)S(1)} custom-call(s32[2]{0:T(128)S(1)} %pad_add_fusion.here_ref, s32[128]{0:T(128)S(1)} %copy-done.4, bf16[32,64,128]{2,1,0:T(8,128)(2,1)S(1)} %all-to-all-done.mine_ref, f32[128,256]{1,0:T(8,128)S(1)} %copy-done.7, f32[128,256]{1,0:T(8,128)S(1)} %copy-done.6), custom_call_target="tpu_custom_call" | custom-call | flops 1000000000 | bytes 1048576 | tf_op jit(solution)/shard_map/pallas_call | solution.py:363
  43.8 0.0 collective-permute-done.other_ref
  43.8 4.5 %shard_map.116.a_ref = bf16[256,128]{1,0:T(8,128)(2,1)S(1)} custom-call(s32[2]{0:T(128)S(1)} %pad_add_fusion.here_ref, s32[128]{0:T(128)S(1)} %copy-done.4, f32[256,256]{1,0:T(8,128)S(1)} %shard_map.114.start_ref, bf16[32,64,128]{2,1,0:T(8,128)(2,1)S(1)} %collective-permute-done.other_ref, f32[128,256]{1,0:T(8,128)S(1)} %copy-done.7, ...), custom_call_target="tpu_custom_call" | custom-call | flops 1000000000 | bytes 1048576 | tf_op jit(solution)/shard_map/pallas_call | solution.py:363
  48.3 0.0 copy-start.3
  48.3 0.5 collective-permute-start.3
  48.8 0.8 collective-permute-start.2
  49.6 0.0 collective-permute-done.6.d_ref
  49.6 1.7 %collective-permute-start.1 = (bf16[256,128]{1,0:T(8,128)(2,1)S(1)}, bf16[256,128]{1,0:T(8,128)(2,1)S(1)}, u32[]{:S(2)}, u32[]{:S(2)}) collective-permute-start(bf16[256,128]{1,0:T(8,128)(2,1)S(1)} %shard_map.116.a_ref), channel_id=1, source_target_pairs={{0,3},{1,0},{2,1},{3,2},{4,7},{5,4},{6,5},{7,6},{8,11},{9,8},{10,9... | collective-permute-start | bytes 196616 | tf_op jit(solution)/shard_map/ppermute | solution.py:394
  51.3 0.0 collective-permute-done.5.c_ref
  51.3 0.0 collective-permute-done.4.b_ref
  51.3 0.2 shard_map.117.turned_ref
  51.5 1.3 %collective-permute-done.3.d_ref = bf16[256,128]{1,0:T(8,128)(2,1)S(1)} collective-permute-done((bf16[256,128]{1,0:T(8,128)(2,1)S(1)}, bf16[256,128]{1,0:T(8,128)(2,1)S(1)}, u32[]{:S(2)}, u32[]{:S(2)}) %collective-permute-start.3) | collective-permute-done | bytes 65568 | tf_op jit(solution)/shard_map/ppermute | solution.py:394
  52.7 0.7 collective-permute-done.2.c_ref
  53.4 0.9 collective-permute-done.1.b_ref
  54.3 0.0 copy-done.3
  54.3 3.1 %shard_map.118 = (f32[256,128]{1,0:T(8,128)S(1)}, bf16[256,256]{1,0:T(8,128)(2,1)S(1)}) custom-call(s32[2]{0:T(128)S(1)} %copy-done.3, bf16[256,128]{1,0:T(8,128)(2,1)S(1)} %shard_map.116.a_ref, bf16[256,128]{1,0:T(8,128)(2,1)S(1)} %collective-permute-done.1.b_ref, bf16[256,128]{1,0:T(8,128)(2,1)S(1)} %collective-permute-done.2.c_ref, ...), custom_call_target="tpu_custom_call" | custom-call | flops 1000000000 | bytes 1048576 | tf_op jit(solution)/shard_map/pallas_call | solution.py:363
  57.4 0.0 copy-start.5
  57.4 2.1 %collective-permute-start.7 = (bf16[256,256]{1,0:T(8,128)(2,1)S(1)}, bf16[256,256]{1,0:T(8,128)(2,1)S(1)}, u32[]{:S(2)}, u32[]{:S(2)}) collective-permute-start(bf16[256,256]{1,0:T(8,128)(2,1)S(1)} %get-tuple-element.16.mine_ref), channel_id=1, source_target_pairs={{0,4},{4,0},{8,12},{12,8},{16,20},{20,16},{24,28},{28,24},{32,36},... | collective-permute-start | bytes 393224 | tf_op jit(solution)/shard_map/ppermute | solution.py:455
  59.5 1.0 %collective-permute-done.7.other_ref = bf16[256,256]{1,0:T(8,128)(2,1)S(1)} collective-permute-done((bf16[256,256]{1,0:T(8,128)(2,1)S(1)}, bf16[256,256]{1,0:T(8,128)(2,1)S(1)}, u32[]{:S(2)}, u32[]{:S(2)}) %collective-permute-start.7) | collective-permute-done | bytes 131104 | tf_op jit(solution)/shard_map/ppermute | solution.py:455
  60.5 4.0 %shard_map.119 = bf16[32,64,128]{2,1,0:T(8,128)(2,1)} custom-call(s32[2]{0:T(128)S(1)} %pad_add_fusion.here_ref, s32[128]{0:T(128)S(1)} %copy-done.4, bf16[256,256]{1,0:T(8,128)(2,1)S(1)} %get-tuple-element.16.mine_ref, bf16[256,256]{1,0:T(8,128)(2,1)S(1)} %collective-permute-done.7.other_ref, f32[128,256]{1,0:T(8,128)S(1)} %copy-done.7, ...), custom_call_target="tpu_custom_call" | custom-call | flops 1000000000 | bytes 1048576 | tf_op jit(solution)/shard_map/pallas_call | solution.py:363
  64.5 4.4 %all-to-all-start.1 = ((bf16[32,64,128]{2,1,0:T(8,128)(2,1)}), bf16[32,64,128]{2,1,0:T(8,128)(2,1)S(1)}, u32[]{:S(2)}, u32[]{:S(2)}) async-start(bf16[32,64,128]{2,1,0:T(8,128)(2,1)} %shard_map.119), calls=%async_computation.1 | async-start | bytes 1048576 | tf_op jit(solution)/shard_map/all_to_all | solution.py:459
  68.9 0.7 reshape.7
  69.7 15.9 %all-to-all-done.1.shares_ref = bf16[32,64,128]{2,1,0:T(8,128)(2,1)S(1)} async-done(((bf16[32,64,128]{2,1,0:T(8,128)(2,1)}), bf16[32,64,128]{2,1,0:T(8,128)(2,1)S(1)}, u32[]{:S(2)}, u32[]{:S(2)}) %all-to-all-start.1) | async-done | bytes 524320 | tf_op jit(solution)/shard_map/all_to_all | solution.py:459
  85.5 0.0 copy-done.5
  85.5 1.8 %shard_map.120 = bf16[64,16384]{1,0:T(8,128)(2,1)} custom-call(bf16[32,64,128]{2,1,0:T(8,128)(2,1)S(1)} %all-to-all-done.1.shares_ref, bf16[128,2048]{1,0:T(8,128)(2,1)S(1)} %copy-done.5), custom_call_target="tpu_custom_call" | custom-call | flops 1000000000 | bytes 1048576 | tf_op jit(solution)/shard_map/pallas_call | solution.py:363
Async XLA Ops:
  0.6 33.7 %copy-start = (s32[3,2,8192]{2,1,0:T(2,128)S(1)}, s32[3,2,8192]{2,1,0:T(2,128)}, u32[]{:S(2)}) copy-start(s32[3,2,8192]{2,1,0:T(2,128)} %cells_ref.5) | copy-start | bytes 589828
  0.6 33.7 %copy-start.1 = (f32[1,2,2,8192]{3,2,1,0:T(2,128)S(1)}, f32[1,2,2,8192]{3,2,1,0:T(2,128)}, u32[]{:S(2)}) copy-start(f32[1,2,2,8192]{3,2,1,0:T(2,128)} %param.15) | copy-start | bytes 393220
  0.7 33.7 %copy-start.2 = (f32[4,4,2,64]{3,2,1,0:T(2,128)S(1)}, f32[4,4,2,64]{3,2,1,0:T(2,128)}, u32[]{:S(2)}) copy-start(f32[4,4,2,64]{3,2,1,0:T(2,128)} %mueller_ref.1) | copy-start | bytes 24580
  0.7 33.7 %copy-start.8 = (bf16[64,256]{1,0:T(8,128)(2,1)S(1)}, bf16[64,256]{1,0:T(8,128)(2,1)}, u32[]{:S(2)}) copy-start(bf16[64,256]{1,0:T(8,128)(2,1)} %constant.18.clone.kernel_ref) | copy-start | bytes 98308
  3.7 28.2 %all-to-all-start = ((bf16[32,64,128]{2,1,0:T(8,128)(2,1)}), bf16[32,64,128]{2,1,0:T(8,128)(2,1)S(1)}, u32[]{:S(2)}, u32[]{:S(2)}) async-start(bf16[32,64,128]{2,1,0:T(8,128)(2,1)} %shard_map.113), calls=%async_computation | async-start | bytes 1048576 | tf_op jit(solution)/shard_map/all_to_all | solution.py:408
  31.9 12.0 %collective-permute-start = (bf16[32,64,128]{2,1,0:T(8,128)(2,1)S(1)}, bf16[32,64,128]{2,1,0:T(8,128)(2,1)S(1)}, u32[]{:S(2)}, u32[]{:S(2)}) collective-permute-start(bf16[32,64,128]{2,1,0:T(8,128)(2,1)S(1)} %all-to-all-done.mine_ref), channel_id=1, source_target_pairs={{0,4},{4,0},{8,12},{12,8},{16,20},{20,16},{24,28},{28,24},{32,36},... | collective-permute-start | bytes 1572872 | tf_op jit(solution)/shard_map/ppermute | solution.py:428
  34.3 7.5 %copy-start.4 = (s32[128]{0:T(128)S(1)}, s32[128]{0:T(128)}, u32[]{:S(2)}) copy-start(s32[128]{0:T(128)} %sub_ref.5) | copy-start | bytes 1540
  34.3 7.5 %copy-start.6 = (f32[128,256]{1,0:T(8,128)S(1)}, f32[128,256]{1,0:T(8,128)}, u32[]{:S(2)}) copy-start(f32[128,256]{1,0:T(8,128)} %constant.20.clone.lift_s_ref) | copy-start | bytes 393220
  34.3 7.5 %copy-start.7 = (f32[128,256]{1,0:T(8,128)S(1)}, f32[128,256]{1,0:T(8,128)}, u32[]{:S(2)}) copy-start(f32[128,256]{1,0:T(8,128)} %constant.19.clone.lift_ref) | copy-start | bytes 393220
  36.8 12.8 %collective-permute-start.6 = (bf16[256,128]{1,0:T(8,128)(2,1)S(1)}, bf16[256,128]{1,0:T(8,128)(2,1)S(1)}, u32[]{:S(2)}, u32[]{:S(2)}) collective-permute-start(bf16[256,128]{1,0:T(8,128)(2,1)S(1)} %get-tuple-element.12), channel_id=1, source_target_pairs={{0,1},{1,2},{2,3},{3,0},{4,5},{5,6},{6,7},{7,4},{8,9},{9,10},{10,1... | collective-permute-start | bytes 196616 | tf_op jit(solution)/shard_map/ppermute | solution.py:394
  38.1 13.2 %collective-permute-start.5 = (bf16[256,128]{1,0:T(8,128)(2,1)S(1)}, bf16[256,128]{1,0:T(8,128)(2,1)S(1)}, u32[]{:S(2)}, u32[]{:S(2)}) collective-permute-start(bf16[256,128]{1,0:T(8,128)(2,1)S(1)} %get-tuple-element.12), channel_id=1, source_target_pairs={{0,2},{1,3},{2,0},{3,1},{4,6},{5,7},{6,4},{7,5},{8,10},{9,11},{10,... | collective-permute-start | bytes 196616 | tf_op jit(solution)/shard_map/ppermute | solution.py:394
  40.7 10.6 %collective-permute-start.4 = (bf16[256,128]{1,0:T(8,128)(2,1)S(1)}, bf16[256,128]{1,0:T(8,128)(2,1)S(1)}, u32[]{:S(2)}, u32[]{:S(2)}) collective-permute-start(bf16[256,128]{1,0:T(8,128)(2,1)S(1)} %get-tuple-element.12), channel_id=1, source_target_pairs={{0,3},{1,0},{2,1},{3,2},{4,7},{5,4},{6,5},{7,6},{8,11},{9,8},{10,9... | collective-permute-start | bytes 196616 | tf_op jit(solution)/shard_map/ppermute | solution.py:394
  48.3 6.0 %copy-start.3 = (s32[2]{0:T(128)S(1)}, s32[2]{0:T(128)}, u32[]{:S(2)}) copy-start(s32[2]{0:T(128)} %counts_ref.1) | copy-start | bytes 28
  48.3 4.4 %collective-permute-start.3 = (bf16[256,128]{1,0:T(8,128)(2,1)S(1)}, bf16[256,128]{1,0:T(8,128)(2,1)S(1)}, u32[]{:S(2)}, u32[]{:S(2)}) collective-permute-start(bf16[256,128]{1,0:T(8,128)(2,1)S(1)} %shard_map.116.a_ref), channel_id=1, source_target_pairs={{0,1},{1,2},{2,3},{3,0},{4,5},{5,6},{6,7},{7,4},{8,9},{9,10},{10,1... | collective-permute-start | bytes 196616 | tf_op jit(solution)/shard_map/ppermute | solution.py:394
  48.8 4.6 %collective-permute-start.2 = (bf16[256,128]{1,0:T(8,128)(2,1)S(1)}, bf16[256,128]{1,0:T(8,128)(2,1)S(1)}, u32[]{:S(2)}, u32[]{:S(2)}) collective-permute-start(bf16[256,128]{1,0:T(8,128)(2,1)S(1)} %shard_map.116.a_ref), channel_id=1, source_target_pairs={{0,2},{1,3},{2,0},{3,1},{4,6},{5,7},{6,4},{7,5},{8,10},{9,11},{10,... | collective-permute-start | bytes 196616 | tf_op jit(solution)/shard_map/ppermute | solution.py:394
  49.6 4.7 %collective-permute-start.1 = (bf16[256,128]{1,0:T(8,128)(2,1)S(1)}, bf16[256,128]{1,0:T(8,128)(2,1)S(1)}, u32[]{:S(2)}, u32[]{:S(2)}) collective-permute-start(bf16[256,128]{1,0:T(8,128)(2,1)S(1)} %shard_map.116.a_ref), channel_id=1, source_target_pairs={{0,3},{1,0},{2,1},{3,2},{4,7},{5,4},{6,5},{7,6},{8,11},{9,8},{10,9... | collective-permute-start | bytes 196616 | tf_op jit(solution)/shard_map/ppermute | solution.py:394
  57.4 28.1 %copy-start.5 = (bf16[128,2048]{1,0:T(8,128)(2,1)S(1)}, bf16[128,2048]{1,0:T(8,128)(2,1)}, u32[]{:S(2)}) copy-start(bf16[128,2048]{1,0:T(8,128)(2,1)} %constant.17.clone.column_ref) | copy-start | bytes 1572868
  57.4 3.1 %collective-permute-start.7 = (bf16[256,256]{1,0:T(8,128)(2,1)S(1)}, bf16[256,256]{1,0:T(8,128)(2,1)S(1)}, u32[]{:S(2)}, u32[]{:S(2)}) collective-permute-start(bf16[256,256]{1,0:T(8,128)(2,1)S(1)} %get-tuple-element.16.mine_ref), channel_id=1, source_target_pairs={{0,4},{4,0},{8,12},{12,8},{16,20},{20,16},{24,28},{28,24},{32,36},... | collective-permute-start | bytes 393224 | tf_op jit(solution)/shard_map/ppermute | solution.py:455
  64.5 21.0 %all-to-all-start.1 = ((bf16[32,64,128]{2,1,0:T(8,128)(2,1)}), bf16[32,64,128]{2,1,0:T(8,128)(2,1)S(1)}, u32[]{:S(2)}, u32[]{:S(2)}) async-start(bf16[32,64,128]{2,1,0:T(8,128)(2,1)} %shard_map.119), calls=%async_computation.1 | async-start | bytes 1048576 | tf_op jit(solution)/shard_map/all_to_all | solution.py:459

commit v5 on v4

--- a/solution.py
+++ b/solution.py
@@ -22,6 +22,8 @@
 VISITS = 8192
 CHUNK = 4096
 GROUP = 16
+PIECES = 4
+PIECE = PERIOD // PIECES
 
 f32 = jnp.float32
 bf16 = jnp.bfloat16
@@ -71,27 +73,32 @@
 
 
 def column_kernel(strips_ref, column_ref, out_ref, strips_buf, column_buf, sems):
-    copies = [
-        pltpu.make_async_copy(
-            strips_ref.at[:, pl.ds(i * PERIOD, PERIOD)], strips_buf.at[i], sems.at[i]
+    copies = []
+    for piece in range(PIECES):
+        start = piece * PIECE
+        group = [
+            pltpu.make_async_copy(
+                strips_ref.at[:, pl.ds(i * PERIOD + start, PIECE)], strips_buf.at[piece, i], sems.at[piece, i]
+            )
+            for i in range(8)
+        ]
+        group.append(
+            pltpu.make_async_copy(
+                column_ref.at[:, pl.ds(start, PIECE)], column_buf.at[piece], sems.at[piece, 8]
+            )
         )
-        for i in range(8)
-    ]
-    table = pltpu.make_async_copy(column_ref, column_buf, sems.at[8])
-    for copy in copies:
-        copy.start()
-    table.start()
-    parts = []
-    for part in range(2):
-        copies[4 * part].wait()
-        copies[4 * part + 1].wait()
-        folded = strips_buf[4 * part].astype(f32) + strips_buf[4 * part + 1].astype(f32)
-        copies[4 * part + 2].wait()
-        copies[4 * part + 3].wait()
-        folded = folded + strips_buf[4 * part + 2].astype(f32) + strips_buf[4 * part + 3].astype(f32)
-        parts.append(folded.astype(bf16))
-    table.wait()
-    product = nt_dot(column_buf[...], jnp.concatenate(parts, 0))
+        for copy in group:
+            copy.start()
+        copies.append(group)
+    product = jnp.zeros((2 * K, 2 * ROWS), f32)
+    for piece in range(PIECES):
+        for copy in copies[piece]:
+            copy.wait()
+        parts = [
+            sum(strips_buf[piece, 4 * part + turn].astype(f32) for turn in range(4)).astype(bf16)
+            for part in range(2)
+        ]
+        product = product + nt_dot(column_buf[piece], jnp.concatenate(parts, 0))
     coeffs = (product[:K] - half_sign() * swap(product[K:])).astype(bf16)
     for q in range(32):
         out_ref[q] = coeffs
@@ -281,8 +288,12 @@
             return sum(mix_ref[here, first + t : first + t + 1] * s for t, s in enumerate(samples))
 
         m_re, m_im = mixed(0, s_re), mixed(0, s_im)
-        resid_ref[re, :] = jnp.where(live, seen_ref[re, :] - (m_re * cosine + m_im * sine), 0.0)
-        resid_ref[im, :] = jnp.where(live, seen_ref[im, :] - (m_im * cosine - m_re * sine), 0.0)
+        left_re = jnp.where(live, seen_ref[re, :] - (m_re * cosine + m_im * sine), 0.0)
+        left_im = jnp.where(live, seen_ref[im, :] - (m_im * cosine - m_re * sine), 0.0)
+        for b in range(MAXB):
+            lanes = slice(b * BLOCK, (b + 1) * BLOCK)
+            resid_ref[sub, 0:1, lanes] = left_re[b : b + 1, :]
+            resid_ref[sub, 1:2, lanes] = left_im[b : b + 1, :]
         back_ref[re, :] = jnp.where(live, turned_ref[re, :] - mixed(16, s_re), 0.0)
         back_ref[im, :] = jnp.where(live, turned_ref[im, :] - mixed(16, s_im), 0.0)
     per = CHUNK // BLOCK
@@ -341,30 +352,42 @@
     lax.fori_loop(0, 16, pair, 0, unroll=4)
 
 
-def image_kernel(shares_ref, column_ref, out_ref):
+def image_kernel(shares_ref, column_ref, out_ref, image_buf, sems):
     total = shares_ref[0].astype(f32)
     for q in range(1, 32):
         total = total + shares_ref[q].astype(f32)
     total = total.astype(bf16).astype(f32)
     both = jnp.concatenate([total, half_sign() * swap(total)], 0)
     left = jnp.transpose(both).astype(bf16)
-    image = (8.0 * jnp.dot(left, column_ref[...], preferred_element_type=f32)).astype(bf16)
-    for turn in range(4):
-        out_ref[:, turn * PERIOD : (turn + 1) * PERIOD] = image[:ROWS]
-        out_ref[:, L + turn * PERIOD : L + (turn + 1) * PERIOD] = image[ROWS:]
-
-
-def call(kernel, out_shape, scratch=(), smem=0, limit=16, flops=10**9, hbm=False):
+    copies = []
+    for piece in range(PIECES):
+        start = piece * PIECE
+        image = jnp.dot(left, column_ref[:, start : start + PIECE], preferred_element_type=f32)
+        image_buf[piece] = (8.0 * image).astype(bf16)
+        for i in range(8):
+            copy = pltpu.make_async_copy(
+                image_buf.at[piece, pl.ds(i // 4 * ROWS, ROWS)],
+                out_ref.at[:, pl.ds(i * PERIOD + start, PIECE)],
+                sems.at[piece, i],
+            )
+            copy.start()
+            copies.append(copy)
+    for copy in copies:
+        copy.wait()
+
+
+def call(kernel, out_shape, scratch=(), smem=0, limit=16, flops=10**9, hbm=False, hbm_out=False):
     vmem = pl.BlockSpec(memory_space=pltpu.VMEM)
 
     def run(*args):
         place = pl.BlockSpec(memory_space=pltpu.HBM) if hbm else vmem
         specs = [pl.BlockSpec(memory_space=pltpu.SMEM)] * smem + [place] * (len(args) - smem)
+        result = pl.BlockSpec(memory_space=pltpu.HBM) if hbm_out else vmem
         return pl.pallas_call(
             kernel,
             out_shape=out_shape,
             in_specs=specs,
-            out_specs=jax.tree.map(lambda _: vmem, out_shape),
+            out_specs=jax.tree.map(lambda _: result, out_shape),
             scratch_shapes=list(scratch),
             cost_estimate=pl.CostEstimate(flops=flops, bytes_accessed=2**20, transcendentals=0),
             compiler_params=pltpu.CompilerParams(vmem_limit_bytes=limit * 2**20),
@@ -398,9 +421,9 @@
         column_kernel,
         shape((32, K, 2 * ROWS), bf16),
         (
-            pltpu.VMEM((8, ROWS, PERIOD), bf16),
-            pltpu.VMEM((2 * K, PERIOD), bf16),
-            pltpu.SemaphoreType.DMA((9,)),
+            pltpu.VMEM((PIECES, 8, ROWS, PIECE), bf16),
+            pltpu.VMEM((PIECES, 2 * K, PIECE), bf16),
+            pltpu.SemaphoreType.DMA((PIECES, 9)),
         ),
         limit=60,
         hbm=True,
@@ -448,7 +471,7 @@
     )(position, sub_u, rows, other, lift_t, lift_s, uvw, weights)
     resid, adj = call(
         residual_kernel,
-        (shape((4 * MAXB, BLOCK), f32), shape((4 * K, G), bf16)),
+        (shape((2, 2, VISITS), f32), shape((4 * K, G), bf16)),
         (pltpu.VMEM((4 * MAXB, BLOCK), f32),),
         smem=1,
     )(counts, *to_stokes(samples), seen, turned, mix, vcos, vsin, uvw, weights)
@@ -457,8 +480,13 @@
         position, sub_u, adj, other_adj, lift_t, lift_s
     )
     shares = lax.all_to_all(shares, "facet", 0, 0, axis_index_groups=groups, tiled=True)
-    image = call(image_kernel, shape((ROWS, 2 * L), bf16))(shares, column)
-    return (image[None], resid.reshape(1, 2, 2, VISITS))
+    image = call(
+        image_kernel,
+        shape((ROWS, 2 * L), bf16),
+        (pltpu.VMEM((PIECES, 2 * ROWS, PIECE), bf16), pltpu.SemaphoreType.DMA((PIECES, 8))),
+        hbm_out=True,
+    )(shares, column)
+    return (image[None], resid[None])
 
 
 def solution(mesh):

time: 88.1 us -> 88.2 us (level)
  blocking collectives: 0 us -> 20.8 us
  waiting for transfers between devices: 35.9 us -> 20 us
  starting transfers between devices: 28.8 us -> 24.3 us
    all_to_all x0 -> x1, blocking collectives: none -> 20.8 us  [column_of_subgrids(): lax.all_to_all(shares, 'facet', 0, 0, axis_index_groups=groups, tiled=True)]
    all_to_all x1 -> x0, waiting for transfers between devices: 15.9 us -> none  [column_of_subgrids(): lax.all_to_all(shares, 'facet', 0, 0, axis_index_groups=groups, tiled=True)]
    all_to_all x1 -> x0, starting transfers between devices: 4.39 us -> none  [column_of_subgrids(): lax.all_to_all(shares, 'facet', 0, 0, axis_index_groups=groups, tiled=True)]
  transfers between devices with their start and end apart: 10 -> 9, of which waited for: 6 -> 5; matrix products, arithmetic and copies ran while one was open for 1% -> 0% of each run, Pallas kernels for 10% -> 10%
where the time goes in v5:
time: 88.2 us; the launch traced here: 87.5 us
  starting transfers between devices  24.3 us (28%)
  Pallas kernels  21.3 us (24%)
  blocking collectives  20.8 us (24%)
  waiting for transfers between devices  20 us (23%)
  between operations  0.93 us (1%)
    pallas_call x8, Pallas kernels, run(): pl.pallas_call(kernel, out_shape=out_shape, in_specs=specs, out_specs=jax...  21.3 us
    all_to_all x1, blocking collectives, column_of_subgrids(): lax.all_to_all(shares, 'facet', 0, 0, axis_index_groups=groups, tiled=True)  20.8 us
    all_to_all x1, waiting for transfers between devices, column_of_subgrids(): lax.all_to_all(spread, 'facet', 0, 0, axis_index_groups=groups, tiled=True)  16.2 us
    all_to_all x1, starting transfers between devices, column_of_subgrids(): lax.all_to_all(spread, 'facet', 0, 0, axis_index_groups=groups, tiled=True)  11.9 us
    ppermute x6, starting transfers between devices, to_stokes(): lax.ppermute(array, 'stokes', [(i, (i - k) % 4) for i in range(4)])  8.03 us
    ppermute x6, waiting for transfers between devices, to_stokes(): lax.ppermute(array, 'stokes', [(i, (i - k) % 4) for i in range(4)])  2.84 us
    ppermute x1, starting transfers between devices, column_of_subgrids(): other = lax.ppermute(mine, 'facet', partner)  2.43 us
    ppermute x1, starting transfers between devices, column_of_subgrids(): other_adj = lax.ppermute(adj, 'facet', partner)  2 us
  transfers between devices with their start and end apart: 9, of which 5 were waited for; matrix products, arithmetic and copies ran while one was open for 0% of the time, Pallas kernels for 10%

profile of v5, /device:TPU:1, one launch (start us, length us, event | category | flops | bytes accessed | tf_op | source)
XLA Modules:
  0.0 87.5 jit_solution(5930367236859783494)
XLA Ops:
  0.6 0.0 copy-start
  0.6 0.0 copy-start.1
  0.7 0.0 copy-start.2
  0.7 0.0 copy-start.8
  0.7 3.3 %shard_map.113 = bf16[32,64,128]{2,1,0:T(8,128)(2,1)} custom-call(bf16[64,16384]{1,0:T(8,128)(2,1)} %bitcast.7, bf16[128,2048]{1,0:T(8,128)(2,1)} %constant.17.clone.column_ref), custom_call_target="tpu_custom_call" | custom-call | flops 1000000000 | bytes 1048576 | tf_op jit(solution)/shard_map/pallas_call | solution.py:386
  4.0 11.9 %all-to-all-start = ((bf16[32,64,128]{2,1,0:T(8,128)(2,1)}), bf16[32,64,128]{2,1,0:T(8,128)(2,1)S(1)}, u32[]{:S(2)}, u32[]{:S(2)}) async-start(bf16[32,64,128]{2,1,0:T(8,128)(2,1)} %shard_map.113), calls=%async_computation | async-start | bytes 1048576 | tf_op jit(solution)/shard_map/all_to_all | solution.py:431
  15.9 0.1 pad_add_fusion.here_ref
  15.9 16.2 %all-to-all-done.mine_ref = bf16[32,64,128]{2,1,0:T(8,128)(2,1)S(1)} async-done(((bf16[32,64,128]{2,1,0:T(8,128)(2,1)}), bf16[32,64,128]{2,1,0:T(8,128)(2,1)S(1)}, u32[]{:S(2)}, u32[]{:S(2)}) %all-to-all-start) | async-done | bytes 524320 | tf_op jit(solution)/shard_map/all_to_all | solution.py:431
  32.1 2.4 %collective-permute-start = (bf16[32,64,128]{2,1,0:T(8,128)(2,1)S(1)}, bf16[32,64,128]{2,1,0:T(8,128)(2,1)S(1)}, u32[]{:S(2)}, u32[]{:S(2)}) collective-permute-start(bf16[32,64,128]{2,1,0:T(8,128)(2,1)S(1)} %all-to-all-done.mine_ref), channel_id=1, source_target_pairs={{0,4},{4,0},{8,12},{12,8},{16,20},{20,16},{24,28},{28,24},{32,36},... | collective-permute-start | bytes 1572872 | tf_op jit(solution)/shard_map/ppermute | solution.py:451
  34.6 0.0 copy-done
  34.6 0.0 copy-done.1
  34.6 0.0 copy-done.2
  34.6 0.0 copy-done.8
  34.6 0.0 copy-start.4
  34.6 0.0 copy-start.6
  34.6 0.0 copy-start.7
  34.6 2.4 %shard_map.115 = (f32[128,128]{1,0:T(8,128)S(1)}, f32[128,128]{1,0:T(8,128)S(1)}, f32[128,128]{1,0:T(8,128)S(1)}, f32[256,128]{1,0:T(8,128)S(1)}, bf16[256,128]{...) custom-call(s32[2]{0:T(128)S(1)} %pad_add_fusion.here_ref, s32[3,2,8192]{2,1,0:T(2,128)S(1)} %copy-done, ...), custom_call_target="tpu_custom_call" | custom-call | flops 10000000000 | bytes 1048576 | tf_op jit(solution)/shard_map/pallas_call | solution.py:386
  37.0 1.4 %collective-permute-start.6 = (bf16[256,128]{1,0:T(8,128)(2,1)S(1)}, bf16[256,128]{1,0:T(8,128)(2,1)S(1)}, u32[]{:S(2)}, u32[]{:S(2)}) collective-permute-start(bf16[256,128]{1,0:T(8,128)(2,1)S(1)} %get-tuple-element.12), channel_id=1, source_target_pairs={{0,1},{1,2},{2,3},{3,0},{4,5},{5,6},{6,7},{7,4},{8,9},{9,10},{10,1... | collective-permute-start | bytes 196616 | tf_op jit(solution)/shard_map/ppermute | solution.py:417
  38.4 2.6 %collective-permute-start.5 = (bf16[256,128]{1,0:T(8,128)(2,1)S(1)}, bf16[256,128]{1,0:T(8,128)(2,1)S(1)}, u32[]{:S(2)}, u32[]{:S(2)}) collective-permute-start(bf16[256,128]{1,0:T(8,128)(2,1)S(1)} %get-tuple-element.12), channel_id=1, source_target_pairs={{0,2},{1,3},{2,0},{3,1},{4,6},{5,7},{6,4},{7,5},{8,10},{9,11},{10,... | collective-permute-start | bytes 196616 | tf_op jit(solution)/shard_map/ppermute | solution.py:417
  41.0 1.1 %collective-permute-start.4 = (bf16[256,128]{1,0:T(8,128)(2,1)S(1)}, bf16[256,128]{1,0:T(8,128)(2,1)S(1)}, u32[]{:S(2)}, u32[]{:S(2)}) collective-permute-start(bf16[256,128]{1,0:T(8,128)(2,1)S(1)} %get-tuple-element.12), channel_id=1, source_target_pairs={{0,3},{1,0},{2,1},{3,2},{4,7},{5,4},{6,5},{7,6},{8,11},{9,8},{10,9... | collective-permute-start | bytes 196616 | tf_op jit(solution)/shard_map/ppermute | solution.py:417
  42.1 0.0 copy-done.4
  42.1 0.0 copy-done.6
  42.1 0.0 copy-done.7
  42.1 2.1 %shard_map.114.start_ref = f32[256,256]{1,0:T(8,128)S(1)} custom-call(s32[2]{0:T(128)S(1)} %pad_add_fusion.here_ref, s32[128]{0:T(128)S(1)} %copy-done.4, bf16[32,64,128]{2,1,0:T(8,128)(2,1)S(1)} %all-to-all-done.mine_ref, f32[128,256]{1,0:T(8,128)S(1)} %copy-done.7, f32[128,256]{1,0:T(8,128)S(1)} %copy-done.6), custom_call_target="tpu_custom_call" | custom-call | flops 1000000000 | bytes 1048576 | tf_op jit(solution)/shard_map/pallas_call | solution.py:386
  44.2 0.0 collective-permute-done.other_ref
  44.2 4.5 %shard_map.116.a_ref = bf16[256,128]{1,0:T(8,128)(2,1)S(1)} custom-call(s32[2]{0:T(128)S(1)} %pad_add_fusion.here_ref, s32[128]{0:T(128)S(1)} %copy-done.4, f32[256,256]{1,0:T(8,128)S(1)} %shard_map.114.start_ref, bf16[32,64,128]{2,1,0:T(8,128)(2,1)S(1)} %collective-permute-done.other_ref, f32[128,256]{1,0:T(8,128)S(1)} %copy-done.7, ...), custom_call_target="tpu_custom_call" | custom-call | flops 1000000000 | bytes 1048576 | tf_op jit(solution)/shard_map/pallas_call | solution.py:386
  48.7 0.0 copy-start.3
  48.7 0.5 collective-permute-start.3
  49.2 0.8 collective-permute-start.2
  50.0 0.0 collective-permute-done.6.d_ref
  50.0 1.7 %collective-permute-start.1 = (bf16[256,128]{1,0:T(8,128)(2,1)S(1)}, bf16[256,128]{1,0:T(8,128)(2,1)S(1)}, u32[]{:S(2)}, u32[]{:S(2)}) collective-permute-start(bf16[256,128]{1,0:T(8,128)(2,1)S(1)} %shard_map.116.a_ref), channel_id=1, source_target_pairs={{0,3},{1,0},{2,1},{3,2},{4,7},{5,4},{6,5},{7,6},{8,11},{9,8},{10,9... | collective-permute-start | bytes 196616 | tf_op jit(solution)/shard_map/ppermute | solution.py:417
  51.7 0.0 collective-permute-done.5.c_ref
  51.7 0.0 collective-permute-done.4.b_ref
  51.7 0.2 shard_map.117.turned_ref
  51.9 1.3 %collective-permute-done.3.d_ref = bf16[256,128]{1,0:T(8,128)(2,1)S(1)} collective-permute-done((bf16[256,128]{1,0:T(8,128)(2,1)S(1)}, bf16[256,128]{1,0:T(8,128)(2,1)S(1)}, u32[]{:S(2)}, u32[]{:S(2)}) %collective-permute-start.3) | collective-permute-done | bytes 65568 | tf_op jit(solution)/shard_map/ppermute | solution.py:417
  53.1 0.7 collective-permute-done.2.c_ref
  53.8 0.9 collective-permute-done.1.b_ref
  54.7 0.0 copy-done.3
  54.7 3.6 %shard_map.118 = (f32[2,2,8192]{2,1,0:T(2,128)}, bf16[256,256]{1,0:T(8,128)(2,1)S(1)}) custom-call(s32[2]{0:T(128)S(1)} %copy-done.3, bf16[256,128]{1,0:T(8,128)(2,1)S(1)} %shard_map.116.a_ref, bf16[256,128]{1,0:T(8,128)(2,1)S(1)} %collective-permute-done.1.b_ref, bf16[256,128]{1,0:T(8,128)(2,1)S(1)} %collective-permute-done.2.c_ref, ...), custom_call_target="tpu_custom_call" | custom-call | flops 1000000000 | bytes 1048576 | tf_op jit(solution)/shard_map/pallas_call | solution.py:386
  58.4 0.0 copy-start.5
  58.4 2.0 %collective-permute-start.7 = (bf16[256,256]{1,0:T(8,128)(2,1)S(1)}, bf16[256,256]{1,0:T(8,128)(2,1)S(1)}, u32[]{:S(2)}, u32[]{:S(2)}) collective-permute-start(bf16[256,256]{1,0:T(8,128)(2,1)S(1)} %get-tuple-element.16.mine_ref), channel_id=1, source_target_pairs={{0,4},{4,0},{8,12},{12,8},{16,20},{20,16},{24,28},{28,24},{32,36},... | collective-permute-start | bytes 393224 | tf_op jit(solution)/shard_map/ppermute | solution.py:478
  60.4 1.0 %collective-permute-done.7.other_ref = bf16[256,256]{1,0:T(8,128)(2,1)S(1)} collective-permute-done((bf16[256,256]{1,0:T(8,128)(2,1)S(1)}, bf16[256,256]{1,0:T(8,128)(2,1)S(1)}, u32[]{:S(2)}, u32[]{:S(2)}) %collective-permute-start.7) | collective-permute-done | bytes 131104 | tf_op jit(solution)/shard_map/ppermute | solution.py:478
  61.3 3.3 %shard_map.119 = bf16[32,64,128]{2,1,0:T(8,128)(2,1)S(1)} custom-call(s32[2]{0:T(128)S(1)} %pad_add_fusion.here_ref, s32[128]{0:T(128)S(1)} %copy-done.4, bf16[256,256]{1,0:T(8,128)(2,1)S(1)} %get-tuple-element.16.mine_ref, bf16[256,256]{1,0:T(8,128)(2,1)S(1)} %collective-permute-done.7.other_ref, f32[128,256]{1,0:T(8,128)S(1)} %copy-done.7, ...), custom_call_target="tpu_custom_call" | custom-call | flops 1000000000 | bytes 1048576 | tf_op jit(solution)/shard_map/pallas_call | solution.py:386
  64.6 20.8 %all_to_all.10.shares_ref = bf16[32,64,128]{2,1,0:T(8,128)(2,1)S(1)} all-to-all(bf16[32,64,128]{2,1,0:T(8,128)(2,1)S(1)} %shard_map.119), channel_id=1, replica_groups={{0,8,16,24,32,40,48,56,64,72,80,88,96,104,112,120,128,136,144,152,160,1..., dimensions={0} | all-to-all | bytes 1048576 | tf_op jit(solution)/shard_map/all_to_all | solution.py:482
  85.4 0.0 copy-done.5
  85.4 1.9 %shard_map.120 = bf16[64,16384]{1,0:T(8,128)(2,1)} custom-call(bf16[32,64,128]{2,1,0:T(8,128)(2,1)S(1)} %all_to_all.10.shares_ref, bf16[128,2048]{1,0:T(8,128)(2,1)S(1)} %copy-done.5), custom_call_target="tpu_custom_call" | custom-call | flops 1000000000 | bytes 1048576 | tf_op jit(solution)/shard_map/pallas_call | solution.py:386
Async XLA Ops:
  0.6 33.9 %copy-start = (s32[3,2,8192]{2,1,0:T(2,128)S(1)}, s32[3,2,8192]{2,1,0:T(2,128)}, u32[]{:S(2)}) copy-start(s32[3,2,8192]{2,1,0:T(2,128)} %cells_ref.5) | copy-start | bytes 589828
  0.6 33.9 %copy-start.1 = (f32[1,2,2,8192]{3,2,1,0:T(2,128)S(1)}, f32[1,2,2,8192]{3,2,1,0:T(2,128)}, u32[]{:S(2)}) copy-start(f32[1,2,2,8192]{3,2,1,0:T(2,128)} %param.15) | copy-start | bytes 393220
  0.7 33.9 %copy-start.2 = (f32[4,4,2,64]{3,2,1,0:T(2,128)S(1)}, f32[4,4,2,64]{3,2,1,0:T(2,128)}, u32[]{:S(2)}) copy-start(f32[4,4,2,64]{3,2,1,0:T(2,128)} %mueller_ref.1) | copy-start | bytes 24580
  0.7 33.9 %copy-start.8 = (bf16[64,256]{1,0:T(8,128)(2,1)S(1)}, bf16[64,256]{1,0:T(8,128)(2,1)}, u32[]{:S(2)}) copy-start(bf16[64,256]{1,0:T(8,128)(2,1)} %constant.18.clone.kernel_ref) | copy-start | bytes 98308
  4.0 28.2 %all-to-all-start = ((bf16[32,64,128]{2,1,0:T(8,128)(2,1)}), bf16[32,64,128]{2,1,0:T(8,128)(2,1)S(1)}, u32[]{:S(2)}, u32[]{:S(2)}) async-start(bf16[32,64,128]{2,1,0:T(8,128)(2,1)} %shard_map.113), calls=%async_computation | async-start | bytes 1048576 | tf_op jit(solution)/shard_map/all_to_all | solution.py:431
  32.1 12.0 %collective-permute-start = (bf16[32,64,128]{2,1,0:T(8,128)(2,1)S(1)}, bf16[32,64,128]{2,1,0:T(8,128)(2,1)S(1)}, u32[]{:S(2)}, u32[]{:S(2)}) collective-permute-start(bf16[32,64,128]{2,1,0:T(8,128)(2,1)S(1)} %all-to-all-done.mine_ref), channel_id=1, source_target_pairs={{0,4},{4,0},{8,12},{12,8},{16,20},{20,16},{24,28},{28,24},{32,36},... | collective-permute-start | bytes 1572872 | tf_op jit(solution)/shard_map/ppermute | solution.py:451
  34.6 7.5 %copy-start.4 = (s32[128]{0:T(128)S(1)}, s32[128]{0:T(128)}, u32[]{:S(2)}) copy-start(s32[128]{0:T(128)} %sub_ref.5) | copy-start | bytes 1540
  34.6 7.5 %copy-start.6 = (f32[128,256]{1,0:T(8,128)S(1)}, f32[128,256]{1,0:T(8,128)}, u32[]{:S(2)}) copy-start(f32[128,256]{1,0:T(8,128)} %constant.20.clone.lift_s_ref) | copy-start | bytes 393220
  34.6 7.5 %copy-start.7 = (f32[128,256]{1,0:T(8,128)S(1)}, f32[128,256]{1,0:T(8,128)}, u32[]{:S(2)}) copy-start(f32[128,256]{1,0:T(8,128)} %constant.19.clone.lift_ref) | copy-start | bytes 393220
  37.0 13.0 %collective-permute-start.6 = (bf16[256,128]{1,0:T(8,128)(2,1)S(1)}, bf16[256,128]{1,0:T(8,128)(2,1)S(1)}, u32[]{:S(2)}, u32[]{:S(2)}) collective-permute-start(bf16[256,128]{1,0:T(8,128)(2,1)S(1)} %get-tuple-element.12), channel_id=1, source_target_pairs={{0,1},{1,2},{2,3},{3,0},{4,5},{5,6},{6,7},{7,4},{8,9},{9,10},{10,1... | collective-permute-start | bytes 196616 | tf_op jit(solution)/shard_map/ppermute | solution.py:417
  38.4 13.3 %collective-permute-start.5 = (bf16[256,128]{1,0:T(8,128)(2,1)S(1)}, bf16[256,128]{1,0:T(8,128)(2,1)S(1)}, u32[]{:S(2)}, u32[]{:S(2)}) collective-permute-start(bf16[256,128]{1,0:T(8,128)(2,1)S(1)} %get-tuple-element.12), channel_id=1, source_target_pairs={{0,2},{1,3},{2,0},{3,1},{4,6},{5,7},{6,4},{7,5},{8,10},{9,11},{10,... | collective-permute-start | bytes 196616 | tf_op jit(solution)/shard_map/ppermute | solution.py:417
  41.0 10.7 %collective-permute-start.4 = (bf16[256,128]{1,0:T(8,128)(2,1)S(1)}, bf16[256,128]{1,0:T(8,128)(2,1)S(1)}, u32[]{:S(2)}, u32[]{:S(2)}) collective-permute-start(bf16[256,128]{1,0:T(8,128)(2,1)S(1)} %get-tuple-element.12), channel_id=1, source_target_pairs={{0,3},{1,0},{2,1},{3,2},{4,7},{5,4},{6,5},{7,6},{8,11},{9,8},{10,9... | collective-permute-start | bytes 196616 | tf_op jit(solution)/shard_map/ppermute | solution.py:417
  48.7 6.0 %copy-start.3 = (s32[2]{0:T(128)S(1)}, s32[2]{0:T(128)}, u32[]{:S(2)}) copy-start(s32[2]{0:T(128)} %counts_ref.1) | copy-start | bytes 28
  48.7 4.4 %collective-permute-start.3 = (bf16[256,128]{1,0:T(8,128)(2,1)S(1)}, bf16[256,128]{1,0:T(8,128)(2,1)S(1)}, u32[]{:S(2)}, u32[]{:S(2)}) collective-permute-start(bf16[256,128]{1,0:T(8,128)(2,1)S(1)} %shard_map.116.a_ref), channel_id=1, source_target_pairs={{0,1},{1,2},{2,3},{3,0},{4,5},{5,6},{6,7},{7,4},{8,9},{9,10},{10,1... | collective-permute-start | bytes 196616 | tf_op jit(solution)/shard_map/ppermute | solution.py:417
  49.2 4.6 %collective-permute-start.2 = (bf16[256,128]{1,0:T(8,128)(2,1)S(1)}, bf16[256,128]{1,0:T(8,128)(2,1)S(1)}, u32[]{:S(2)}, u32[]{:S(2)}) collective-permute-start(bf16[256,128]{1,0:T(8,128)(2,1)S(1)} %shard_map.116.a_ref), channel_id=1, source_target_pairs={{0,2},{1,3},{2,0},{3,1},{4,6},{5,7},{6,4},{7,5},{8,10},{9,11},{10,... | collective-permute-start | bytes 196616 | tf_op jit(solution)/shard_map/ppermute | solution.py:417
  50.0 4.7 %collective-permute-start.1 = (bf16[256,128]{1,0:T(8,128)(2,1)S(1)}, bf16[256,128]{1,0:T(8,128)(2,1)S(1)}, u32[]{:S(2)}, u32[]{:S(2)}) collective-permute-start(bf16[256,128]{1,0:T(8,128)(2,1)S(1)} %shard_map.116.a_ref), channel_id=1, source_target_pairs={{0,3},{1,0},{2,1},{3,2},{4,7},{5,4},{6,5},{7,6},{8,11},{9,8},{10,9... | collective-permute-start | bytes 196616 | tf_op jit(solution)/shard_map/ppermute | solution.py:417
  58.4 27.0 %copy-start.5 = (bf16[128,2048]{1,0:T(8,128)(2,1)S(1)}, bf16[128,2048]{1,0:T(8,128)(2,1)}, u32[]{:S(2)}) copy-start(bf16[128,2048]{1,0:T(8,128)(2,1)} %constant.17.clone.column_ref) | copy-start | bytes 1572868
  58.4 3.0 %collective-permute-start.7 = (bf16[256,256]{1,0:T(8,128)(2,1)S(1)}, bf16[256,256]{1,0:T(8,128)(2,1)S(1)}, u32[]{:S(2)}, u32[]{:S(2)}) collective-permute-start(bf16[256,256]{1,0:T(8,128)(2,1)S(1)} %get-tuple-element.16.mine_ref), channel_id=1, source_target_pairs={{0,4},{4,0},{8,12},{12,8},{16,20},{20,16},{24,28},{28,24},{32,36},... | collective-permute-start | bytes 393224 | tf_op jit(solution)/shard_map/ppermute | solution.py:478

commit v6 on v4

--- a/solution.py
+++ b/solution.py
@@ -156,7 +156,7 @@
         lax.fori_loop(0, VISITS // CHUNK, chunk, 0, unroll=2)
 
 
-def phases(offsets, parity, cos_ref, sin_ref, fcos_ref, fsin_ref):
+def row_phases(offsets, parity, cos_ref, sin_ref):
     step = lax.broadcasted_iota(jnp.int32, (32, 2 * ROWS), 0)
     lane = lax.broadcasted_iota(jnp.int32, (32, 2 * ROWS), 1) & (ROWS - 1)
     rows = (2 * step + parity) * ROWS + lane
@@ -164,6 +164,9 @@
         cosine, sine = turn((rows * offset) & (TOTAL - 1), TOTAL)
         cos_ref[32 * i : 32 * i + 32, :] = cosine
         sin_ref[32 * i : 32 * i + 32, :] = sine
+
+
+def facet_phases(parity, fcos_ref, fsin_ref):
     step = lax.broadcasted_iota(jnp.int32, (32, G), 0)
     lane = lax.broadcasted_iota(jnp.int32, (32, G), 1)
     cosine, sine = turn(((2 * step + parity) * lane) & (FACETS - 1), FACETS)
@@ -180,7 +183,9 @@
     here = here_ref[0]
     core = here & 1
     offsets = [sub_ref[2 * here + sub] for sub in range(2)]
-    phases(offsets, core if side == 0 else 1 - core, *tables)
+    parity = core if side == 0 else 1 - core
+    row_phases(offsets, parity, cos_ref, sin_ref)
+    facet_phases(parity, fcos_ref, fsin_ref)
     sign = half_sign()
 
     def group(i, carry):
@@ -266,7 +271,7 @@
 
 def residual_kernel(
     counts_ref, a_ref, b_ref, c_ref, d_ref, seen_ref, turned_ref, mix_ref, cos_ref, sin_ref, cells_ref,
-    weights_ref, resid_ref, out_ref, back_ref,
+    weights_ref, final_ref, out_ref, back_ref, resid_ref, sem,
 ):
     planes = (a_ref, b_ref, c_ref, d_ref)
     block = lax.broadcasted_iota(jnp.int32, (MAXB, BLOCK), 0)
@@ -281,10 +286,16 @@
             return sum(mix_ref[here, first + t : first + t + 1] * s for t, s in enumerate(samples))
 
         m_re, m_im = mixed(0, s_re), mixed(0, s_im)
-        resid_ref[re, :] = jnp.where(live, seen_ref[re, :] - (m_re * cosine + m_im * sine), 0.0)
-        resid_ref[im, :] = jnp.where(live, seen_ref[im, :] - (m_im * cosine - m_re * sine), 0.0)
+        left_re = jnp.where(live, seen_ref[re, :] - (m_re * cosine + m_im * sine), 0.0)
+        left_im = jnp.where(live, seen_ref[im, :] - (m_im * cosine - m_re * sine), 0.0)
+        for b in range(MAXB):
+            lanes = slice(b * BLOCK, (b + 1) * BLOCK)
+            resid_ref[sub, 0:1, lanes] = left_re[b : b + 1, :]
+            resid_ref[sub, 1:2, lanes] = left_im[b : b + 1, :]
         back_ref[re, :] = jnp.where(live, turned_ref[re, :] - mixed(16, s_re), 0.0)
         back_ref[im, :] = jnp.where(live, turned_ref[im, :] - mixed(16, s_im), 0.0)
+    finish = pltpu.make_async_copy(resid_ref, final_ref, sem)
+    finish.start()
     per = CHUNK // BLOCK
     for sub in range(2):
 
@@ -303,27 +314,30 @@
 
         total = lax.fori_loop(0, VISITS // CHUNK, chunk, jnp.zeros((G, 2 * K), f32), unroll=2)
         out_ref[sub * 2 * K : (sub + 1) * 2 * K, :] = jnp.transpose(total).astype(bf16)
+    finish.wait()
+
+
+def table_kernel(here_ref, lift_ref, lift_s_ref, out_ref, fcos_ref, fsin_ref):
+    facet_phases(here_ref[0] & 1, fcos_ref, fsin_ref)
+    for q in range(32):
+        out_ref[q * 2 * ROWS : (q + 1) * 2 * ROWS, :] = facet_lift(
+            fcos_ref[q : q + 1, :], fsin_ref[q : q + 1, :], lift_ref, lift_s_ref
+        )
 
 
 def share_kernel(
-    here_ref, sub_ref, mine_ref, other_ref, lift_ref, lift_s_ref, out_ref, *tables
+    here_ref, sub_ref, mine_ref, other_ref, table_ref, out_ref, cos_ref, sin_ref
 ):
-    cos_ref, sin_ref, fcos_ref, fsin_ref = tables
     sign = half_sign()
     here = here_ref[0]
     core = here & 1
     firsts = (2 * here, 2 * (here + 1 - 2 * core))
-    phases([sub_ref[first + sub] for first in firsts for sub in range(2)], core, *tables)
+    row_phases([sub_ref[first + sub] for first in firsts for sub in range(2)], core, cos_ref, sin_ref)
     left = jnp.concatenate([mine_ref[...], other_ref[...]], 0)
 
     def pair(i, carry):
-        rights = []
-        for e in range(2):
-            q = 2 * i + e
-            rights.append(
-                facet_lift(fcos_ref[pl.ds(q, 1), :], fsin_ref[pl.ds(q, 1), :], lift_ref, lift_s_ref)
-            )
-        product = nt_dot(left, jnp.concatenate(rights, 0))
+        at = pl.ds(pl.multiple_of(i * 4 * ROWS, 4 * ROWS), 4 * ROWS)
+        product = nt_dot(left, table_ref[at, :])
         for e in range(2):
             q = 2 * i + e
             total = jnp.zeros((K, 2 * ROWS), f32)
@@ -354,7 +368,7 @@
         out_ref[:, L + turn * PERIOD : L + (turn + 1) * PERIOD] = image[ROWS:]
 
 
-def call(kernel, out_shape, scratch=(), smem=0, limit=16, flops=10**9, hbm=False):
+def call(kernel, out_shape, scratch=(), smem=0, limit=16, flops=10**9, hbm=False, hbm_first=False):
     vmem = pl.BlockSpec(memory_space=pltpu.VMEM)
 
     def run(*args):
@@ -364,7 +378,9 @@
             kernel,
             out_shape=out_shape,
             in_specs=specs,
-            out_specs=jax.tree.map(lambda _: vmem, out_shape),
+            out_specs=(pl.BlockSpec(memory_space=pltpu.HBM), vmem)
+            if hbm_first
+            else jax.tree.map(lambda _: vmem, out_shape),
             scratch_shapes=list(scratch),
             cost_estimate=pl.CostEstimate(flops=flops, bytes_accessed=2**20, transcendentals=0),
             compiler_params=pltpu.CompilerParams(vmem_limit_bytes=limit * 2**20),
@@ -446,19 +462,27 @@
         + scratch(2),
         smem=2,
     )(position, sub_u, rows, other, lift_t, lift_s, uvw, weights)
+    table = call(table_kernel, shape((64 * ROWS, G), bf16), scratch(0)[2:], smem=1)(
+        position, lift_t, lift_s
+    )
     resid, adj = call(
         residual_kernel,
-        (shape((4 * MAXB, BLOCK), f32), shape((4 * K, G), bf16)),
-        (pltpu.VMEM((4 * MAXB, BLOCK), f32),),
+        (shape((2, 2, VISITS), f32), shape((4 * K, G), bf16)),
+        (
+            pltpu.VMEM((4 * MAXB, BLOCK), f32),
+            pltpu.VMEM((2, 2, VISITS), f32),
+            pltpu.SemaphoreType.DMA(()),
+        ),
         smem=1,
+        hbm_first=True,
     )(counts, *to_stokes(samples), seen, turned, mix, vcos, vsin, uvw, weights)
     other_adj = lax.ppermute(adj, "facet", partner)
-    shares = call(share_kernel, shape((32, K, 2 * ROWS), bf16), scratch(4), smem=2)(
-        position, sub_u, adj, other_adj, lift_t, lift_s
+    shares = call(share_kernel, shape((32, K, 2 * ROWS), bf16), scratch(4)[:2], smem=2)(
+        position, sub_u, adj, other_adj, table
     )
     shares = lax.all_to_all(shares, "facet", 0, 0, axis_index_groups=groups, tiled=True)
     image = call(image_kernel, shape((ROWS, 2 * L), bf16))(shares, column)
-    return (image[None], resid.reshape(1, 2, 2, VISITS))
+    return (image[None], resid[None])
 
 
 def solution(mesh):

time: 88.1 us -> 88.8 us (level)
  blocking collectives: 0 us -> 20.9 us
  waiting for transfers between devices: 35.9 us -> 21.2 us
  starting transfers between devices: 28.8 us -> 23.5 us
  Pallas kernels: 21 us -> 22.1 us
    all_to_all x0 -> x1, blocking collectives: none -> 20.9 us  [column_of_subgrids(): lax.all_to_all(shares, 'facet', 0, 0, axis_index_groups=groups, tiled=True)]
    all_to_all x1 -> x0, waiting for transfers between devices: 15.9 us -> none  [column_of_subgrids(): lax.all_to_all(shares, 'facet', 0, 0, axis_index_groups=groups, tiled=True)]
    all_to_all x1 -> x0, starting transfers between devices: 4.39 us -> none  [column_of_subgrids(): lax.all_to_all(shares, 'facet', 0, 0, axis_index_groups=groups, tiled=True)]
    ppermute x6, waiting for transfers between devices: 2.84 us -> 4.94 us  [to_stokes(): lax.ppermute(array, 'stokes', [(i, (i - k) % 4) for i in range(4)])]
    pallas_call x8 -> x9, Pallas kernels: 21 us -> 22.1 us  [run(): pl.pallas_call(kernel, out_shape=out_shape, in_specs=specs, out_specs=(pl...]
    ppermute x1, waiting for transfers between devices: 0.99 us -> 0.01 us  [column_of_subgrids(): other_adj = lax.ppermute(adj, 'facet', partner)]
  transfers between devices with their start and end apart: 10 -> 9, of which waited for: 6 -> 3; matrix products, arithmetic and copies ran while one was open for 1% -> 0% of each run, Pallas kernels for 10% -> 12%
where the time goes in v6:
time: 88.8 us; the launch traced here: 88.5 us
  starting transfers between devices  23.5 us (26%)
  Pallas kernels  22.1 us (25%)
  waiting for transfers between devices  21.2 us (24%)
  blocking collectives  20.9 us (24%)
    pallas_call x9, Pallas kernels, run(): pl.pallas_call(kernel, out_shape=out_shape, in_specs=specs, out_specs=(pl...  22.1 us
    all_to_all x1, blocking collectives, column_of_subgrids(): lax.all_to_all(shares, 'facet', 0, 0, axis_index_groups=groups, tiled=True)  20.9 us
    all_to_all x1, waiting for transfers between devices, column_of_subgrids(): lax.all_to_all(spread, 'facet', 0, 0, axis_index_groups=groups, tiled=True)  16.2 us
    all_to_all x1, starting transfers between devices, column_of_subgrids(): lax.all_to_all(spread, 'facet', 0, 0, axis_index_groups=groups, tiled=True)  11.9 us
    ppermute x6, starting transfers between devices, to_stokes(): lax.ppermute(array, 'stokes', [(i, (i - k) % 4) for i in range(4)])  7.31 us
    ppermute x6, waiting for transfers between devices, to_stokes(): lax.ppermute(array, 'stokes', [(i, (i - k) % 4) for i in range(4)])  4.94 us
    ppermute x1, starting transfers between devices, column_of_subgrids(): other = lax.ppermute(mine, 'facet', partner)  2.43 us
    ppermute x1, starting transfers between devices, column_of_subgrids(): other_adj = lax.ppermute(adj, 'facet', partner)  1.86 us
  transfers between devices with their start and end apart: 9, of which 3 were waited for; matrix products, arithmetic and copies ran while one was open for 0% of the time, Pallas kernels for 12%

profile of v6, /device:TPU:1, one launch (start us, length us, event | category | flops | bytes accessed | tf_op | source)
XLA Modules:
  0.0 88.5 jit_solution(5019256689570760453)
XLA Ops:
  0.6 0.0 copy-start
  0.6 0.0 copy-start.1
  0.7 0.0 copy-start.2
  0.7 0.0 copy-start.8
  0.7 3.0 %shard_map.113 = bf16[32,64,128]{2,1,0:T(8,128)(2,1)} custom-call(bf16[64,16384]{1,0:T(8,128)(2,1)} %bitcast.7, bf16[128,2048]{1,0:T(8,128)(2,1)} %constant.17.clone.column_ref), custom_call_target="tpu_custom_call" | custom-call | flops 1000000000 | bytes 1048576 | tf_op jit(solution)/shard_map/pallas_call | solution.py:377
  3.7 11.9 %all-to-all-start = ((bf16[32,64,128]{2,1,0:T(8,128)(2,1)}), bf16[32,64,128]{2,1,0:T(8,128)(2,1)S(1)}, u32[]{:S(2)}, u32[]{:S(2)}) async-start(bf16[32,64,128]{2,1,0:T(8,128)(2,1)} %shard_map.113), calls=%async_computation | async-start | bytes 1048576 | tf_op jit(solution)/shard_map/all_to_all | solution.py:424
  15.6 0.1 pad_add_fusion.here_ref
  15.7 16.2 %all-to-all-done.mine_ref = bf16[32,64,128]{2,1,0:T(8,128)(2,1)S(1)} async-done(((bf16[32,64,128]{2,1,0:T(8,128)(2,1)}), bf16[32,64,128]{2,1,0:T(8,128)(2,1)S(1)}, u32[]{:S(2)}, u32[]{:S(2)}) %all-to-all-start) | async-done | bytes 524320 | tf_op jit(solution)/shard_map/all_to_all | solution.py:424
  31.9 2.4 %collective-permute-start = (bf16[32,64,128]{2,1,0:T(8,128)(2,1)S(1)}, bf16[32,64,128]{2,1,0:T(8,128)(2,1)S(1)}, u32[]{:S(2)}, u32[]{:S(2)}) collective-permute-start(bf16[32,64,128]{2,1,0:T(8,128)(2,1)S(1)} %all-to-all-done.mine_ref), channel_id=1, source_target_pairs={{0,4},{4,0},{8,12},{12,8},{16,20},{20,16},{24,28},{28,24},{32,36},... | collective-permute-start | bytes 1572872 | tf_op jit(solution)/shard_map/ppermute | solution.py:444
  34.3 0.0 copy-done
  34.3 0.0 copy-done.1
  34.3 0.0 copy-done.2
  34.3 0.0 copy-done.8
  34.3 0.0 copy-start.4
  34.3 0.0 copy-start.6
  34.3 0.0 copy-start.7
  34.4 2.4 %shard_map.115 = (f32[128,128]{1,0:T(8,128)S(1)}, f32[128,128]{1,0:T(8,128)S(1)}, f32[128,128]{1,0:T(8,128)S(1)}, f32[256,128]{1,0:T(8,128)S(1)}, bf16[256,128]{...) custom-call(s32[2]{0:T(128)S(1)} %pad_add_fusion.here_ref, s32[3,2,8192]{2,1,0:T(2,128)S(1)} %copy-done, ...), custom_call_target="tpu_custom_call" | custom-call | flops 10000000000 | bytes 1048576 | tf_op jit(solution)/shard_map/pallas_call | solution.py:377
  36.8 2.8 %collective-permute-start.4 = (bf16[256,128]{1,0:T(8,128)(2,1)S(1)}, bf16[256,128]{1,0:T(8,128)(2,1)S(1)}, u32[]{:S(2)}, u32[]{:S(2)}) collective-permute-start(bf16[256,128]{1,0:T(8,128)(2,1)S(1)} %get-tuple-element.12), channel_id=1, source_target_pairs={{0,3},{1,0},{2,1},{3,2},{4,7},{5,4},{6,5},{7,6},{8,11},{9,8},{10,9... | collective-permute-start | bytes 196616 | tf_op jit(solution)/shard_map/ppermute | solution.py:410
  39.6 0.4 collective-permute-start.5
  39.9 0.7 collective-permute-start.6
  40.6 0.0 copy-done.4
  40.6 0.0 copy-done.6
  40.6 0.0 copy-done.7
  40.6 2.1 %shard_map.114.start_ref = f32[256,256]{1,0:T(8,128)S(1)} custom-call(s32[2]{0:T(128)S(1)} %pad_add_fusion.here_ref, s32[128]{0:T(128)S(1)} %copy-done.4, bf16[32,64,128]{2,1,0:T(8,128)(2,1)S(1)} %all-to-all-done.mine_ref, f32[128,256]{1,0:T(8,128)S(1)} %copy-done.6, f32[128,256]{1,0:T(8,128)S(1)} %copy-done.7), custom_call_target="tpu_custom_call" | custom-call | flops 1000000000 | bytes 1048576 | tf_op jit(solution)/shard_map/pallas_call | solution.py:377
  42.7 0.0 collective-permute-done.other_ref
  42.7 4.5 %shard_map.116.a_ref = bf16[256,128]{1,0:T(8,128)(2,1)S(1)} custom-call(s32[2]{0:T(128)S(1)} %pad_add_fusion.here_ref, s32[128]{0:T(128)S(1)} %copy-done.4, f32[256,256]{1,0:T(8,128)S(1)} %shard_map.114.start_ref, bf16[32,64,128]{2,1,0:T(8,128)(2,1)S(1)} %collective-permute-done.other_ref, f32[128,256]{1,0:T(8,128)S(1)} %copy-done.6, ...), custom_call_target="tpu_custom_call" | custom-call | flops 1000000000 | bytes 1048576 | tf_op jit(solution)/shard_map/pallas_call | solution.py:377
  47.3 0.0 copy-start.3
  47.3 2.1 %collective-permute-start.1 = (bf16[256,128]{1,0:T(8,128)(2,1)S(1)}, bf16[256,128]{1,0:T(8,128)(2,1)S(1)}, u32[]{:S(2)}, u32[]{:S(2)}) collective-permute-start(bf16[256,128]{1,0:T(8,128)(2,1)S(1)} %shard_map.116.a_ref), channel_id=1, source_target_pairs={{0,3},{1,0},{2,1},{3,2},{4,7},{5,4},{6,5},{7,6},{8,11},{9,8},{10,9... | collective-permute-start | bytes 196616 | tf_op jit(solution)/shard_map/ppermute | solution.py:410
  49.4 1.4 %collective-permute-start.2 = (bf16[256,128]{1,0:T(8,128)(2,1)S(1)}, bf16[256,128]{1,0:T(8,128)(2,1)S(1)}, u32[]{:S(2)}, u32[]{:S(2)}) collective-permute-start(bf16[256,128]{1,0:T(8,128)(2,1)S(1)} %shard_map.116.a_ref), channel_id=1, source_target_pairs={{0,2},{1,3},{2,0},{3,1},{4,6},{5,7},{6,4},{7,5},{8,10},{9,11},{10,... | collective-permute-start | bytes 196616 | tf_op jit(solution)/shard_map/ppermute | solution.py:410
  50.7 0.0 collective-permute-done.4.b_ref
  50.7 0.0 collective-permute-start.3
  50.7 0.0 collective-permute-done.5.c_ref
  50.8 0.0 collective-permute-done.6.d_ref
  50.8 0.2 shard_map.117.turned_ref
  50.9 0.0 collective-permute-done.1.b_ref
  50.9 3.0 %collective-permute-done.2.c_ref = bf16[256,128]{1,0:T(8,128)(2,1)S(1)} collective-permute-done((bf16[256,128]{1,0:T(8,128)(2,1)S(1)}, bf16[256,128]{1,0:T(8,128)(2,1)S(1)}, u32[]{:S(2)}, u32[]{:S(2)}) %collective-permute-start.2) | collective-permute-done | bytes 65568 | tf_op jit(solution)/shard_map/ppermute | solution.py:410
  54.0 1.9 %collective-permute-done.3.d_ref = bf16[256,128]{1,0:T(8,128)(2,1)S(1)} collective-permute-done((bf16[256,128]{1,0:T(8,128)(2,1)S(1)}, bf16[256,128]{1,0:T(8,128)(2,1)S(1)}, u32[]{:S(2)}, u32[]{:S(2)}) %collective-permute-start.3) | collective-permute-done | bytes 65568 | tf_op jit(solution)/shard_map/ppermute | solution.py:410
  55.9 0.0 copy-done.3
  55.9 3.6 %shard_map.118 = (f32[2,2,8192]{2,1,0:T(2,128)}, bf16[256,256]{1,0:T(8,128)(2,1)S(1)}) custom-call(s32[2]{0:T(128)S(1)} %copy-done.3, bf16[256,128]{1,0:T(8,128)(2,1)S(1)} %shard_map.116.a_ref, bf16[256,128]{1,0:T(8,128)(2,1)S(1)} %collective-permute-done.1.b_ref, bf16[256,128]{1,0:T(8,128)(2,1)S(1)} %collective-permute-done.2.c_ref, ...), custom_call_target="tpu_custom_call" | custom-call | flops 1000000000 | bytes 1048576 | tf_op jit(solution)/shard_map/pallas_call | solution.py:377
  59.5 1.9 %collective-permute-start.7 = (bf16[256,256]{1,0:T(8,128)(2,1)S(1)}, bf16[256,256]{1,0:T(8,128)(2,1)S(1)}, u32[]{:S(2)}, u32[]{:S(2)}) collective-permute-start(bf16[256,256]{1,0:T(8,128)(2,1)S(1)} %get-tuple-element.16.mine_ref), channel_id=1, source_target_pairs={{0,4},{4,0},{8,12},{12,8},{16,20},{20,16},{24,28},{28,24},{32,36},... | collective-permute-start | bytes 393224 | tf_op jit(solution)/shard_map/ppermute | solution.py:479
  61.4 1.3 %shard_map.119.table_ref = bf16[4096,256]{1,0:T(8,128)(2,1)S(1)} custom-call(s32[2]{0:T(128)S(1)} %pad_add_fusion.here_ref, f32[128,256]{1,0:T(8,128)S(1)} %copy-done.6, f32[128,256]{1,0:T(8,128)S(1)} %copy-done.7), custom_call_target="tpu_custom_call" | custom-call | flops 1000000000 | bytes 1048576 | tf_op jit(solution)/shard_map/pallas_call | solution.py:377
  62.7 0.0 copy-start.5
  62.7 0.0 collective-permute-done.7.other_ref
  62.7 3.1 %shard_map.120 = bf16[32,64,128]{2,1,0:T(8,128)(2,1)S(1)} custom-call(s32[2]{0:T(128)S(1)} %pad_add_fusion.here_ref, s32[128]{0:T(128)S(1)} %copy-done.4, bf16[256,256]{1,0:T(8,128)(2,1)S(1)} %get-tuple-element.16.mine_ref, bf16[256,256]{1,0:T(8,128)(2,1)S(1)} %collective-permute-done.7.other_ref, bf16[4096,256]{1,0:T(8,128)(2,1)S(1)} %shard_map.119.table_ref), custom_call_target="tpu_custom_call" | custom-call | flops 1000000000 | bytes 1048576 | tf_op jit(solution)/shard_map/pallas_call | solution.py:377
  65.8 20.9 %all_to_all.10.shares_ref = bf16[32,64,128]{2,1,0:T(8,128)(2,1)S(1)} all-to-all(bf16[32,64,128]{2,1,0:T(8,128)(2,1)S(1)} %shard_map.120), channel_id=1, replica_groups={{0,8,16,24,32,40,48,56,64,72,80,88,96,104,112,120,128,136,144,152,160,1..., dimensions={0} | all-to-all | bytes 1048576 | tf_op jit(solution)/shard_map/all_to_all | solution.py:483
  86.7 0.0 copy-done.5
  86.7 1.8 %shard_map.121 = bf16[64,16384]{1,0:T(8,128)(2,1)} custom-call(bf16[32,64,128]{2,1,0:T(8,128)(2,1)S(1)} %all_to_all.10.shares_ref, bf16[128,2048]{1,0:T(8,128)(2,1)S(1)} %copy-done.5), custom_call_target="tpu_custom_call" | custom-call | flops 1000000000 | bytes 1048576 | tf_op jit(solution)/shard_map/pallas_call | solution.py:377
Async XLA Ops:
  0.6 33.7 %copy-start = (s32[3,2,8192]{2,1,0:T(2,128)S(1)}, s32[3,2,8192]{2,1,0:T(2,128)}, u32[]{:S(2)}) copy-start(s32[3,2,8192]{2,1,0:T(2,128)} %cells_ref.5) | copy-start | bytes 589828
  0.6 33.7 %copy-start.1 = (f32[1,2,2,8192]{3,2,1,0:T(2,128)S(1)}, f32[1,2,2,8192]{3,2,1,0:T(2,128)}, u32[]{:S(2)}) copy-start(f32[1,2,2,8192]{3,2,1,0:T(2,128)} %param.15) | copy-start | bytes 393220
  0.7 33.7 %copy-start.2 = (f32[4,4,2,64]{3,2,1,0:T(2,128)S(1)}, f32[4,4,2,64]{3,2,1,0:T(2,128)}, u32[]{:S(2)}) copy-start(f32[4,4,2,64]{3,2,1,0:T(2,128)} %mueller_ref.1) | copy-start | bytes 24580
  0.7 33.7 %copy-start.8 = (bf16[64,256]{1,0:T(8,128)(2,1)S(1)}, bf16[64,256]{1,0:T(8,128)(2,1)}, u32[]{:S(2)}) copy-start(bf16[64,256]{1,0:T(8,128)(2,1)} %constant.18.clone.kernel_ref) | copy-start | bytes 98308
  3.7 28.2 %all-to-all-start = ((bf16[32,64,128]{2,1,0:T(8,128)(2,1)}), bf16[32,64,128]{2,1,0:T(8,128)(2,1)S(1)}, u32[]{:S(2)}, u32[]{:S(2)}) async-start(bf16[32,64,128]{2,1,0:T(8,128)(2,1)} %shard_map.113), calls=%async_computation | async-start | bytes 1048576 | tf_op jit(solution)/shard_map/all_to_all | solution.py:424
  31.9 10.8 %collective-permute-start = (bf16[32,64,128]{2,1,0:T(8,128)(2,1)S(1)}, bf16[32,64,128]{2,1,0:T(8,128)(2,1)S(1)}, u32[]{:S(2)}, u32[]{:S(2)}) collective-permute-start(bf16[32,64,128]{2,1,0:T(8,128)(2,1)S(1)} %all-to-all-done.mine_ref), channel_id=1, source_target_pairs={{0,4},{4,0},{8,12},{12,8},{16,20},{20,16},{24,28},{28,24},{32,36},... | collective-permute-start | bytes 1572872 | tf_op jit(solution)/shard_map/ppermute | solution.py:444
  34.3 6.3 %copy-start.4 = (s32[128]{0:T(128)S(1)}, s32[128]{0:T(128)}, u32[]{:S(2)}) copy-start(s32[128]{0:T(128)} %sub_ref.5) | copy-start | bytes 1540
  34.3 6.3 %copy-start.6 = (f32[128,256]{1,0:T(8,128)S(1)}, f32[128,256]{1,0:T(8,128)}, u32[]{:S(2)}) copy-start(f32[128,256]{1,0:T(8,128)} %constant.19.clone.lift_ref) | copy-start | bytes 393220
  34.3 6.3 %copy-start.7 = (f32[128,256]{1,0:T(8,128)S(1)}, f32[128,256]{1,0:T(8,128)}, u32[]{:S(2)}) copy-start(f32[128,256]{1,0:T(8,128)} %constant.20.clone.lift_s_ref) | copy-start | bytes 393220
  36.8 14.0 %collective-permute-start.4 = (bf16[256,128]{1,0:T(8,128)(2,1)S(1)}, bf16[256,128]{1,0:T(8,128)(2,1)S(1)}, u32[]{:S(2)}, u32[]{:S(2)}) collective-permute-start(bf16[256,128]{1,0:T(8,128)(2,1)S(1)} %get-tuple-element.12), channel_id=1, source_target_pairs={{0,3},{1,0},{2,1},{3,2},{4,7},{5,4},{6,5},{7,6},{8,11},{9,8},{10,9... | collective-permute-start | bytes 196616 | tf_op jit(solution)/shard_map/ppermute | solution.py:410
  39.6 11.2 %collective-permute-start.5 = (bf16[256,128]{1,0:T(8,128)(2,1)S(1)}, bf16[256,128]{1,0:T(8,128)(2,1)S(1)}, u32[]{:S(2)}, u32[]{:S(2)}) collective-permute-start(bf16[256,128]{1,0:T(8,128)(2,1)S(1)} %get-tuple-element.12), channel_id=1, source_target_pairs={{0,2},{1,3},{2,0},{3,1},{4,6},{5,7},{6,4},{7,5},{8,10},{9,11},{10,... | collective-permute-start | bytes 196616 | tf_op jit(solution)/shard_map/ppermute | solution.py:410
  39.9 10.8 %collective-permute-start.6 = (bf16[256,128]{1,0:T(8,128)(2,1)S(1)}, bf16[256,128]{1,0:T(8,128)(2,1)S(1)}, u32[]{:S(2)}, u32[]{:S(2)}) collective-permute-start(bf16[256,128]{1,0:T(8,128)(2,1)S(1)} %get-tuple-element.12), channel_id=1, source_target_pairs={{0,1},{1,2},{2,3},{3,0},{4,5},{5,6},{6,7},{7,4},{8,9},{9,10},{10,1... | collective-permute-start | bytes 196616 | tf_op jit(solution)/shard_map/ppermute | solution.py:410
  47.3 8.6 %copy-start.3 = (s32[2]{0:T(128)S(1)}, s32[2]{0:T(128)}, u32[]{:S(2)}) copy-start(s32[2]{0:T(128)} %counts_ref.1) | copy-start | bytes 28
  47.3 3.7 %collective-permute-start.1 = (bf16[256,128]{1,0:T(8,128)(2,1)S(1)}, bf16[256,128]{1,0:T(8,128)(2,1)S(1)}, u32[]{:S(2)}, u32[]{:S(2)}) collective-permute-start(bf16[256,128]{1,0:T(8,128)(2,1)S(1)} %shard_map.116.a_ref), channel_id=1, source_target_pairs={{0,3},{1,0},{2,1},{3,2},{4,7},{5,4},{6,5},{7,6},{8,11},{9,8},{10,9... | collective-permute-start | bytes 196616 | tf_op jit(solution)/shard_map/ppermute | solution.py:410
  49.4 4.6 %collective-permute-start.2 = (bf16[256,128]{1,0:T(8,128)(2,1)S(1)}, bf16[256,128]{1,0:T(8,128)(2,1)S(1)}, u32[]{:S(2)}, u32[]{:S(2)}) collective-permute-start(bf16[256,128]{1,0:T(8,128)(2,1)S(1)} %shard_map.116.a_ref), channel_id=1, source_target_pairs={{0,2},{1,3},{2,0},{3,1},{4,6},{5,7},{6,4},{7,5},{8,10},{9,11},{10,... | collective-permute-start | bytes 196616 | tf_op jit(solution)/shard_map/ppermute | solution.py:410
  50.7 5.1 %collective-permute-start.3 = (bf16[256,128]{1,0:T(8,128)(2,1)S(1)}, bf16[256,128]{1,0:T(8,128)(2,1)S(1)}, u32[]{:S(2)}, u32[]{:S(2)}) collective-permute-start(bf16[256,128]{1,0:T(8,128)(2,1)S(1)} %shard_map.116.a_ref), channel_id=1, source_target_pairs={{0,1},{1,2},{2,3},{3,0},{4,5},{5,6},{6,7},{7,4},{8,9},{9,10},{10,1... | collective-permute-start | bytes 196616 | tf_op jit(solution)/shard_map/ppermute | solution.py:410
  59.5 3.2 %collective-permute-start.7 = (bf16[256,256]{1,0:T(8,128)(2,1)S(1)}, bf16[256,256]{1,0:T(8,128)(2,1)S(1)}, u32[]{:S(2)}, u32[]{:S(2)}) collective-permute-start(bf16[256,256]{1,0:T(8,128)(2,1)S(1)} %get-tuple-element.16.mine_ref), channel_id=1, source_target_pairs={{0,4},{4,0},{8,12},{12,8},{16,20},{20,16},{24,28},{28,24},{32,36},... | collective-permute-start | bytes 393224 | tf_op jit(solution)/shard_map/ppermute | solution.py:479
  62.7 24.1 %copy-start.5 = (bf16[128,2048]{1,0:T(8,128)(2,1)S(1)}, bf16[128,2048]{1,0:T(8,128)(2,1)}, u32[]{:S(2)}) copy-start(bf16[128,2048]{1,0:T(8,128)(2,1)} %constant.17.clone.column_ref) | copy-start | bytes 1572868

commit v7 on v4

--- a/solution.py
+++ b/solution.py
@@ -264,9 +264,12 @@
         out_ref[im, :] = back_im * cosine + back_re * sine
 
 
+def mixed(mix_ref, here, first, samples):
+    return sum(mix_ref[here, first + t : first + t + 1] * s for t, s in enumerate(samples))
+
+
 def residual_kernel(
-    counts_ref, a_ref, b_ref, c_ref, d_ref, seen_ref, turned_ref, mix_ref, cos_ref, sin_ref, cells_ref,
-    weights_ref, resid_ref, out_ref, back_ref,
+    counts_ref, a_ref, b_ref, c_ref, d_ref, seen_ref, mix_ref, cos_ref, sin_ref, out_ref
 ):
     planes = (a_ref, b_ref, c_ref, d_ref)
     block = lax.broadcasted_iota(jnp.int32, (MAXB, BLOCK), 0)
@@ -274,17 +277,30 @@
         live = block < counts_ref[sub]
         here, re, im = parts_of(sub)
         cosine, sine = cos_ref[here, :], sin_ref[here, :]
-        s_re = [p[re, :].astype(f32) for p in planes]
-        s_im = [p[im, :].astype(f32) for p in planes]
-
-        def mixed(first, samples):
-            return sum(mix_ref[here, first + t : first + t + 1] * s for t, s in enumerate(samples))
-
-        m_re, m_im = mixed(0, s_re), mixed(0, s_im)
-        resid_ref[re, :] = jnp.where(live, seen_ref[re, :] - (m_re * cosine + m_im * sine), 0.0)
-        resid_ref[im, :] = jnp.where(live, seen_ref[im, :] - (m_im * cosine - m_re * sine), 0.0)
-        back_ref[re, :] = jnp.where(live, turned_ref[re, :] - mixed(16, s_re), 0.0)
-        back_ref[im, :] = jnp.where(live, turned_ref[im, :] - mixed(16, s_im), 0.0)
+        m_re = mixed(mix_ref, here, 0, [p[re, :].astype(f32) for p in planes])
+        m_im = mixed(mix_ref, here, 0, [p[im, :].astype(f32) for p in planes])
+        left_re = jnp.where(live, seen_ref[re, :] - (m_re * cosine + m_im * sine), 0.0)
+        left_im = jnp.where(live, seen_ref[im, :] - (m_im * cosine - m_re * sine), 0.0)
+        for b in range(MAXB):
+            lanes = slice(b * BLOCK, (b + 1) * BLOCK)
+            out_ref[sub, 0:1, lanes] = left_re[b : b + 1, :]
+            out_ref[sub, 1:2, lanes] = left_im[b : b + 1, :]
+
+
+def adjoint_kernel(
+    counts_ref, a_ref, b_ref, c_ref, d_ref, turned_ref, mix_ref, cells_ref, weights_ref,
+    out_ref, back_ref,
+):
+    planes = (a_ref, b_ref, c_ref, d_ref)
+    block = lax.broadcasted_iota(jnp.int32, (MAXB, BLOCK), 0)
+    for sub in range(2):
+        live = block < counts_ref[sub]
+        here, re, im = parts_of(sub)
+        for part in (re, im):
+            samples = [p[part, :].astype(f32) for p in planes]
+            back_ref[part, :] = jnp.where(
+                live, turned_ref[part, :] - mixed(mix_ref, here, 16, samples), 0.0
+            )
     per = CHUNK // BLOCK
     for sub in range(2):
 
@@ -446,19 +462,23 @@
         + scratch(2),
         smem=2,
     )(position, sub_u, rows, other, lift_t, lift_s, uvw, weights)
-    resid, adj = call(
-        residual_kernel,
-        (shape((4 * MAXB, BLOCK), f32), shape((4 * K, G), bf16)),
+    planes = to_stokes(samples)
+    adj = call(
+        adjoint_kernel,
+        shape((4 * K, G), bf16),
         (pltpu.VMEM((4 * MAXB, BLOCK), f32),),
         smem=1,
-    )(counts, *to_stokes(samples), seen, turned, mix, vcos, vsin, uvw, weights)
+    )(counts, *planes, turned, mix, uvw, weights)
     other_adj = lax.ppermute(adj, "facet", partner)
+    resid = call(residual_kernel, shape((2, 2, VISITS), f32), smem=1)(
+        counts, *planes, seen, mix, vcos, vsin
+    )
     shares = call(share_kernel, shape((32, K, 2 * ROWS), bf16), scratch(4), smem=2)(
         position, sub_u, adj, other_adj, lift_t, lift_s
     )
     shares = lax.all_to_all(shares, "facet", 0, 0, axis_index_groups=groups, tiled=True)
     image = call(image_kernel, shape((ROWS, 2 * L), bf16))(shares, column)
-    return (image[None], resid.reshape(1, 2, 2, VISITS))
+    return (image[None], resid[None])
 
 
 def solution(mesh):

time: 88.1 us -> 88.2 us (level)
  Pallas kernels: 21 us -> 22.5 us
    pallas_call x8 -> x9, Pallas kernels: 21 us -> 22.5 us  [run(): pl.pallas_call(kernel, out_shape=out_shape, in_specs=specs, out_specs=jax...]
  transfers between devices with their start and end apart: 10 -> 10, of which waited for: 6 -> 6; matrix products, arithmetic and copies ran while one was open for 1% -> 0% of each run, Pallas kernels for 10% -> 12%
where the time goes in v7:
time: 88.2 us; the launch traced here: 87.4 us
  waiting for transfers between devices  35.2 us (40%)
  starting transfers between devices  28.8 us (33%)
  Pallas kernels  22.5 us (26%)
    pallas_call x9, Pallas kernels, run(): pl.pallas_call(kernel, out_shape=out_shape, in_specs=specs, out_specs=jax...  22.5 us
    all_to_all x1, waiting for transfers between devices, column_of_subgrids(): lax.all_to_all(spread, 'facet', 0, 0, axis_index_groups=groups, tiled=True)  16.2 us
    all_to_all x1, waiting for transfers between devices, column_of_subgrids(): lax.all_to_all(shares, 'facet', 0, 0, axis_index_groups=groups, tiled=True)  15.2 us
    all_to_all x1, starting transfers between devices, column_of_subgrids(): lax.all_to_all(spread, 'facet', 0, 0, axis_index_groups=groups, tiled=True)  11.9 us
    ppermute x6, starting transfers between devices, to_stokes(): lax.ppermute(array, 'stokes', [(i, (i - k) % 4) for i in range(4)])  8.01 us
    all_to_all x1, starting transfers between devices, column_of_subgrids(): lax.all_to_all(shares, 'facet', 0, 0, axis_index_groups=groups, tiled=True)  4.38 us
    ppermute x6, waiting for transfers between devices, to_stokes(): lax.ppermute(array, 'stokes', [(i, (i - k) % 4) for i in range(4)])  2.85 us
    ppermute x1, starting transfers between devices, column_of_subgrids(): other = lax.ppermute(mine, 'facet', partner)  2.43 us
  transfers between devices with their start and end apart: 10, of which 6 were waited for; matrix products, arithmetic and copies ran while one was open for 0% of the time, Pallas kernels for 12%

profile of v7, /device:TPU:1, one launch (start us, length us, event | category | flops | bytes accessed | tf_op | source)
XLA Modules:
  0.0 87.4 jit_solution(4927405153980365874)
XLA Ops:
  0.6 0.0 copy-start
  0.6 0.0 copy-start.1
  0.7 0.0 copy-start.2
  0.7 0.0 copy-start.8
  0.7 3.0 %shard_map.113 = bf16[32,64,128]{2,1,0:T(8,128)(2,1)} custom-call(bf16[64,16384]{1,0:T(8,128)(2,1)} %bitcast.7, bf16[128,2048]{1,0:T(8,128)(2,1)} %constant.17.clone.column_ref), custom_call_target="tpu_custom_call" | custom-call | flops 1000000000 | bytes 1048576 | tf_op jit(solution)/shard_map/pallas_call | solution.py:379
  3.7 11.9 %all-to-all-start = ((bf16[32,64,128]{2,1,0:T(8,128)(2,1)}), bf16[32,64,128]{2,1,0:T(8,128)(2,1)S(1)}, u32[]{:S(2)}, u32[]{:S(2)}) async-start(bf16[32,64,128]{2,1,0:T(8,128)(2,1)} %shard_map.113), calls=%async_computation | async-start | bytes 1048576 | tf_op jit(solution)/shard_map/all_to_all | solution.py:424
  15.6 0.1 pad_add_fusion.here_ref
  15.7 16.2 %all-to-all-done.mine_ref = bf16[32,64,128]{2,1,0:T(8,128)(2,1)S(1)} async-done(((bf16[32,64,128]{2,1,0:T(8,128)(2,1)}), bf16[32,64,128]{2,1,0:T(8,128)(2,1)S(1)}, u32[]{:S(2)}, u32[]{:S(2)}) %all-to-all-start) | async-done | bytes 524320 | tf_op jit(solution)/shard_map/all_to_all | solution.py:424
  31.9 2.4 %collective-permute-start = (bf16[32,64,128]{2,1,0:T(8,128)(2,1)S(1)}, bf16[32,64,128]{2,1,0:T(8,128)(2,1)S(1)}, u32[]{:S(2)}, u32[]{:S(2)}) collective-permute-start(bf16[32,64,128]{2,1,0:T(8,128)(2,1)S(1)} %all-to-all-done.mine_ref), channel_id=1, source_target_pairs={{0,4},{4,0},{8,12},{12,8},{16,20},{20,16},{24,28},{28,24},{32,36},... | collective-permute-start | bytes 1572872 | tf_op jit(solution)/shard_map/ppermute | solution.py:444
  34.3 0.0 copy-done
  34.3 0.0 copy-done.1
  34.3 0.0 copy-done.2
  34.3 0.0 copy-done.8
  34.3 0.0 copy-start.3
  34.3 0.0 copy-start.6
  34.3 0.0 copy-start.7
  34.4 2.4 %shard_map.115 = (f32[128,128]{1,0:T(8,128)S(1)}, f32[128,128]{1,0:T(8,128)S(1)}, f32[128,128]{1,0:T(8,128)S(1)}, f32[256,128]{1,0:T(8,128)S(1)}, bf16[256,128]{...) custom-call(s32[2]{0:T(128)S(1)} %pad_add_fusion.here_ref, s32[3,2,8192]{2,1,0:T(2,128)S(1)} %copy-done, ...), custom_call_target="tpu_custom_call" | custom-call | flops 10000000000 | bytes 1048576 | tf_op jit(solution)/shard_map/pallas_call | solution.py:379
  36.8 1.4 %collective-permute-start.6 = (bf16[256,128]{1,0:T(8,128)(2,1)S(1)}, bf16[256,128]{1,0:T(8,128)(2,1)S(1)}, u32[]{:S(2)}, u32[]{:S(2)}) collective-permute-start(bf16[256,128]{1,0:T(8,128)(2,1)S(1)} %get-tuple-element.10), channel_id=1, source_target_pairs={{0,1},{1,2},{2,3},{3,0},{4,5},{5,6},{6,7},{7,4},{8,9},{9,10},{10,1... | collective-permute-start | bytes 196616 | tf_op jit(solution)/shard_map/ppermute | solution.py:410
  38.1 2.6 %collective-permute-start.5 = (bf16[256,128]{1,0:T(8,128)(2,1)S(1)}, bf16[256,128]{1,0:T(8,128)(2,1)S(1)}, u32[]{:S(2)}, u32[]{:S(2)}) collective-permute-start(bf16[256,128]{1,0:T(8,128)(2,1)S(1)} %get-tuple-element.10), channel_id=1, source_target_pairs={{0,2},{1,3},{2,0},{3,1},{4,6},{5,7},{6,4},{7,5},{8,10},{9,11},{10,... | collective-permute-start | bytes 196616 | tf_op jit(solution)/shard_map/ppermute | solution.py:410
  40.7 1.1 %collective-permute-start.4 = (bf16[256,128]{1,0:T(8,128)(2,1)S(1)}, bf16[256,128]{1,0:T(8,128)(2,1)S(1)}, u32[]{:S(2)}, u32[]{:S(2)}) collective-permute-start(bf16[256,128]{1,0:T(8,128)(2,1)S(1)} %get-tuple-element.10), channel_id=1, source_target_pairs={{0,3},{1,0},{2,1},{3,2},{4,7},{5,4},{6,5},{7,6},{8,11},{9,8},{10,9... | collective-permute-start | bytes 196616 | tf_op jit(solution)/shard_map/ppermute | solution.py:410
  41.8 0.0 copy-done.3
  41.8 0.0 copy-done.6
  41.8 0.0 copy-done.7
  41.8 2.1 %shard_map.114.start_ref = f32[256,256]{1,0:T(8,128)S(1)} custom-call(s32[2]{0:T(128)S(1)} %pad_add_fusion.here_ref, s32[128]{0:T(128)S(1)} %copy-done.3, bf16[32,64,128]{2,1,0:T(8,128)(2,1)S(1)} %all-to-all-done.mine_ref, f32[128,256]{1,0:T(8,128)S(1)} %copy-done.7, f32[128,256]{1,0:T(8,128)S(1)} %copy-done.6), custom_call_target="tpu_custom_call" | custom-call | flops 1000000000 | bytes 1048576 | tf_op jit(solution)/shard_map/pallas_call | solution.py:379
  43.9 0.0 collective-permute-done.other_ref
  43.9 4.5 %shard_map.116.a_ref = bf16[256,128]{1,0:T(8,128)(2,1)S(1)} custom-call(s32[2]{0:T(128)S(1)} %pad_add_fusion.here_ref, s32[128]{0:T(128)S(1)} %copy-done.3, f32[256,256]{1,0:T(8,128)S(1)} %shard_map.114.start_ref, bf16[32,64,128]{2,1,0:T(8,128)(2,1)S(1)} %collective-permute-done.other_ref, f32[128,256]{1,0:T(8,128)S(1)} %copy-done.7, ...), custom_call_target="tpu_custom_call" | custom-call | flops 1000000000 | bytes 1048576 | tf_op jit(solution)/shard_map/pallas_call | solution.py:379
  48.4 0.0 copy-start.4
  48.5 0.5 collective-permute-start.3
  48.9 0.8 collective-permute-start.2
  49.7 0.0 collective-permute-done.6.d_ref
  49.7 1.7 %collective-permute-start.1 = (bf16[256,128]{1,0:T(8,128)(2,1)S(1)}, bf16[256,128]{1,0:T(8,128)(2,1)S(1)}, u32[]{:S(2)}, u32[]{:S(2)}) collective-permute-start(bf16[256,128]{1,0:T(8,128)(2,1)S(1)} %shard_map.116.a_ref), channel_id=1, source_target_pairs={{0,3},{1,0},{2,1},{3,2},{4,7},{5,4},{6,5},{7,6},{8,11},{9,8},{10,9... | collective-permute-start | bytes 196616 | tf_op jit(solution)/shard_map/ppermute | solution.py:410
  51.4 0.0 collective-permute-done.5.c_ref
  51.4 0.0 collective-permute-done.4.b_ref
  51.4 0.2 shard_map.117.turned_ref
  51.6 1.3 %collective-permute-done.3.d_ref = bf16[256,128]{1,0:T(8,128)(2,1)S(1)} collective-permute-done((bf16[256,128]{1,0:T(8,128)(2,1)S(1)}, bf16[256,128]{1,0:T(8,128)(2,1)S(1)}, u32[]{:S(2)}, u32[]{:S(2)}) %collective-permute-start.3) | collective-permute-done | bytes 65568 | tf_op jit(solution)/shard_map/ppermute | solution.py:410
  52.9 0.7 collective-permute-done.2.c_ref
  53.6 0.9 collective-permute-done.1.b_ref
  54.4 0.0 copy-done.4
  54.4 3.1 %shard_map.118.mine_ref = bf16[256,256]{1,0:T(8,128)(2,1)S(1)} custom-call(s32[2]{0:T(128)S(1)} %copy-done.4, bf16[256,128]{1,0:T(8,128)(2,1)S(1)} %shard_map.116.a_ref, bf16[256,128]{1,0:T(8,128)(2,1)S(1)} %collective-permute-done.1.b_ref, bf16[256,128]{1,0:T(8,128)(2,1)S(1)} %collective-permute-done.2.c_ref, ...), custom_call_target="tpu_custom_call" | custom-call | flops 1000000000 | bytes 1048576 | tf_op jit(solution)/shard_map/pallas_call | solution.py:379
  57.5 2.1 %collective-permute-start.7 = (bf16[256,256]{1,0:T(8,128)(2,1)S(1)}, bf16[256,256]{1,0:T(8,128)(2,1)S(1)}, u32[]{:S(2)}, u32[]{:S(2)}) collective-permute-start(bf16[256,256]{1,0:T(8,128)(2,1)S(1)} %shard_map.118.mine_ref), channel_id=1, source_target_pairs={{0,4},{4,0},{8,12},{12,8},{16,20},{20,16},{24,28},{28,24},{32,36},... | collective-permute-start | bytes 393224 | tf_op jit(solution)/shard_map/ppermute | solution.py:472
  59.6 1.0 %collective-permute-done.7.other_ref = bf16[256,256]{1,0:T(8,128)(2,1)S(1)} collective-permute-done((bf16[256,256]{1,0:T(8,128)(2,1)S(1)}, bf16[256,256]{1,0:T(8,128)(2,1)S(1)}, u32[]{:S(2)}, u32[]{:S(2)}) %collective-permute-start.7) | collective-permute-done | bytes 131104 | tf_op jit(solution)/shard_map/ppermute | solution.py:472
  60.6 4.0 %shard_map.119 = bf16[32,64,128]{2,1,0:T(8,128)(2,1)} custom-call(s32[2]{0:T(128)S(1)} %pad_add_fusion.here_ref, s32[128]{0:T(128)S(1)} %copy-done.3, bf16[256,256]{1,0:T(8,128)(2,1)S(1)} %shard_map.118.mine_ref, bf16[256,256]{1,0:T(8,128)(2,1)S(1)} %collective-permute-done.7.other_ref, f32[128,256]{1,0:T(8,128)S(1)} %copy-done.7, f32[128,256]{1,0:T(8,128)S(1)} %copy-done.6), custom_call_target="tpu_custom_call" | custom-call | flops 1000000000 | bytes 1048576 | tf_op jit(solution)/shard_map/pallas_call | solution.py:379
  64.6 4.4 %all-to-all-start.1 = ((bf16[32,64,128]{2,1,0:T(8,128)(2,1)}), bf16[32,64,128]{2,1,0:T(8,128)(2,1)S(1)}, u32[]{:S(2)}, u32[]{:S(2)}) async-start(bf16[32,64,128]{2,1,0:T(8,128)(2,1)} %shard_map.119), calls=%async_computation.1 | async-start | bytes 1048576 | tf_op jit(solution)/shard_map/all_to_all | solution.py:479
  69.0 0.0 copy-start.5
  69.0 1.4 %shard_map.121 = f32[2,2,8192]{2,1,0:T(2,128)} custom-call(s32[2]{0:T(128)S(1)} %copy-done.4, bf16[256,128]{1,0:T(8,128)(2,1)S(1)} %shard_map.116.a_ref, bf16[256,128]{1,0:T(8,128)(2,1)S(1)} %collective-permute-done.1.b_ref, bf16[256,128]{1,0:T(8,128)(2,1)S(1)} %collective-permute-done.2.c_ref, bf16[256,128]{1,0:T(8,128)(2,1)S(1)} %collective-permute-done.3.d_ref, ...), custom_call_target="tpu_custom_call" | custom-call | flops 1000000000 | bytes 1048576 | tf_op jit(solution)/shard_map/pallas_call | solution.py:379
  70.4 15.2 %all-to-all-done.1.shares_ref = bf16[32,64,128]{2,1,0:T(8,128)(2,1)S(1)} async-done(((bf16[32,64,128]{2,1,0:T(8,128)(2,1)}), bf16[32,64,128]{2,1,0:T(8,128)(2,1)S(1)}, u32[]{:S(2)}, u32[]{:S(2)}) %all-to-all-start.1) | async-done | bytes 524320 | tf_op jit(solution)/shard_map/all_to_all | solution.py:479
  85.6 0.0 copy-done.5
  85.6 1.8 %shard_map.120 = bf16[64,16384]{1,0:T(8,128)(2,1)} custom-call(bf16[32,64,128]{2,1,0:T(8,128)(2,1)S(1)} %all-to-all-done.1.shares_ref, bf16[128,2048]{1,0:T(8,128)(2,1)S(1)} %copy-done.5), custom_call_target="tpu_custom_call" | custom-call | flops 1000000000 | bytes 1048576 | tf_op jit(solution)/shard_map/pallas_call | solution.py:379
Async XLA Ops:
  0.6 33.7 %copy-start = (s32[3,2,8192]{2,1,0:T(2,128)S(1)}, s32[3,2,8192]{2,1,0:T(2,128)}, u32[]{:S(2)}) copy-start(s32[3,2,8192]{2,1,0:T(2,128)} %cells_ref.5) | copy-start | bytes 589828
  0.6 33.7 %copy-start.1 = (f32[1,2,2,8192]{3,2,1,0:T(2,128)S(1)}, f32[1,2,2,8192]{3,2,1,0:T(2,128)}, u32[]{:S(2)}) copy-start(f32[1,2,2,8192]{3,2,1,0:T(2,128)} %param.15) | copy-start | bytes 393220
  0.7 33.7 %copy-start.2 = (f32[4,4,2,64]{3,2,1,0:T(2,128)S(1)}, f32[4,4,2,64]{3,2,1,0:T(2,128)}, u32[]{:S(2)}) copy-start(f32[4,4,2,64]{3,2,1,0:T(2,128)} %mueller_ref.1) | copy-start | bytes 24580
  0.7 33.7 %copy-start.8 = (bf16[64,256]{1,0:T(8,128)(2,1)S(1)}, bf16[64,256]{1,0:T(8,128)(2,1)}, u32[]{:S(2)}) copy-start(bf16[64,256]{1,0:T(8,128)(2,1)} %constant.18.clone.kernel_ref) | copy-start | bytes 98308
  3.7 28.2 %all-to-all-start = ((bf16[32,64,128]{2,1,0:T(8,128)(2,1)}), bf16[32,64,128]{2,1,0:T(8,128)(2,1)S(1)}, u32[]{:S(2)}, u32[]{:S(2)}) async-start(bf16[32,64,128]{2,1,0:T(8,128)(2,1)} %shard_map.113), calls=%async_computation | async-start | bytes 1048576 | tf_op jit(solution)/shard_map/all_to_all | solution.py:424
  31.9 12.0 %collective-permute-start = (bf16[32,64,128]{2,1,0:T(8,128)(2,1)S(1)}, bf16[32,64,128]{2,1,0:T(8,128)(2,1)S(1)}, u32[]{:S(2)}, u32[]{:S(2)}) collective-permute-start(bf16[32,64,128]{2,1,0:T(8,128)(2,1)S(1)} %all-to-all-done.mine_ref), channel_id=1, source_target_pairs={{0,4},{4,0},{8,12},{12,8},{16,20},{20,16},{24,28},{28,24},{32,36},... | collective-permute-start | bytes 1572872 | tf_op jit(solution)/shard_map/ppermute | solution.py:444
  34.3 7.5 %copy-start.3 = (s32[128]{0:T(128)S(1)}, s32[128]{0:T(128)}, u32[]{:S(2)}) copy-start(s32[128]{0:T(128)} %sub_ref.5) | copy-start | bytes 1540
  34.3 7.5 %copy-start.6 = (f32[128,256]{1,0:T(8,128)S(1)}, f32[128,256]{1,0:T(8,128)}, u32[]{:S(2)}) copy-start(f32[128,256]{1,0:T(8,128)} %constant.20.clone.lift_s_ref) | copy-start | bytes 393220
  34.3 7.5 %copy-start.7 = (f32[128,256]{1,0:T(8,128)S(1)}, f32[128,256]{1,0:T(8,128)}, u32[]{:S(2)}) copy-start(f32[128,256]{1,0:T(8,128)} %constant.19.clone.lift_ref) | copy-start | bytes 393220
  36.8 13.0 %collective-permute-start.6 = (bf16[256,128]{1,0:T(8,128)(2,1)S(1)}, bf16[256,128]{1,0:T(8,128)(2,1)S(1)}, u32[]{:S(2)}, u32[]{:S(2)}) collective-permute-start(bf16[256,128]{1,0:T(8,128)(2,1)S(1)} %get-tuple-element.10), channel_id=1, source_target_pairs={{0,1},{1,2},{2,3},{3,0},{4,5},{5,6},{6,7},{7,4},{8,9},{9,10},{10,1... | collective-permute-start | bytes 196616 | tf_op jit(solution)/shard_map/ppermute | solution.py:410
  38.1 13.3 %collective-permute-start.5 = (bf16[256,128]{1,0:T(8,128)(2,1)S(1)}, bf16[256,128]{1,0:T(8,128)(2,1)S(1)}, u32[]{:S(2)}, u32[]{:S(2)}) collective-permute-start(bf16[256,128]{1,0:T(8,128)(2,1)S(1)} %get-tuple-element.10), channel_id=1, source_target_pairs={{0,2},{1,3},{2,0},{3,1},{4,6},{5,7},{6,4},{7,5},{8,10},{9,11},{10,... | collective-permute-start | bytes 196616 | tf_op jit(solution)/shard_map/ppermute | solution.py:410
  40.7 10.7 %collective-permute-start.4 = (bf16[256,128]{1,0:T(8,128)(2,1)S(1)}, bf16[256,128]{1,0:T(8,128)(2,1)S(1)}, u32[]{:S(2)}, u32[]{:S(2)}) collective-permute-start(bf16[256,128]{1,0:T(8,128)(2,1)S(1)} %get-tuple-element.10), channel_id=1, source_target_pairs={{0,3},{1,0},{2,1},{3,2},{4,7},{5,4},{6,5},{7,6},{8,11},{9,8},{10,9... | collective-permute-start | bytes 196616 | tf_op jit(solution)/shard_map/ppermute | solution.py:410
  48.4 6.0 %copy-start.4 = (s32[2]{0:T(128)S(1)}, s32[2]{0:T(128)}, u32[]{:S(2)}) copy-start(s32[2]{0:T(128)} %counts_ref.3) | copy-start | bytes 28
  48.5 4.4 %collective-permute-start.3 = (bf16[256,128]{1,0:T(8,128)(2,1)S(1)}, bf16[256,128]{1,0:T(8,128)(2,1)S(1)}, u32[]{:S(2)}, u32[]{:S(2)}) collective-permute-start(bf16[256,128]{1,0:T(8,128)(2,1)S(1)} %shard_map.116.a_ref), channel_id=1, source_target_pairs={{0,1},{1,2},{2,3},{3,0},{4,5},{5,6},{6,7},{7,4},{8,9},{9,10},{10,1... | collective-permute-start | bytes 196616 | tf_op jit(solution)/shard_map/ppermute | solution.py:410
  48.9 4.6 %collective-permute-start.2 = (bf16[256,128]{1,0:T(8,128)(2,1)S(1)}, bf16[256,128]{1,0:T(8,128)(2,1)S(1)}, u32[]{:S(2)}, u32[]{:S(2)}) collective-permute-start(bf16[256,128]{1,0:T(8,128)(2,1)S(1)} %shard_map.116.a_ref), channel_id=1, source_target_pairs={{0,2},{1,3},{2,0},{3,1},{4,6},{5,7},{6,4},{7,5},{8,10},{9,11},{10,... | collective-permute-start | bytes 196616 | tf_op jit(solution)/shard_map/ppermute | solution.py:410
  49.7 4.7 %collective-permute-start.1 = (bf16[256,128]{1,0:T(8,128)(2,1)S(1)}, bf16[256,128]{1,0:T(8,128)(2,1)S(1)}, u32[]{:S(2)}, u32[]{:S(2)}) collective-permute-start(bf16[256,128]{1,0:T(8,128)(2,1)S(1)} %shard_map.116.a_ref), channel_id=1, source_target_pairs={{0,3},{1,0},{2,1},{3,2},{4,7},{5,4},{6,5},{7,6},{8,11},{9,8},{10,9... | collective-permute-start | bytes 196616 | tf_op jit(solution)/shard_map/ppermute | solution.py:410
  57.5 3.1 %collective-permute-start.7 = (bf16[256,256]{1,0:T(8,128)(2,1)S(1)}, bf16[256,256]{1,0:T(8,128)(2,1)S(1)}, u32[]{:S(2)}, u32[]{:S(2)}) collective-permute-start(bf16[256,256]{1,0:T(8,128)(2,1)S(1)} %shard_map.118.mine_ref), channel_id=1, source_target_pairs={{0,4},{4,0},{8,12},{12,8},{16,20},{20,16},{24,28},{28,24},{32,36},... | collective-permute-start | bytes 393224 | tf_op jit(solution)/shard_map/ppermute | solution.py:472
  64.6 21.0 %all-to-all-start.1 = ((bf16[32,64,128]{2,1,0:T(8,128)(2,1)}), bf16[32,64,128]{2,1,0:T(8,128)(2,1)S(1)}, u32[]{:S(2)}, u32[]{:S(2)}) async-start(bf16[32,64,128]{2,1,0:T(8,128)(2,1)} %shard_map.119), calls=%async_computation.1 | async-start | bytes 1048576 | tf_op jit(solution)/shard_map/all_to_all | solution.py:479
  69.0 16.6 %copy-start.5 = (bf16[128,2048]{1,0:T(8,128)(2,1)S(1)}, bf16[128,2048]{1,0:T(8,128)(2,1)}, u32[]{:S(2)}) copy-start(bf16[128,2048]{1,0:T(8,128)(2,1)} %constant.17.clone.column_ref) | copy-start | bytes 1572868

commit v8 on v7

--- a/solution.py
+++ b/solution.py
@@ -250,7 +250,7 @@
     )
 
 
-def observed_kernel(a_ref, b_ref, c_ref, d_ref, mix_ref, cos_ref, sin_ref, out_ref):
+def observed_kernel(a_ref, b_ref, d_ref, c_ref, mix_ref, cos_ref, sin_ref, out_ref):
     for sub in range(2):
         here, re, im = parts_of(sub)
         cosine, sine = cos_ref[here, :], sin_ref[here, :]
@@ -269,7 +269,7 @@
 
 
 def residual_kernel(
-    counts_ref, a_ref, b_ref, c_ref, d_ref, seen_ref, mix_ref, cos_ref, sin_ref, out_ref
+    counts_ref, a_ref, b_ref, d_ref, c_ref, seen_ref, mix_ref, cos_ref, sin_ref, out_ref
 ):
     planes = (a_ref, b_ref, c_ref, d_ref)
     block = lax.broadcasted_iota(jnp.int32, (MAXB, BLOCK), 0)
@@ -288,7 +288,7 @@
 
 
 def adjoint_kernel(
-    counts_ref, a_ref, b_ref, c_ref, d_ref, turned_ref, mix_ref, cells_ref, weights_ref,
+    counts_ref, a_ref, b_ref, d_ref, c_ref, turned_ref, mix_ref, cells_ref, weights_ref,
     out_ref, back_ref,
 ):
     planes = (a_ref, b_ref, c_ref, d_ref)
@@ -354,7 +354,7 @@
             out_ref[q] = (total * sign + swap(swapped)).astype(bf16)
         return carry
 
-    lax.fori_loop(0, 16, pair, 0, unroll=4)
+    lax.fori_loop(0, 16, pair, 0, unroll=8)
 
 
 def image_kernel(shares_ref, column_ref, out_ref):
@@ -405,10 +405,10 @@
     partner = [(i, i ^ 1) for i in range(FACETS)]
 
     def to_stokes(array):
-        out = [array]
+        out = [array] * 4
         for k in (1, 2, 3):
-            out.append(lax.ppermute(array, "stokes", [(i, (i - k) % 4) for i in range(4)]))
-        return out
+            out[k] = lax.ppermute(array, "stokes", [(i, (i - k) % 4) for i in range(4)])
+        return [out[0], out[1], out[3], out[2]]
 
     spread = call(
         column_kernel,

time: 88.2 us -> 88.1 us (level)
  transfers between devices with their start and end apart: 10 -> 10, of which waited for: 6 -> 5; matrix products, arithmetic and copies ran while one was open for 0% -> 0% of each run, Pallas kernels for 12% -> 12%
where the time goes in v8:
time: 88.1 us; the launch traced here: 87.3 us
  waiting for transfers between devices  35 us (40%)
  starting transfers between devices  29 us (33%)
  Pallas kernels  22.4 us (25%)
    pallas_call x9, Pallas kernels, run(): pl.pallas_call(kernel, out_shape=out_shape, in_specs=specs, out_specs=jax...  22.4 us
    all_to_all x1, waiting for transfers between devices, column_of_subgrids(): lax.all_to_all(spread, 'facet', 0, 0, axis_index_groups=groups, tiled=True)  16.2 us
    all_to_all x1, waiting for transfers between devices, column_of_subgrids(): lax.all_to_all(shares, 'facet', 0, 0, axis_index_groups=groups, tiled=True)  15.2 us
    all_to_all x1, starting transfers between devices, column_of_subgrids(): lax.all_to_all(spread, 'facet', 0, 0, axis_index_groups=groups, tiled=True)  11.9 us
    ppermute x6, starting transfers between devices, to_stokes(): out[k] = lax.ppermute(array, 'stokes', [(i, (i - k) % 4) for i in range(4)])  8.51 us
    all_to_all x1, starting transfers between devices, column_of_subgrids(): lax.all_to_all(shares, 'facet', 0, 0, axis_index_groups=groups, tiled=True)  4.37 us
    ppermute x6, waiting for transfers between devices, to_stokes(): out[k] = lax.ppermute(array, 'stokes', [(i, (i - k) % 4) for i in range(4)])  2.58 us
    ppermute x1, starting transfers between devices, column_of_subgrids(): other = lax.ppermute(mine, 'facet', partner)  2.43 us
  transfers between devices with their start and end apart: 10, of which 5 were waited for; matrix products, arithmetic and copies ran while one was open for 0% of the time, Pallas kernels for 12%

profile of v8, /device:TPU:1, one launch (start us, length us, event | category | flops | bytes accessed | tf_op | source)
XLA Modules:
  0.0 87.3 jit_solution(14891128731940380375)
XLA Ops:
  0.6 0.0 copy-start
  0.6 0.0 copy-start.1
  0.7 0.0 copy-start.2
  0.7 0.0 copy-start.8
  0.7 3.0 %shard_map.113 = bf16[32,64,128]{2,1,0:T(8,128)(2,1)} custom-call(bf16[64,16384]{1,0:T(8,128)(2,1)} %bitcast.7, bf16[128,2048]{1,0:T(8,128)(2,1)} %constant.17.clone.column_ref), custom_call_target="tpu_custom_call" | custom-call | flops 1000000000 | bytes 1048576 | tf_op jit(solution)/shard_map/pallas_call | solution.py:379
  3.7 11.9 %all-to-all-start = ((bf16[32,64,128]{2,1,0:T(8,128)(2,1)}), bf16[32,64,128]{2,1,0:T(8,128)(2,1)S(1)}, u32[]{:S(2)}, u32[]{:S(2)}) async-start(bf16[32,64,128]{2,1,0:T(8,128)(2,1)} %shard_map.113), calls=%async_computation | async-start | bytes 1048576 | tf_op jit(solution)/shard_map/all_to_all | solution.py:424
  15.6 0.1 pad_add_fusion.here_ref
  15.7 16.2 %all-to-all-done.mine_ref = bf16[32,64,128]{2,1,0:T(8,128)(2,1)S(1)} async-done(((bf16[32,64,128]{2,1,0:T(8,128)(2,1)}), bf16[32,64,128]{2,1,0:T(8,128)(2,1)S(1)}, u32[]{:S(2)}, u32[]{:S(2)}) %all-to-all-start) | async-done | bytes 524320 | tf_op jit(solution)/shard_map/all_to_all | solution.py:424
  31.9 2.4 %collective-permute-start = (bf16[32,64,128]{2,1,0:T(8,128)(2,1)S(1)}, bf16[32,64,128]{2,1,0:T(8,128)(2,1)S(1)}, u32[]{:S(2)}, u32[]{:S(2)}) collective-permute-start(bf16[32,64,128]{2,1,0:T(8,128)(2,1)S(1)} %all-to-all-done.mine_ref), channel_id=1, source_target_pairs={{0,4},{4,0},{8,12},{12,8},{16,20},{20,16},{24,28},{28,24},{32,36},... | collective-permute-start | bytes 1572872 | tf_op jit(solution)/shard_map/ppermute | solution.py:444
  34.3 0.0 copy-done
  34.3 0.0 copy-done.1
  34.3 0.0 copy-done.2
  34.3 0.0 copy-done.8
  34.3 0.0 copy-start.3
  34.3 0.0 copy-start.6
  34.3 0.0 copy-start.7
  34.4 2.4 %shard_map.115 = (f32[128,128]{1,0:T(8,128)S(1)}, f32[128,128]{1,0:T(8,128)S(1)}, f32[128,128]{1,0:T(8,128)S(1)}, f32[256,128]{1,0:T(8,128)S(1)}, bf16[256,128]{...) custom-call(s32[2]{0:T(128)S(1)} %pad_add_fusion.here_ref, s32[3,2,8192]{2,1,0:T(2,128)S(1)} %copy-done, ...), custom_call_target="tpu_custom_call" | custom-call | flops 10000000000 | bytes 1048576 | tf_op jit(solution)/shard_map/pallas_call | solution.py:379
  36.8 3.0 %collective-permute-start.6 = (bf16[256,128]{1,0:T(8,128)(2,1)S(1)}, bf16[256,128]{1,0:T(8,128)(2,1)S(1)}, u32[]{:S(2)}, u32[]{:S(2)}) collective-permute-start(bf16[256,128]{1,0:T(8,128)(2,1)S(1)} %get-tuple-element.10), channel_id=1, source_target_pairs={{0,2},{1,3},{2,0},{3,1},{4,6},{5,7},{6,4},{7,5},{8,10},{9,11},{10,... | collective-permute-start | bytes 196616 | tf_op jit(solution)/shard_map/ppermute | solution.py:410
  39.7 0.4 collective-permute-start.5
  40.1 2.3 %collective-permute-start.4 = (bf16[256,128]{1,0:T(8,128)(2,1)S(1)}, bf16[256,128]{1,0:T(8,128)(2,1)S(1)}, u32[]{:S(2)}, u32[]{:S(2)}) collective-permute-start(bf16[256,128]{1,0:T(8,128)(2,1)S(1)} %get-tuple-element.10), channel_id=1, source_target_pairs={{0,3},{1,0},{2,1},{3,2},{4,7},{5,4},{6,5},{7,6},{8,11},{9,8},{10,9... | collective-permute-start | bytes 196616 | tf_op jit(solution)/shard_map/ppermute | solution.py:410
  42.4 0.0 copy-done.3
  42.4 0.0 copy-done.6
  42.4 0.0 copy-done.7
  42.4 2.1 %shard_map.114.start_ref = f32[256,256]{1,0:T(8,128)S(1)} custom-call(s32[2]{0:T(128)S(1)} %pad_add_fusion.here_ref, s32[128]{0:T(128)S(1)} %copy-done.3, bf16[32,64,128]{2,1,0:T(8,128)(2,1)S(1)} %all-to-all-done.mine_ref, f32[128,256]{1,0:T(8,128)S(1)} %copy-done.7, f32[128,256]{1,0:T(8,128)S(1)} %copy-done.6), custom_call_target="tpu_custom_call" | custom-call | flops 1000000000 | bytes 1048576 | tf_op jit(solution)/shard_map/pallas_call | solution.py:379
  44.5 0.0 collective-permute-done.other_ref
  44.5 4.5 %shard_map.116.a_ref = bf16[256,128]{1,0:T(8,128)(2,1)S(1)} custom-call(s32[2]{0:T(128)S(1)} %pad_add_fusion.here_ref, s32[128]{0:T(128)S(1)} %copy-done.3, f32[256,256]{1,0:T(8,128)S(1)} %shard_map.114.start_ref, bf16[32,64,128]{2,1,0:T(8,128)(2,1)S(1)} %collective-permute-done.other_ref, f32[128,256]{1,0:T(8,128)S(1)} %copy-done.7, ...), custom_call_target="tpu_custom_call" | custom-call | flops 1000000000 | bytes 1048576 | tf_op jit(solution)/shard_map/pallas_call | solution.py:379
  49.1 0.0 copy-start.4
  49.1 0.1 collective-permute-start.3
  49.2 0.6 collective-permute-start.2
  49.7 0.0 collective-permute-done.6.c_ref
  49.7 2.2 %collective-permute-start.1 = (bf16[256,128]{1,0:T(8,128)(2,1)S(1)}, bf16[256,128]{1,0:T(8,128)(2,1)S(1)}, u32[]{:S(2)}, u32[]{:S(2)}) collective-permute-start(bf16[256,128]{1,0:T(8,128)(2,1)S(1)} %shard_map.116.a_ref), channel_id=1, source_target_pairs={{0,3},{1,0},{2,1},{3,2},{4,7},{5,4},{6,5},{7,6},{8,11},{9,8},{10,9... | collective-permute-start | bytes 196616 | tf_op jit(solution)/shard_map/ppermute | solution.py:410
  51.9 0.0 collective-permute-done.5.d_ref
  51.9 0.0 collective-permute-done.4.b_ref
  51.9 0.2 shard_map.117.turned_ref
  52.1 1.8 %collective-permute-done.3.c_ref = bf16[256,128]{1,0:T(8,128)(2,1)S(1)} collective-permute-done((bf16[256,128]{1,0:T(8,128)(2,1)S(1)}, bf16[256,128]{1,0:T(8,128)(2,1)S(1)}, u32[]{:S(2)}, u32[]{:S(2)}) %collective-permute-start.3) | collective-permute-done | bytes 65568 | tf_op jit(solution)/shard_map/ppermute | solution.py:410
  53.9 0.8 collective-permute-done.2.d_ref
  54.7 0.0 collective-permute-done.1.b_ref
  54.7 0.0 copy-done.4
  54.7 3.1 %shard_map.118.mine_ref = bf16[256,256]{1,0:T(8,128)(2,1)S(1)} custom-call(s32[2]{0:T(128)S(1)} %copy-done.4, bf16[256,128]{1,0:T(8,128)(2,1)S(1)} %shard_map.116.a_ref, bf16[256,128]{1,0:T(8,128)(2,1)S(1)} %collective-permute-done.1.b_ref, bf16[256,128]{1,0:T(8,128)(2,1)S(1)} %collective-permute-done.2.d_ref, ...), custom_call_target="tpu_custom_call" | custom-call | flops 1000000000 | bytes 1048576 | tf_op jit(solution)/shard_map/pallas_call | solution.py:379
  57.8 1.8 %collective-permute-start.7 = (bf16[256,256]{1,0:T(8,128)(2,1)S(1)}, bf16[256,256]{1,0:T(8,128)(2,1)S(1)}, u32[]{:S(2)}, u32[]{:S(2)}) collective-permute-start(bf16[256,256]{1,0:T(8,128)(2,1)S(1)} %shard_map.118.mine_ref), channel_id=1, source_target_pairs={{0,4},{4,0},{8,12},{12,8},{16,20},{20,16},{24,28},{28,24},{32,36},... | collective-permute-start | bytes 393224 | tf_op jit(solution)/shard_map/ppermute | solution.py:472
  59.5 1.0 %collective-permute-done.7.other_ref = bf16[256,256]{1,0:T(8,128)(2,1)S(1)} collective-permute-done((bf16[256,256]{1,0:T(8,128)(2,1)S(1)}, bf16[256,256]{1,0:T(8,128)(2,1)S(1)}, u32[]{:S(2)}, u32[]{:S(2)}) %collective-permute-start.7) | collective-permute-done | bytes 131104 | tf_op jit(solution)/shard_map/ppermute | solution.py:472
  60.5 4.0 %shard_map.119 = bf16[32,64,128]{2,1,0:T(8,128)(2,1)} custom-call(s32[2]{0:T(128)S(1)} %pad_add_fusion.here_ref, s32[128]{0:T(128)S(1)} %copy-done.3, bf16[256,256]{1,0:T(8,128)(2,1)S(1)} %shard_map.118.mine_ref, bf16[256,256]{1,0:T(8,128)(2,1)S(1)} %collective-permute-done.7.other_ref, f32[128,256]{1,0:T(8,128)S(1)} %copy-done.7, f32[128,256]{1,0:T(8,128)S(1)} %copy-done.6), custom_call_target="tpu_custom_call" | custom-call | flops 1000000000 | bytes 1048576 | tf_op jit(solution)/shard_map/pallas_call | solution.py:379
  64.5 4.4 %all-to-all-start.1 = ((bf16[32,64,128]{2,1,0:T(8,128)(2,1)}), bf16[32,64,128]{2,1,0:T(8,128)(2,1)S(1)}, u32[]{:S(2)}, u32[]{:S(2)}) async-start(bf16[32,64,128]{2,1,0:T(8,128)(2,1)} %shard_map.119), calls=%async_computation.1 | async-start | bytes 1048576 | tf_op jit(solution)/shard_map/all_to_all | solution.py:479
  68.9 0.0 copy-start.5
  68.9 1.4 %shard_map.121 = f32[2,2,8192]{2,1,0:T(2,128)} custom-call(s32[2]{0:T(128)S(1)} %copy-done.4, bf16[256,128]{1,0:T(8,128)(2,1)S(1)} %shard_map.116.a_ref, bf16[256,128]{1,0:T(8,128)(2,1)S(1)} %collective-permute-done.1.b_ref, bf16[256,128]{1,0:T(8,128)(2,1)S(1)} %collective-permute-done.2.d_ref, bf16[256,128]{1,0:T(8,128)(2,1)S(1)} %collective-permute-done.3.c_ref, ...), custom_call_target="tpu_custom_call" | custom-call | flops 1000000000 | bytes 1048576 | tf_op jit(solution)/shard_map/pallas_call | solution.py:379
  70.3 15.2 %all-to-all-done.1.shares_ref = bf16[32,64,128]{2,1,0:T(8,128)(2,1)S(1)} async-done(((bf16[32,64,128]{2,1,0:T(8,128)(2,1)}), bf16[32,64,128]{2,1,0:T(8,128)(2,1)S(1)}, u32[]{:S(2)}, u32[]{:S(2)}) %all-to-all-start.1) | async-done | bytes 524320 | tf_op jit(solution)/shard_map/all_to_all | solution.py:479
  85.5 0.0 copy-done.5
  85.5 1.8 %shard_map.120 = bf16[64,16384]{1,0:T(8,128)(2,1)} custom-call(bf16[32,64,128]{2,1,0:T(8,128)(2,1)S(1)} %all-to-all-done.1.shares_ref, bf16[128,2048]{1,0:T(8,128)(2,1)S(1)} %copy-done.5), custom_call_target="tpu_custom_call" | custom-call | flops 1000000000 | bytes 1048576 | tf_op jit(solution)/shard_map/pallas_call | solution.py:379
Async XLA Ops:
  0.6 33.7 %copy-start = (s32[3,2,8192]{2,1,0:T(2,128)S(1)}, s32[3,2,8192]{2,1,0:T(2,128)}, u32[]{:S(2)}) copy-start(s32[3,2,8192]{2,1,0:T(2,128)} %cells_ref.5) | copy-start | bytes 589828
  0.6 33.7 %copy-start.1 = (f32[1,2,2,8192]{3,2,1,0:T(2,128)S(1)}, f32[1,2,2,8192]{3,2,1,0:T(2,128)}, u32[]{:S(2)}) copy-start(f32[1,2,2,8192]{3,2,1,0:T(2,128)} %param.15) | copy-start | bytes 393220
  0.7 33.7 %copy-start.2 = (f32[4,4,2,64]{3,2,1,0:T(2,128)S(1)}, f32[4,4,2,64]{3,2,1,0:T(2,128)}, u32[]{:S(2)}) copy-start(f32[4,4,2,64]{3,2,1,0:T(2,128)} %mueller_ref.1) | copy-start | bytes 24580
  0.7 33.7 %copy-start.8 = (bf16[64,256]{1,0:T(8,128)(2,1)S(1)}, bf16[64,256]{1,0:T(8,128)(2,1)}, u32[]{:S(2)}) copy-start(bf16[64,256]{1,0:T(8,128)(2,1)} %constant.18.clone.kernel_ref) | copy-start | bytes 98308
  3.7 28.2 %all-to-all-start = ((bf16[32,64,128]{2,1,0:T(8,128)(2,1)}), bf16[32,64,128]{2,1,0:T(8,128)(2,1)S(1)}, u32[]{:S(2)}, u32[]{:S(2)}) async-start(bf16[32,64,128]{2,1,0:T(8,128)(2,1)} %shard_map.113), calls=%async_computation | async-start | bytes 1048576 | tf_op jit(solution)/shard_map/all_to_all | solution.py:424
  31.9 12.6 %collective-permute-start = (bf16[32,64,128]{2,1,0:T(8,128)(2,1)S(1)}, bf16[32,64,128]{2,1,0:T(8,128)(2,1)S(1)}, u32[]{:S(2)}, u32[]{:S(2)}) collective-permute-start(bf16[32,64,128]{2,1,0:T(8,128)(2,1)S(1)} %all-to-all-done.mine_ref), channel_id=1, source_target_pairs={{0,4},{4,0},{8,12},{12,8},{16,20},{20,16},{24,28},{28,24},{32,36},... | collective-permute-start | bytes 1572872 | tf_op jit(solution)/shard_map/ppermute | solution.py:444
  34.3 8.1 %copy-start.3 = (s32[128]{0:T(128)S(1)}, s32[128]{0:T(128)}, u32[]{:S(2)}) copy-start(s32[128]{0:T(128)} %sub_ref.5) | copy-start | bytes 1540
  34.3 8.1 %copy-start.6 = (f32[128,256]{1,0:T(8,128)S(1)}, f32[128,256]{1,0:T(8,128)}, u32[]{:S(2)}) copy-start(f32[128,256]{1,0:T(8,128)} %constant.20.clone.lift_s_ref) | copy-start | bytes 393220
  34.3 8.1 %copy-start.7 = (f32[128,256]{1,0:T(8,128)S(1)}, f32[128,256]{1,0:T(8,128)}, u32[]{:S(2)}) copy-start(f32[128,256]{1,0:T(8,128)} %constant.19.clone.lift_ref) | copy-start | bytes 393220
  36.8 13.0 %collective-permute-start.6 = (bf16[256,128]{1,0:T(8,128)(2,1)S(1)}, bf16[256,128]{1,0:T(8,128)(2,1)S(1)}, u32[]{:S(2)}, u32[]{:S(2)}) collective-permute-start(bf16[256,128]{1,0:T(8,128)(2,1)S(1)} %get-tuple-element.10), channel_id=1, source_target_pairs={{0,2},{1,3},{2,0},{3,1},{4,6},{5,7},{6,4},{7,5},{8,10},{9,11},{10,... | collective-permute-start | bytes 196616 | tf_op jit(solution)/shard_map/ppermute | solution.py:410
  39.7 12.2 %collective-permute-start.5 = (bf16[256,128]{1,0:T(8,128)(2,1)S(1)}, bf16[256,128]{1,0:T(8,128)(2,1)S(1)}, u32[]{:S(2)}, u32[]{:S(2)}) collective-permute-start(bf16[256,128]{1,0:T(8,128)(2,1)S(1)} %get-tuple-element.10), channel_id=1, source_target_pairs={{0,1},{1,2},{2,3},{3,0},{4,5},{5,6},{6,7},{7,4},{8,9},{9,10},{10,1... | collective-permute-start | bytes 196616 | tf_op jit(solution)/shard_map/ppermute | solution.py:410
  40.1 11.8 %collective-permute-start.4 = (bf16[256,128]{1,0:T(8,128)(2,1)S(1)}, bf16[256,128]{1,0:T(8,128)(2,1)S(1)}, u32[]{:S(2)}, u32[]{:S(2)}) collective-permute-start(bf16[256,128]{1,0:T(8,128)(2,1)S(1)} %get-tuple-element.10), channel_id=1, source_target_pairs={{0,3},{1,0},{2,1},{3,2},{4,7},{5,4},{6,5},{7,6},{8,11},{9,8},{10,9... | collective-permute-start | bytes 196616 | tf_op jit(solution)/shard_map/ppermute | solution.py:410
  49.1 5.6 %copy-start.4 = (s32[2]{0:T(128)S(1)}, s32[2]{0:T(128)}, u32[]{:S(2)}) copy-start(s32[2]{0:T(128)} %counts_ref.3) | copy-start | bytes 28
  49.1 4.8 %collective-permute-start.3 = (bf16[256,128]{1,0:T(8,128)(2,1)S(1)}, bf16[256,128]{1,0:T(8,128)(2,1)S(1)}, u32[]{:S(2)}, u32[]{:S(2)}) collective-permute-start(bf16[256,128]{1,0:T(8,128)(2,1)S(1)} %shard_map.116.a_ref), channel_id=1, source_target_pairs={{0,2},{1,3},{2,0},{3,1},{4,6},{5,7},{6,4},{7,5},{8,10},{9,11},{10,... | collective-permute-start | bytes 196616 | tf_op jit(solution)/shard_map/ppermute | solution.py:410
  49.2 5.5 %collective-permute-start.2 = (bf16[256,128]{1,0:T(8,128)(2,1)S(1)}, bf16[256,128]{1,0:T(8,128)(2,1)S(1)}, u32[]{:S(2)}, u32[]{:S(2)}) collective-permute-start(bf16[256,128]{1,0:T(8,128)(2,1)S(1)} %shard_map.116.a_ref), channel_id=1, source_target_pairs={{0,1},{1,2},{2,3},{3,0},{4,5},{5,6},{6,7},{7,4},{8,9},{9,10},{10,1... | collective-permute-start | bytes 196616 | tf_op jit(solution)/shard_map/ppermute | solution.py:410
  49.7 4.9 %collective-permute-start.1 = (bf16[256,128]{1,0:T(8,128)(2,1)S(1)}, bf16[256,128]{1,0:T(8,128)(2,1)S(1)}, u32[]{:S(2)}, u32[]{:S(2)}) collective-permute-start(bf16[256,128]{1,0:T(8,128)(2,1)S(1)} %shard_map.116.a_ref), channel_id=1, source_target_pairs={{0,3},{1,0},{2,1},{3,2},{4,7},{5,4},{6,5},{7,6},{8,11},{9,8},{10,9... | collective-permute-start | bytes 196616 | tf_op jit(solution)/shard_map/ppermute | solution.py:410
  57.8 2.8 %collective-permute-start.7 = (bf16[256,256]{1,0:T(8,128)(2,1)S(1)}, bf16[256,256]{1,0:T(8,128)(2,1)S(1)}, u32[]{:S(2)}, u32[]{:S(2)}) collective-permute-start(bf16[256,256]{1,0:T(8,128)(2,1)S(1)} %shard_map.118.mine_ref), channel_id=1, source_target_pairs={{0,4},{4,0},{8,12},{12,8},{16,20},{20,16},{24,28},{28,24},{32,36},... | collective-permute-start | bytes 393224 | tf_op jit(solution)/shard_map/ppermute | solution.py:472
  64.5 21.0 %all-to-all-start.1 = ((bf16[32,64,128]{2,1,0:T(8,128)(2,1)}), bf16[32,64,128]{2,1,0:T(8,128)(2,1)S(1)}, u32[]{:S(2)}, u32[]{:S(2)}) async-start(bf16[32,64,128]{2,1,0:T(8,128)(2,1)} %shard_map.119), calls=%async_computation.1 | async-start | bytes 1048576 | tf_op jit(solution)/shard_map/all_to_all | solution.py:479
  68.9 16.6 %copy-start.5 = (bf16[128,2048]{1,0:T(8,128)(2,1)S(1)}, bf16[128,2048]{1,0:T(8,128)(2,1)}, u32[]{:S(2)}) copy-start(bf16[128,2048]{1,0:T(8,128)(2,1)} %constant.17.clone.column_ref) | copy-start | bytes 1572868
